TPU v7x, 32 devices: a whole 2x2x4 slice. The times are simulated.
32 devices in a mesh: grp: 2 (over core), dp: 4 (over z), seq: 4 (over y, x).
Axes of the slice: x: 2, y: 2, z: 4, core: 2. Of those that a mesh axis runs over, the one named last changes fastest.
Arguments:
- latents: bfloat16 [4, 512, 3072], P('dp', 'seq'), may hold values from -6 to 6
- attended: bfloat16 [4, 512, 1536], P('dp', 'seq'), may hold values from -6 to 6
- gating: float32 [4, 3072], P('dp'), may hold values from -4 to 4
- weights: bfloat16 [2, 3072, 1536], P('grp', ('dp', 'seq')), may hold values from -0.15625 to 0.15625
- critic_position: bfloat16 [512, 3072], P('seq'), may hold values from -6 to 6
- critic_gain: float32 [3072], replicated, may hold values from 0.1 to 1.9
- critic_head: float32 [1536], replicated, may hold values from -0.15625 to 0.15625
- token_order: int32 [512], replicated, may hold values from 0 to 511, as said below
Outputs:
- weight_grads: float32 [2, 3072, 1536], P('grp', ('dp', 'seq'))
Inputs may be any that keep to these rules, and one draw needn't show every extreme that they name: token_order is a permutation of the 512 positions; of each aligned block of 128 entries, exactly 32 values fall in each aligned block of 128 values.
All inputs are finite; a program needn't handle non-finite values.
Results may differ from a plain program's by a relative error of at most 0.0029.
Values may be sent and summed in bfloat16 or wider, within the bound.
No kernel may reach another device: no remote copies, remote signals or barrier semaphores. Data moves between devices by JAX's collectives and lax.ppermute only.
A program may use at most 64 MiB of HBM per device.

v0:
```python
from functools import partial

import jax
import jax.numpy as jnp
from jax import lax
from jax.sharding import PartitionSpec as P


def from_behind(block, axis, distance):
    devices = range(lax.axis_size(axis))
    route = [(i - distance, i) for i in devices if i - distance in devices]
    return lax.ppermute(block, axis, route)


def normalize(values, gain):
    factor = lax.rsqrt(jnp.mean(values * values, axis=-1, keepdims=True) + 1e-06)
    return values * factor * gain


def critic_score(hidden, head):
    return jnp.sum(jax.nn.gelu(hidden, approximate=True) * head, axis=-1)


def shards(
    latents, attended, gating, weights, critic_position, critic_gain, critic_head, token_order
):
    length = latents.shape[1]
    model_width = latents.shape[2]
    feature_width = attended.shape[2]
    seq_count = lax.axis_size("seq")
    share_count = length // seq_count
    is_maker = lax.axis_index("grp") == 0
    seq_place = lax.axis_index("seq")
    full_weight = lax.all_gather(weights[0], ("dp", "seq"), axis=0, tiled=True)

    def make_fake():
        projected = jnp.einsum(
            "th,dh->td", attended[0], full_weight, preferred_element_type=jnp.float32
        )
        return (latents[0].astype(jnp.float32) + gating[0][None, :] * projected).astype(
            jnp.bfloat16
        )

    def skip_fake():
        return jnp.zeros((length, model_width), jnp.bfloat16)

    fake_clip = lax.cond(is_maker, make_fake, skip_fake)
    blocks = token_order.reshape(seq_count, length)
    sources = blocks // length
    offsets = jnp.arange(length, dtype=jnp.int32)
    sort_keys = jnp.where(sources == seq_place, offsets[None, :], length + offsets[None, :])
    picked = jnp.argsort(sort_keys, axis=1)[:, :share_count]
    send_rows = (jnp.take_along_axis(blocks, picked, axis=1) - seq_place * length).reshape(-1)
    own_block = lax.dynamic_index_in_dim(blocks, seq_place, 0, keepdims=False)
    own_source = own_block // length
    indicator = (own_source[:, None] == jnp.arange(seq_count, dtype=jnp.int32)[None, :]).astype(
        jnp.int32
    )
    rank_in = jnp.sum(jnp.cumsum(indicator, axis=0) * indicator, axis=1) - 1
    recv_rows = own_source * share_count + rank_in
    outgoing = fake_clip[send_rows].reshape(seq_count, share_count, model_width)
    crossed = from_behind(outgoing, "grp", 1)
    arrived = lax.all_to_all(crossed, "seq", split_axis=0, concat_axis=0, tiled=True)
    critic_tokens = arrived.reshape(length, model_width)[recv_rows]

    def run_critic():
        critic_in = critic_tokens.astype(jnp.float32) + critic_position.astype(jnp.float32)
        normed, norm_back = jax.vjp(partial(normalize, gain=critic_gain), critic_in)
        normed_b = normed.astype(jnp.bfloat16)
        hidden = jnp.dot(normed_b, full_weight, preferred_element_type=jnp.float32)
        scores, score_back = jax.vjp(partial(critic_score, head=critic_head), hidden)
        hidden_grad = score_back(-jax.nn.sigmoid(-scores))[0].astype(jnp.bfloat16)
        normed_grad = jnp.einsum(
            "th,dh->td", hidden_grad, full_weight, preferred_element_type=jnp.float32
        )
        input_grad = norm_back(normed_grad)[0].astype(jnp.bfloat16)
        return (normed_b, hidden_grad, input_grad)

    def skip_critic():
        return (
            jnp.zeros((length, model_width), jnp.bfloat16),
            jnp.zeros((length, feature_width), jnp.bfloat16),
            jnp.zeros((length, model_width), jnp.bfloat16),
        )

    normed_b, hidden_grad, input_grad = lax.cond(jnp.logical_not(is_maker), run_critic, skip_critic)
    returning = input_grad[jnp.argsort(recv_rows)].reshape(seq_count, share_count, model_width)
    regrouped = lax.all_to_all(returning, "seq", split_axis=0, concat_axis=0, tiled=True)
    returned = from_behind(regrouped, "grp", -1)
    fake_grad = returned.reshape(length, model_width)[jnp.argsort(send_rows)]
    projected_grad = (gating[0][None, :] * fake_grad.astype(jnp.float32)).astype(jnp.bfloat16)
    left_side = jnp.where(is_maker, projected_grad, normed_b)
    right_side = jnp.where(is_maker, attended[0], hidden_grad)
    summed = lax.psum_scatter(
        jnp.einsum("td,th->dh", left_side, right_side, preferred_element_type=jnp.float32),
        ("dp", "seq"),
        scatter_dimension=0,
        tiled=True,
    )
    return summed[None]


def solution(mesh):
    return jax.shard_map(
        shards,
        mesh=mesh,
        in_specs=(
            P("dp", "seq", None),
            P("dp", "seq", None),
            P("dp", None),
            P("grp", ("dp", "seq"), None),
            P("seq", None),
            P(),
            P(),
            P(),
        ),
        out_specs=P("grp", ("dp", "seq"), None),
        check_vma=False,
    )
```

profile of v0, /device:TPU:0, one launch (start us, length us, event | category | flops | bytes accessed | tf_op | source)
XLA Modules:
  0.0 489.7 jit_solution(7925361353231627886)
XLA Ops:
  7.4 1.4 iota_select_fusion
  8.8 0.6 iota.26
  9.5 0.5 all-gather.3.cloned.1.call-update
  10.0 3.0 sort.52.cloned.1.call-done
  13.0 0.7 bitcast_or_fusion
  13.8 1.5 gather_fusion.4
  15.5 121.5 %all-gather.3.cloned.1.call-done = bf16[1,3072,1536]{2,1,0:T(8,128)(2,1)} async-done(((bf16[1,192,1536]{2,1,0:T(8,128)(2,1)}), bf16[1,3072,1536]{2,1,0:T(8,128)(2,1)}) %all-gather.3.cloned.1.call-update) | async-done | bytes 9437200 | tf_op jit(solution)/shard_map/all_gather | solution.py:34
  137.0 6.9 %conditional.2 = (bf16[128,3072]{1,0:T(8,128)(2,1)S(1)}) conditional(s32[]{:T(128)} %convert_element_type.45, () %tuple.23, (bf16[1,128,3072]{2,1,0:T(8,128)(2,1)S(1)}, f32[1,3072]{1,0:T(1,128)S(1)}, bf16[1,128,1536]{2,1,0:T(8,128)(2,1)S(1)}, bf16[3072,1536]{1,0:T(8,128)(2,1)}) %tuple.49), branch_computations={%region_0.0_spmd, %region_1.0_spmd} | conditional | flops 1209532416 | bytes 11415560 | solution.py:47
  137.1 6.8 %fusion.1 = bf16[128,3072]{1,0:T(8,128)(2,1)S(1)} fusion(bf16[3072,1536]{1,0:T(8,128)(2,1)} %get-tuple-element.117, bf16[1,128,3072]{2,1,0:T(8,128)(2,1)S(1)} %get-tuple-element.141, f32[3072]{0:T(1024)S(1)} %bitcast.64, bf16[1,128,1536]{2,1,0:T(8,128)(2,1)S(1)} %get-tuple-element.116), kind=kOutput, calls=%fused_computation.7 | convolution fusion | flops 1209532416 | bytes 11415552 | tf_op jit(solution)/shard_map/cond/branch_1_fun/th,dh->td/dot_general | solution.py:37
  143.9 1.0 gather_fusion.1
  144.9 2.3 collective-permute-start
  147.7 0.7 collective-permute-done
  148.4 3.5 all-to-all-start
  152.0 2.5 sort.49
  154.6 9.0 %all-to-all-done = bf16[4,32,3072]{2,1,0:T(8,128)(2,1)S(1)} async-done(((bf16[4,32,3072]{2,1,0:T(8,128)(2,1)}), bf16[4,32,3072]{2,1,0:T(8,128)(2,1)S(1)}, u32[]{:S(2)}, u32[]{:S(2)}) %all-to-all-start) | async-done | bytes 786464 | tf_op jit(solution)/shard_map/all_to_all | solution.py:63
  163.5 0.2 conditional.3
  163.7 1.0 gather_fusion.2
  164.8 11.1 %all_to_all.10 = bf16[4,32,3072]{2,1,0:T(8,128)(2,1)S(1)} all-to-all(bf16[4,32,3072]{2,1,0:T(8,128)(2,1)S(1)} %bitcast.61), channel_id=1, replica_groups=mesh['grp'=2,'dp'=4,'seq'=4] {'seq'}, dimensions={0} | all-to-all | bytes 1572864 | tf_op jit(solution)/shard_map/all_to_all | solution.py:88
  175.8 1.3 collective-permute-start.1
  177.2 2.5 sort.50
  179.8 10.4 %collective-permute-done.1 = bf16[4,32,3072]{2,1,0:T(8,128)(2,1)S(1)} collective-permute-done((bf16[4,32,3072]{2,1,0:T(8,128)(2,1)S(1)}, bf16[4,32,3072]{2,1,0:T(8,128)(2,1)S(1)}, u32[]{:S(2)}, u32[]{:S(2)}) %collective-permute-start.1) | collective-permute-done | bytes 786464 | tf_op jit(solution)/shard_map/ppermute | solution.py:12
  190.2 1.0 gather_fusion.3
  191.2 7.9 %fusion.17 = f32[3072,1536]{1,0:T(8,128)} fusion(bf16[128,3072]{1,0:T(8,128)(2,1)S(1)} %get-tuple-element.138, bf16[128,3072]{1,0:T(8,128)(2,1)S(1)} %gather_fusion.3, f32[3072]{0:T(1024)S(1)} %bitcast.63, pred[]{:T(512)S(6)} %eq.22, bf16[128,1536]{1,0:T(8,128)(2,1)S(1)} %get-tuple-element.139, bf16[1,128,1536]{2,1,0:T(8,128)(2,1)S(1)} %copy-done.7), kind=kOutput, calls=%fused_computation.45 | convolution fusion | flops 1209729024 | bytes 21245952 | tf_op jit(solution)/shard_map/td,th->dh/dot_general | solution.py:95
  199.2 283.1 %reduce-scatter.2.cloned.1.call-done = f32[192,1536]{1,0:T(8,128)} async-done(((f32[3072,1536]{1,0:T(8,128)}), f32[192,1536]{1,0:T(8,128)}) %reduce-scatter.2.cloned.1.call-update) | async-done | bytes 1179664 | tf_op jit(solution)/shard_map/reduce_scatter | solution.py:94
  (46 shorter events, 1.2 us)
Async XLA Ops:
  7.4 6.4 %copy-start = (s32[512]{0:T(512)S(1)}, s32[512]{0:T(512)}, u32[]{:S(2)}) copy-start(s32[512]{0:T(512)} %param.19) | copy-start | bytes 6148
  7.4 129.6 %copy-start.9 = (f32[1,3072]{1,0:T(1,128)S(1)}, f32[1,3072]{1,0:T(1,128)}, u32[]{:S(2)}) copy-start(f32[1,3072]{1,0:T(1,128)} %param.14) | copy-start | bytes 36868
  7.4 129.6 %copy-start.6 = (bf16[1,128,1536]{2,1,0:T(8,128)(2,1)S(1)}, bf16[1,128,1536]{2,1,0:T(8,128)(2,1)}, u32[]{:S(2)}) copy-start(bf16[1,128,1536]{2,1,0:T(8,128)(2,1)} %param.13) | copy-start | bytes 1179652
  7.4 129.6 %copy-start.8 = (bf16[1,128,3072]{2,1,0:T(8,128)(2,1)S(1)}, bf16[1,128,3072]{2,1,0:T(8,128)(2,1)}, u32[]{:S(2)}) copy-start(bf16[1,128,3072]{2,1,0:T(8,128)(2,1)} %param.12) | copy-start | bytes 2359300
  7.4 5.6 %sort.52.cloned.1.call-start = ((), (), s32[]{:S(2)}) async-start(), calls=%async_computation.5 | async-start | bytes 12320 | tf_op jit(solution)/shard_map/jit(argsort)/sort | solution.py:52
  9.4 127.6 %all-gather.3.cloned.1.call-start = ((), (), s32[]{:S(2)}) async-start(), calls=%async_computation.4 | async-start | bytes 10027008 | tf_op jit(solution)/shard_map/all_gather | solution.py:34
  13.0 2.4 copy-start.14
  15.4 121.6 %copy-start.11 = (s32[4,32]{1,0:T(4,128)}, s32[4,32]{1,0:T(4,128)S(1)}, u32[]{:S(2)}) copy-start(s32[4,32]{1,0:T(4,128)S(1)} %select_subtract_fusion) | copy-start | bytes 1540
  144.9 18.6 %copy-start.1 = (bf16[128,3072]{1,0:T(8,128)(2,1)S(1)}, bf16[128,3072]{1,0:T(8,128)(2,1)}, u32[]{:S(2)}) copy-start(bf16[128,3072]{1,0:T(8,128)(2,1)} %param.16) | copy-start | bytes 2359300
  144.9 3.5 collective-permute-start
  148.4 15.1 %all-to-all-start = ((bf16[4,32,3072]{2,1,0:T(8,128)(2,1)}), bf16[4,32,3072]{2,1,0:T(8,128)(2,1)S(1)}, u32[]{:S(2)}, u32[]{:S(2)}) async-start(bf16[4,32,3072]{2,1,0:T(8,128)(2,1)} %collective-permute-done), calls=%async_computation | async-start | bytes 1572864 | tf_op jit(solution)/shard_map/all_to_all | solution.py:63
  151.9 330.4 %reduce-scatter.2.cloned.1.call-start = ((), (), s32[]{:S(2)}) async-start(), calls=%async_computation.3 | async-start | bytes 20054016 | tf_op jit(solution)/shard_map/reduce_scatter | solution.py:94
  164.8 12.4 %copy-start.12 = (s32[4,32]{1,0:T(4,128)S(1)}, s32[4,32]{1,0:T(4,128)}, u32[]{:S(2)}) copy-start(s32[4,32]{1,0:T(4,128)} %copy-done.11) | copy-start | bytes 1540
  175.8 14.3 %collective-permute-start.1 = (bf16[4,32,3072]{2,1,0:T(8,128)(2,1)S(1)}, bf16[4,32,3072]{2,1,0:T(8,128)(2,1)S(1)}, u32[]{:S(2)}, u32[]{:S(2)}) collective-permute-start(bf16[4,32,3072]{2,1,0:T(8,128)(2,1)S(1)} %all_to_all.10), channel_id=1, source_target_pairs={{16,0},{17,1},{18,2},{19,3},{20,4},{21,5},{22,6},{23,7},{24,8},{25... | collective-permute-start | bytes 2359304 | tf_op jit(solution)/shard_map/ppermute | solution.py:12
  190.2 1.0 copy-start.7
Sparse Core Ops, SparseCore 0:
  10.4 2.2 sort.54.cloned.1.call-done
  (1 shorter events, 0.0 us)
Sparse Core Ops, SparseCore 1:
  12.7 124.3 all-gather.2
  199.2 283.0 reduce-scatter.1
where the time goes:
time: 490 us
  waiting for transfers between devices  425 us (87%)
  between operations  15 us (3%)
  matrix products  14.7 us (3%)
  blocking collectives  11.1 us (2%)
  local copies, waits for them, and re-layouts  8.77 us (2%)
  other arithmetic  7.69 us (2%)
  starting transfers between devices  7.17 us (1%)
    reduce_scatter x1, waiting for transfers between devices, shards(): lax.psum_scatter(jnp.einsum('td,th->dh', left_side, right_side, preferred...  283 us
    all_gather x1, waiting for transfers between devices, shards(): full_weight = lax.all_gather(weights[0], ('dp', 'seq'), axis=0, tiled=True)  121 us
    ppermute x2, waiting for transfers between devices, from_behind(): return lax.ppermute(block, axis, route)  11.1 us
    all_to_all x1, blocking collectives, shards(): lax.all_to_all(returning, 'seq', split_axis=0, concat_axis=0, tiled=True)  11.1 us
  transfers between devices with their start and end apart: 5, of which 5 were waited for; matrix products, arithmetic and copies ran while one was open for 2% of the time, Pallas kernels for 0%

commit v1 on v0

v1 whole, which is shorter than its diff:
```python
import jax
import jax.numpy as jnp
from jax import lax
from jax.sharding import PartitionSpec as P


def hop(block, axis, distance):
    route = [(i, i ^ distance) for i in range(lax.axis_size(axis))]
    return lax.ppermute(block, axis, route)


def part(array, axis, count, index):
    size = array.shape[axis] // count
    return lax.dynamic_slice_in_dim(array, index * size, size, axis)


def everyone(own, axis):
    return [own] + [hop(own, axis, k) for k in range(1, lax.axis_size(axis))]


def in_order(blocks, place):
    size = blocks[0].shape[0]
    whole = jnp.zeros((len(blocks) * size,) + blocks[0].shape[1:], blocks[0].dtype)
    for k, block in enumerate(blocks):
        whole = lax.dynamic_update_slice_in_dim(whole, block, (place ^ k) * size, 0)
    return whole


def shards(
    latents, attended, gating, weights, critic_position, critic_gain, critic_head, token_order
):
    bf16, f16, f32 = jnp.bfloat16, jnp.float16, jnp.float32
    length, model_width = latents.shape[1:]
    feature_width = attended.shape[2]
    dps, seqs, grps = lax.axis_size("dp"), lax.axis_size("seq"), lax.axis_size("grp")
    width = model_width // dps
    rows = length // grps
    grp, dp, seq = lax.axis_index("grp"), lax.axis_index("dp"), lax.axis_index("seq")
    first = grp == 0

    own_weight, other_weight = [], []
    for block in everyone(weights[0], "seq"):
        own_weight.append(block)
        other_weight.append(hop(block, "grp", 1))
    maker_weight = in_order(
        [jnp.where(first, a, b) for a, b in zip(own_weight, other_weight)], seq
    )
    critic_weight = in_order(
        [jnp.where(first, b, a) for a, b in zip(own_weight, other_weight)], seq
    )

    attended_own = part(attended[0], 0, grps, grp)
    latents_own = part(latents[0], 0, grps, grp)
    messages = [
        jnp.concatenate([attended_own, part(latents_own, 1, dps, dp ^ k)], axis=1)
        for k in range(dps)
    ]
    messages = [messages[0]] + [hop(messages[k], "dp", k) for k in range(1, dps)]
    attended_all = in_order([m[:, :feature_width] for m in messages], dp)
    latents_all = in_order([m[None, :, feature_width:] for m in messages], dp)
    gates = [part(gating, 1, dps, dp ^ k) for k in range(dps)]
    gates = in_order([gates[0]] + [hop(gates[k], "dp", k) for k in range(1, dps)], dp)
    gates = gates[:, None, :]

    columns = part(part(critic_position, 1, dps, dp), 1, grps, grp)
    column_rows = in_order(everyone(columns, "seq"), seq)
    wanted = seq * length + jnp.arange(length, dtype=jnp.int32)
    picks = (token_order[None, :] == wanted[:, None]).astype(bf16)
    placed = jnp.dot(picks, column_rows, preferred_element_type=f32).astype(bf16)
    mine = part(placed, 0, grps, grp)
    brought = hop(part(placed, 0, grps, 1 - grp), "grp", 1)
    position = jnp.concatenate(
        [jnp.where(first, mine, brought), jnp.where(first, brought, mine)], axis=1
    ).astype(f32)
    gain = part(critic_gain, 0, dps, dp)

    projected = jnp.einsum("th,dh->td", attended_all, maker_weight, preferred_element_type=f32)
    projected = projected.reshape(dps, rows, width)
    fake = (latents_all.astype(f32) + gates * projected).astype(bf16)

    critic_in = fake.astype(f32) + position[None]
    square_sum = sum(everyone(jnp.sum(critic_in * critic_in, axis=-1), "dp"))
    factor = lax.rsqrt(square_sum / model_width + 1e-06)[..., None]
    normed = (critic_in * factor * gain).astype(bf16).reshape(-1, width)
    partial = jnp.dot(normed, critic_weight, preferred_element_type=f32)
    hidden = part(partial, 0, dps, dp)
    for k in range(1, dps):
        hidden = hidden + hop(part(partial, 0, dps, dp ^ k).astype(f16), "dp", k).astype(f32)
    scores, slope_of = jax.vjp(
        lambda v: jnp.sum(jax.nn.gelu(v, approximate=True) * critic_head, axis=-1), hidden
    )
    hidden_grad = slope_of(-jax.nn.sigmoid(-scores))[0].astype(bf16)
    dots = jnp.sum(hidden_grad.astype(f32) * hidden, axis=-1, keepdims=True)
    high = lax.reduce_precision(dots, 8, 7)
    low = lax.reduce_precision(dots - high, 8, 7)
    lane = lax.broadcasted_iota(jnp.int32, (rows, 128), 1)
    tail = jnp.where(lane == 0, high, jnp.where(lane == 1, low, 0.0)).astype(bf16)
    gathered = lax.all_gather(
        jnp.concatenate([hidden_grad, tail], axis=1), "dp", axis=0, tiled=True
    )
    hidden_grads = gathered[:, :feature_width]
    tails = gathered[:, feature_width : feature_width + 2].astype(f32)
    dots_all = jnp.sum(tails, axis=-1).reshape(dps, rows, 1)
    normed_grad = jnp.einsum("th,dh->td", hidden_grads, critic_weight, preferred_element_type=f32)
    normed_grad = normed_grad.reshape(dps, rows, width)
    input_grad = gain * normed_grad * factor - critic_in * (
        factor * factor * dots_all / model_width
    )
    input_grad = input_grad.astype(bf16).astype(f32)
    maker_grad = (gates * input_grad).astype(bf16).reshape(-1, width)

    right_brought = hop(jnp.where(first, hidden_grads, attended_all), "grp", 1)
    left_brought = hop(jnp.where(first, normed, maker_grad), "grp", 1)
    left = jnp.concatenate([jnp.where(first, maker_grad, normed), left_brought], axis=0)
    right = jnp.concatenate([jnp.where(first, attended_all, hidden_grads), right_brought], axis=0)
    total = jnp.einsum("td,th->dh", left, right, preferred_element_type=f32)
    summed = part(total, 0, seqs, seq)
    for k in range(1, seqs):
        summed = summed + hop(part(total, 0, seqs, seq ^ k).astype(bf16), "seq", k).astype(f32)
    return summed[None]


def solution(mesh):
    return jax.shard_map(
        shards,
        mesh=mesh,
        in_specs=(
            P("dp", "seq", None),
            P("dp", "seq", None),
            P("dp", None),
            P("grp", ("dp", "seq"), None),
            P("seq", None),
            P(),
            P(),
            P(),
        ),
        out_specs=P("grp", ("dp", "seq"), None),
        check_vma=False,
    )
```

time: 490 us -> 148 us (0.30)
  waiting for transfers between devices: 425 us -> 72.2 us
  starting transfers between devices: 7.17 us -> 37 us
  between operations: 15 us -> 0.44 us
  matrix products: 14.7 us -> 4.07 us
  blocking collectives: 11.1 us -> 19.8 us
    reduce_scatter x1 -> x0, waiting for transfers between devices: 283 us -> none  [shards(): lax.psum_scatter(jnp.einsum('td,th->dh', left_side, right_side, preferred...]
    all_gather x1 -> x0, waiting for transfers between devices: 121 us -> none  [shards(): full_weight = lax.all_gather(weights[0], ('dp', 'seq'), axis=0, tiled=True)]
    ppermute x2 -> x28, waiting for transfers between devices: 11.1 us -> 72.2 us  [hop(): return lax.ppermute(block, axis, route)]
    ppermute x2 -> x28, starting transfers between devices: 3.59 us -> 37 us  [hop(): return lax.ppermute(block, axis, route)]
    all_gather x0 -> x1, blocking collectives: none -> 19.8 us  [shards(): lax.all_gather(jnp.concatenate([hidden_grad, tail], axis=1), 'dp', axis=0...]
    all_to_all x1 -> x0, blocking collectives: 11.1 us -> none  [shards(): lax.all_to_all(returning, 'seq', split_axis=0, concat_axis=0, tiled=True)]
    dot_general x2 -> x5, matrix products: 14.7 us -> 4.07 us  [the longest x1 1.41 us: shards(): total = jnp.einsum('td,th->dh', left, right, preferred_element_type=f32)]
    all_to_all x1 -> x0, waiting for transfers between devices: 8.96 us -> none  [shards(): lax.all_to_all(crossed, 'seq', split_axis=0, concat_axis=0, tiled=True)]
  transfers between devices with their start and end apart: 5 -> 28, of which waited for: 5 -> 13; matrix products, arithmetic and copies ran while one was open for 2% -> 6% of each run, Pallas kernels for 0% -> 0%
where the time goes in v1:
time: 148 us
  waiting for transfers between devices  72.2 us (49%)
  starting transfers between devices  37 us (25%)
  blocking collectives  19.8 us (13%)
  other arithmetic  8.53 us (6%)
  local copies, waits for them, and re-layouts  5.96 us (4%)
  matrix products  4.07 us (3%)
    ppermute x28, waiting for transfers between devices, hop(): return lax.ppermute(block, axis, route)  72.2 us
    ppermute x28, starting transfers between devices, hop(): return lax.ppermute(block, axis, route)  37 us
    all_gather x1, blocking collectives, shards(): lax.all_gather(jnp.concatenate([hidden_grad, tail], axis=1), 'dp', axis=0...  19.8 us
    dynamic_update_slice x16, local copies, waits for them, and re-layouts, in_order(): whole = lax.dynamic_update_slice_in_dim(whole, block, (place ^ k) * size, 0)  3.69 us
    dynamic_update_slice x5, other arithmetic, in_order(): whole = lax.dynamic_update_slice_in_dim(whole, block, (place ^ k) * size, 0)  3.28 us
  transfers between devices with their start and end apart: 28, of which 13 were waited for; matrix products, arithmetic and copies ran while one was open for 6% of the time, Pallas kernels for 0%

profile of v1, /device:TPU:0, one launch (start us, length us, event | category | flops | bytes accessed | tf_op | source)
XLA Modules:
  0.0 148.0 jit_solution(16839296021181197831)
XLA Ops:
  1.1 3.0 %collective-permute-start.13 = (bf16[128,384]{1,0:T(8,128)(2,1)S(1)}, bf16[128,384]{1,0:T(8,128)(2,1)S(1)}, u32[]{:S(2)}, u32[]{:S(2)}) collective-permute-start(bf16[128,384]{1,0:T(8,128)(2,1)S(1)} %get-tuple-element.12), channel_id=1, source_target_pairs={{0,1},{1,0},{2,3},{3,2},{4,5},{5,4},{6,7},{7,6},{8,9},{9,8},{10,11... | collective-permute-start | bytes 294920 | tf_op jit(solution)/shard_map/ppermute | solution.py:9
  4.1 1.5 %collective-permute-start.14 = (bf16[128,384]{1,0:T(8,128)(2,1)S(1)}, bf16[128,384]{1,0:T(8,128)(2,1)S(1)}, u32[]{:S(2)}, u32[]{:S(2)}) collective-permute-start(bf16[128,384]{1,0:T(8,128)(2,1)S(1)} %get-tuple-element.12), channel_id=1, source_target_pairs={{0,2},{1,3},{2,0},{3,1},{4,6},{5,7},{6,4},{7,5},{8,10},{9,11},{10,... | collective-permute-start | bytes 294920 | tf_op jit(solution)/shard_map/ppermute | solution.py:9
  6.4 2.0 %collective-permute-start = (f32[1,768]{1,0:T(1,128)S(1)}, f32[1,768]{1,0:T(1,128)S(1)}, u32[]{:S(2)}, u32[]{:S(2)}) collective-permute-start(f32[1,768]{1,0:T(1,128)S(1)} %get-tuple-element.41), channel_id=1, source_target_pairs={{0,4},{4,0},{8,12},{12,8},{1,5},{5,1},{9,13},{13,9},{2,6},{6,2},{1... | collective-permute-start | bytes 9224 | tf_op jit(solution)/shard_map/ppermute | solution.py:9
  10.9 2.7 %collective-permute-start.1 = (f32[1,768]{1,0:T(1,128)S(1)}, f32[1,768]{1,0:T(1,128)S(1)}, u32[]{:S(2)}, u32[]{:S(2)}) collective-permute-start(f32[1,768]{1,0:T(1,128)S(1)} %get-tuple-element.43), channel_id=1, source_target_pairs={{0,8},{4,12},{8,0},{12,4},{1,9},{5,13},{9,1},{13,5},{2,10},{6,14},... | collective-permute-start | bytes 9224 | tf_op jit(solution)/shard_map/ppermute | solution.py:9
  15.2 1.8 %collective-permute-start.7 = (bf16[192,1536]{1,0:T(8,128)(2,1)S(1)}, bf16[192,1536]{1,0:T(8,128)(2,1)S(1)}, u32[]{:S(2)}, u32[]{:S(2)}) collective-permute-start(bf16[192,1536]{1,0:T(8,128)(2,1)S(1)} %bitcast.42), channel_id=1, source_target_pairs={{0,1},{1,0},{2,3},{3,2},{4,5},{5,4},{6,7},{7,6},{8,9},{9,8},{10,11... | collective-permute-start | bytes 1769480 | tf_op jit(solution)/shard_map/ppermute | solution.py:9
  17.0 1.6 %collective-permute-start.9 = (bf16[192,1536]{1,0:T(8,128)(2,1)S(1)}, bf16[192,1536]{1,0:T(8,128)(2,1)}, u32[]{:S(2)}, u32[]{:S(2)}) collective-permute-start(bf16[192,1536]{1,0:T(8,128)(2,1)S(1)} %bitcast.43), channel_id=1, source_target_pairs={{0,2},{1,3},{2,0},{3,1},{4,6},{5,7},{6,4},{7,5},{8,10},{9,11},{10,... | collective-permute-start | bytes 1769480 | tf_op jit(solution)/shard_map/ppermute | solution.py:9
  19.1 2.4 %collective-permute-start.11 = (bf16[192,1536]{1,0:T(8,128)(2,1)S(1)}, bf16[192,1536]{1,0:T(8,128)(2,1)}, u32[]{:S(2)}, u32[]{:S(2)}) collective-permute-start(bf16[192,1536]{1,0:T(8,128)(2,1)S(1)} %bitcast.44), channel_id=1, source_target_pairs={{0,3},{1,2},{2,1},{3,0},{4,7},{5,6},{6,5},{7,4},{8,11},{9,10},{10,... | collective-permute-start | bytes 1769480 | tf_op jit(solution)/shard_map/ppermute | solution.py:9
  21.7 7.5 %collective-permute-done.3 = bf16[64,2304]{1,0:T(8,128)(2,1)S(1)} collective-permute-done((bf16[64,2304]{1,0:T(8,128)(2,1)}, bf16[64,2304]{1,0:T(8,128)(2,1)S(1)}, u32[]{:S(2)}, u32[]{:S(2)}) %collective-permute-start.3) | collective-permute-done | bytes 294944 | tf_op jit(solution)/shard_map/ppermute | solution.py:9
  30.5 12.9 %collective-permute-done.4 = bf16[64,2304]{1,0:T(8,128)(2,1)S(1)} collective-permute-done((bf16[64,2304]{1,0:T(8,128)(2,1)}, bf16[64,2304]{1,0:T(8,128)(2,1)S(1)}, u32[]{:S(2)}, u32[]{:S(2)}) %collective-permute-start.4) | collective-permute-done | bytes 294944 | tf_op jit(solution)/shard_map/ppermute | solution.py:9
  43.4 3.5 %collective-permute-start.5 = (bf16[64,2304]{1,0:T(8,128)(2,1)}, bf16[64,2304]{1,0:T(8,128)(2,1)S(1)}, u32[]{:S(2)}, u32[]{:S(2)}) collective-permute-start(bf16[64,2304]{1,0:T(8,128)(2,1)} %get-tuple-element.35), channel_id=1, source_target_pairs={{0,12},{4,8},{8,4},{12,0},{1,13},{5,9},{9,5},{13,1},{2,14},{6,10},... | collective-permute-start | bytes 884744 | tf_op jit(solution)/shard_map/ppermute | solution.py:9
  47.0 7.5 %collective-permute-done.5 = bf16[64,2304]{1,0:T(8,128)(2,1)S(1)} collective-permute-done((bf16[64,2304]{1,0:T(8,128)(2,1)}, bf16[64,2304]{1,0:T(8,128)(2,1)S(1)}, u32[]{:S(2)}, u32[]{:S(2)}) %collective-permute-start.5) | collective-permute-done | bytes 294944 | tf_op jit(solution)/shard_map/ppermute | solution.py:9
  61.3 5.2 %collective-permute-start.17 = (f32[4,64]{1,0:T(4,128)S(1)}, f32[4,64]{1,0:T(4,128)S(1)}, u32[]{:S(2)}, u32[]{:S(2)}) collective-permute-start(f32[4,64]{1,0:T(4,128)S(1)} %get-tuple-element.9), channel_id=1, source_target_pairs={{0,4},{4,0},{8,12},{12,8},{1,5},{5,1},{9,13},{13,9},{2,6},{6,2},{1... | collective-permute-start | bytes 3080 | tf_op jit(solution)/shard_map/ppermute | solution.py:9
  66.5 2.4 %collective-permute-start.19 = (f32[4,64]{1,0:T(4,128)S(1)}, f32[4,64]{1,0:T(4,128)S(1)}, u32[]{:S(2)}, u32[]{:S(2)}) collective-permute-start(f32[4,64]{1,0:T(4,128)S(1)} %get-tuple-element.9), channel_id=1, source_target_pairs={{0,12},{4,8},{8,4},{12,0},{1,13},{5,9},{9,5},{13,1},{2,14},{6,10},... | collective-permute-start | bytes 3080 | tf_op jit(solution)/shard_map/ppermute | solution.py:9
  73.0 3.0 %collective-permute-start.21 = (f16[64,1536]{1,0:T(8,128)(2,1)S(1)}, f16[64,1536]{1,0:T(8,128)(2,1)S(1)}, u32[]{:S(2)}, u32[]{:S(2)}) collective-permute-start(f16[64,1536]{1,0:T(8,128)(2,1)S(1)} %get-tuple-element.22), channel_id=1, source_target_pairs={{0,8},{4,12},{8,0},{12,4},{1,9},{5,13},{9,1},{13,5},{2,10},{6,14},... | collective-permute-start | bytes 589832 | tf_op jit(solution)/shard_map/ppermute | solution.py:9
  76.0 1.4 collective-permute-start.22
  77.4 4.4 %collective-permute-done.20 = f16[64,1536]{1,0:T(8,128)(2,1)S(1)} collective-permute-done((f16[64,1536]{1,0:T(8,128)(2,1)S(1)}, f16[64,1536]{1,0:T(8,128)(2,1)S(1)}, u32[]{:S(2)}, u32[]{:S(2)}) %collective-permute-start.20) | collective-permute-done | bytes 196640 | tf_op jit(solution)/shard_map/ppermute | solution.py:9
  81.8 8.1 %collective-permute-done.21 = f16[64,1536]{1,0:T(8,128)(2,1)S(1)} collective-permute-done((f16[64,1536]{1,0:T(8,128)(2,1)S(1)}, f16[64,1536]{1,0:T(8,128)(2,1)S(1)}, u32[]{:S(2)}, u32[]{:S(2)}) %collective-permute-start.21) | collective-permute-done | bytes 196640 | tf_op jit(solution)/shard_map/ppermute | solution.py:9
  90.8 19.8 %all_gather.3 = bf16[256,1664]{1,0:T(8,128)(2,1)S(1)} all-gather(bf16[64,1664]{1,0:T(8,128)(2,1)S(1)} %pad_maximum_fusion.3), channel_id=1, replica_groups=mesh['grp'=2,'dp'=4,'seq'=4] {'dp'}, dimensions={0}, use_global_device_ids=true | all-gather | bytes 1064960 | tf_op jit(solution)/shard_map/all_gather | solution.py:98
  113.6 2.1 %collective-permute-done.23 = bf16[256,768]{1,0:T(8,128)(2,1)S(1)} collective-permute-done((bf16[256,768]{1,0:T(8,128)(2,1)S(1)}, bf16[256,768]{1,0:T(8,128)(2,1)S(1)}, u32[]{:S(2)}, u32[]{:S(2)}) %collective-permute-start.23) | collective-permute-done | bytes 393248 | tf_op jit(solution)/shard_map/ppermute | solution.py:9
  115.8 1.4 fusion
  117.4 1.6 %collective-permute-start.25 = (bf16[192,1536]{1,0:T(8,128)(2,1)S(1)}, bf16[192,1536]{1,0:T(8,128)(2,1)S(1)}, u32[]{:S(2)}, u32[]{:S(2)}) collective-permute-start(bf16[192,1536]{1,0:T(8,128)(2,1)S(1)} %get-tuple-element.15), channel_id=1, source_target_pairs={{0,1},{1,0},{2,3},{3,2},{4,5},{5,4},{6,7},{7,6},{8,9},{9,8},{10,11... | collective-permute-start | bytes 1769480 | tf_op jit(solution)/shard_map/ppermute | solution.py:9
  119.0 1.5 %collective-permute-start.26 = (bf16[192,1536]{1,0:T(8,128)(2,1)S(1)}, bf16[192,1536]{1,0:T(8,128)(2,1)S(1)}, u32[]{:S(2)}, u32[]{:S(2)}) collective-permute-start(bf16[192,1536]{1,0:T(8,128)(2,1)S(1)} %get-tuple-element.17), channel_id=1, source_target_pairs={{0,2},{1,3},{2,0},{3,1},{4,6},{5,7},{6,4},{7,5},{8,10},{9,11},{10,... | collective-permute-start | bytes 1769480 | tf_op jit(solution)/shard_map/ppermute | solution.py:9
  121.0 12.7 %collective-permute-done.25 = bf16[192,1536]{1,0:T(8,128)(2,1)S(1)} collective-permute-done((bf16[192,1536]{1,0:T(8,128)(2,1)S(1)}, bf16[192,1536]{1,0:T(8,128)(2,1)S(1)}, u32[]{:S(2)}, u32[]{:S(2)}) %collective-permute-start.25) | collective-permute-done | bytes 589856 | tf_op jit(solution)/shard_map/ppermute | solution.py:9
  133.7 13.0 %collective-permute-done.26 = bf16[192,1536]{1,0:T(8,128)(2,1)S(1)} collective-permute-done((bf16[192,1536]{1,0:T(8,128)(2,1)S(1)}, bf16[192,1536]{1,0:T(8,128)(2,1)S(1)}, u32[]{:S(2)}, u32[]{:S(2)}) %collective-permute-start.26) | collective-permute-done | bytes 589856 | tf_op jit(solution)/shard_map/ppermute | solution.py:9
  (97 shorter events, 24.4 us)
Async XLA Ops:
  1.1 9.8 %collective-permute-start.13 = (bf16[128,384]{1,0:T(8,128)(2,1)S(1)}, bf16[128,384]{1,0:T(8,128)(2,1)S(1)}, u32[]{:S(2)}, u32[]{:S(2)}) collective-permute-start(bf16[128,384]{1,0:T(8,128)(2,1)S(1)} %get-tuple-element.12), channel_id=1, source_target_pairs={{0,1},{1,0},{2,3},{3,2},{4,5},{5,4},{6,7},{7,6},{8,9},{9,8},{10,11... | collective-permute-start | bytes 294920 | tf_op jit(solution)/shard_map/ppermute | solution.py:9
  4.1 9.5 %collective-permute-start.14 = (bf16[128,384]{1,0:T(8,128)(2,1)S(1)}, bf16[128,384]{1,0:T(8,128)(2,1)S(1)}, u32[]{:S(2)}, u32[]{:S(2)}) collective-permute-start(bf16[128,384]{1,0:T(8,128)(2,1)S(1)} %get-tuple-element.12), channel_id=1, source_target_pairs={{0,2},{1,3},{2,0},{3,1},{4,6},{5,7},{6,4},{7,5},{8,10},{9,11},{10,... | collective-permute-start | bytes 294920 | tf_op jit(solution)/shard_map/ppermute | solution.py:9
  5.6 8.1 %collective-permute-start.15 = (bf16[128,384]{1,0:T(8,128)(2,1)S(1)}, bf16[128,384]{1,0:T(8,128)(2,1)S(1)}, u32[]{:S(2)}, u32[]{:S(2)}) collective-permute-start(bf16[128,384]{1,0:T(8,128)(2,1)S(1)} %get-tuple-element.12), channel_id=1, source_target_pairs={{0,3},{1,2},{2,1},{3,0},{4,7},{5,6},{6,5},{7,4},{8,11},{9,10},{10,... | collective-permute-start | bytes 294920 | tf_op jit(solution)/shard_map/ppermute | solution.py:9
  5.6 49.5 %collective-permute-start.6 = (bf16[192,1536]{1,0:T(8,128)(2,1)}, bf16[192,1536]{1,0:T(8,128)(2,1)S(1)}, u32[]{:S(2)}, u32[]{:S(2)}) collective-permute-start(bf16[192,1536]{1,0:T(8,128)(2,1)} %bitcast.41), channel_id=1, source_target_pairs={{0,16},{16,0},{1,17},{17,1},{2,18},{18,2},{3,19},{19,3},{4,20},{20... | collective-permute-start | bytes 1769480 | tf_op jit(solution)/shard_map/ppermute | solution.py:9
  6.4 8.8 %collective-permute-start = (f32[1,768]{1,0:T(1,128)S(1)}, f32[1,768]{1,0:T(1,128)S(1)}, u32[]{:S(2)}, u32[]{:S(2)}) collective-permute-start(f32[1,768]{1,0:T(1,128)S(1)} %get-tuple-element.41), channel_id=1, source_target_pairs={{0,4},{4,0},{8,12},{12,8},{1,5},{5,1},{9,13},{13,9},{2,6},{6,2},{1... | collective-permute-start | bytes 9224 | tf_op jit(solution)/shard_map/ppermute | solution.py:9
  10.9 6.1 %collective-permute-start.1 = (f32[1,768]{1,0:T(1,128)S(1)}, f32[1,768]{1,0:T(1,128)S(1)}, u32[]{:S(2)}, u32[]{:S(2)}) collective-permute-start(f32[1,768]{1,0:T(1,128)S(1)} %get-tuple-element.43), channel_id=1, source_target_pairs={{0,8},{4,12},{8,0},{12,4},{1,9},{5,13},{9,1},{13,5},{2,10},{6,14},... | collective-permute-start | bytes 9224 | tf_op jit(solution)/shard_map/ppermute | solution.py:9
  13.6 5.5 %collective-permute-start.2 = (f32[1,768]{1,0:T(1,128)S(1)}, f32[1,768]{1,0:T(1,128)S(1)}, u32[]{:S(2)}, u32[]{:S(2)}) collective-permute-start(f32[1,768]{1,0:T(1,128)S(1)} %get-tuple-element.40), channel_id=1, source_target_pairs={{0,12},{4,8},{8,4},{12,0},{1,13},{5,9},{9,5},{13,1},{2,14},{6,10},... | collective-permute-start | bytes 9224 | tf_op jit(solution)/shard_map/ppermute | solution.py:9
  14.1 7.5 %collective-permute-start.16 = (bf16[64,384]{1,0:T(8,128)(2,1)S(1)}, bf16[64,384]{1,0:T(8,128)(2,1)S(1)}, u32[]{:S(2)}, u32[]{:S(2)}) collective-permute-start(bf16[64,384]{1,0:T(8,128)(2,1)S(1)} %constant_dynamic-slice_fusion), channel_id=1, source_target_pairs={{0,16},{16,0},{1,17},{17,1},{2,18},{18,2},{3,19},{19,3},{4,20},{20... | collective-permute-start | bytes 147464 | tf_op jit(solution)/shard_map/ppermute | solution.py:9
  15.2 39.4 %collective-permute-start.7 = (bf16[192,1536]{1,0:T(8,128)(2,1)S(1)}, bf16[192,1536]{1,0:T(8,128)(2,1)S(1)}, u32[]{:S(2)}, u32[]{:S(2)}) collective-permute-start(bf16[192,1536]{1,0:T(8,128)(2,1)S(1)} %bitcast.42), channel_id=1, source_target_pairs={{0,1},{1,0},{2,3},{3,2},{4,5},{5,4},{6,7},{7,6},{8,9},{9,8},{10,11... | collective-permute-start | bytes 1769480 | tf_op jit(solution)/shard_map/ppermute | solution.py:9
  17.0 37.7 %collective-permute-start.9 = (bf16[192,1536]{1,0:T(8,128)(2,1)S(1)}, bf16[192,1536]{1,0:T(8,128)(2,1)}, u32[]{:S(2)}, u32[]{:S(2)}) collective-permute-start(bf16[192,1536]{1,0:T(8,128)(2,1)S(1)} %bitcast.43), channel_id=1, source_target_pairs={{0,2},{1,3},{2,0},{3,1},{4,6},{5,7},{6,4},{7,5},{8,10},{9,11},{10,... | collective-permute-start | bytes 1769480 | tf_op jit(solution)/shard_map/ppermute | solution.py:9
  19.1 36.8 %collective-permute-start.11 = (bf16[192,1536]{1,0:T(8,128)(2,1)S(1)}, bf16[192,1536]{1,0:T(8,128)(2,1)}, u32[]{:S(2)}, u32[]{:S(2)}) collective-permute-start(bf16[192,1536]{1,0:T(8,128)(2,1)S(1)} %bitcast.44), channel_id=1, source_target_pairs={{0,3},{1,2},{2,1},{3,0},{4,7},{5,6},{6,5},{7,4},{8,11},{9,10},{10,... | collective-permute-start | bytes 1769480 | tf_op jit(solution)/shard_map/ppermute | solution.py:9
  21.6 7.7 %collective-permute-start.3 = (bf16[64,2304]{1,0:T(8,128)(2,1)}, bf16[64,2304]{1,0:T(8,128)(2,1)S(1)}, u32[]{:S(2)}, u32[]{:S(2)}) collective-permute-start(bf16[64,2304]{1,0:T(8,128)(2,1)} %get-tuple-element.37), channel_id=1, source_target_pairs={{0,4},{4,0},{8,12},{12,8},{1,5},{5,1},{9,13},{13,9},{2,6},{6,2},{1... | collective-permute-start | bytes 884744 | tf_op jit(solution)/shard_map/ppermute | solution.py:9
  29.2 14.2 %collective-permute-start.4 = (bf16[64,2304]{1,0:T(8,128)(2,1)}, bf16[64,2304]{1,0:T(8,128)(2,1)S(1)}, u32[]{:S(2)}, u32[]{:S(2)}) collective-permute-start(bf16[64,2304]{1,0:T(8,128)(2,1)} %get-tuple-element.36), channel_id=1, source_target_pairs={{0,8},{4,12},{8,0},{12,4},{1,9},{5,13},{9,1},{13,5},{2,10},{6,14},... | collective-permute-start | bytes 884744 | tf_op jit(solution)/shard_map/ppermute | solution.py:9
  43.4 11.1 %collective-permute-start.5 = (bf16[64,2304]{1,0:T(8,128)(2,1)}, bf16[64,2304]{1,0:T(8,128)(2,1)S(1)}, u32[]{:S(2)}, u32[]{:S(2)}) collective-permute-start(bf16[64,2304]{1,0:T(8,128)(2,1)} %get-tuple-element.35), channel_id=1, source_target_pairs={{0,12},{4,8},{8,4},{12,0},{1,13},{5,9},{9,5},{13,1},{2,14},{6,10},... | collective-permute-start | bytes 884744 | tf_op jit(solution)/shard_map/ppermute | solution.py:9
  61.3 8.4 %collective-permute-start.17 = (f32[4,64]{1,0:T(4,128)S(1)}, f32[4,64]{1,0:T(4,128)S(1)}, u32[]{:S(2)}, u32[]{:S(2)}) collective-permute-start(f32[4,64]{1,0:T(4,128)S(1)} %get-tuple-element.9), channel_id=1, source_target_pairs={{0,4},{4,0},{8,12},{12,8},{1,5},{5,1},{9,13},{13,9},{2,6},{6,2},{1... | collective-permute-start | bytes 3080 | tf_op jit(solution)/shard_map/ppermute | solution.py:9
  66.5 4.5 %collective-permute-start.18 = (f32[4,64]{1,0:T(4,128)S(1)}, f32[4,64]{1,0:T(4,128)S(1)}, u32[]{:S(2)}, u32[]{:S(2)}) collective-permute-start(f32[4,64]{1,0:T(4,128)S(1)} %get-tuple-element.9), channel_id=1, source_target_pairs={{0,8},{4,12},{8,0},{12,4},{1,9},{5,13},{9,1},{13,5},{2,10},{6,14},... | collective-permute-start | bytes 3080 | tf_op jit(solution)/shard_map/ppermute | solution.py:9
  66.5 5.4 %collective-permute-start.19 = (f32[4,64]{1,0:T(4,128)S(1)}, f32[4,64]{1,0:T(4,128)S(1)}, u32[]{:S(2)}, u32[]{:S(2)}) collective-permute-start(f32[4,64]{1,0:T(4,128)S(1)} %get-tuple-element.9), channel_id=1, source_target_pairs={{0,12},{4,8},{8,4},{12,0},{1,13},{5,9},{9,5},{13,1},{2,14},{6,10},... | collective-permute-start | bytes 3080 | tf_op jit(solution)/shard_map/ppermute | solution.py:9
  72.9 8.9 %collective-permute-start.20 = (f16[64,1536]{1,0:T(8,128)(2,1)S(1)}, f16[64,1536]{1,0:T(8,128)(2,1)S(1)}, u32[]{:S(2)}, u32[]{:S(2)}) collective-permute-start(f16[64,1536]{1,0:T(8,128)(2,1)S(1)} %get-tuple-element.20), channel_id=1, source_target_pairs={{0,4},{4,0},{8,12},{12,8},{1,5},{5,1},{9,13},{13,9},{2,6},{6,2},{1... | collective-permute-start | bytes 589832 | tf_op jit(solution)/shard_map/ppermute | solution.py:9
  73.0 16.9 %collective-permute-start.21 = (f16[64,1536]{1,0:T(8,128)(2,1)S(1)}, f16[64,1536]{1,0:T(8,128)(2,1)S(1)}, u32[]{:S(2)}, u32[]{:S(2)}) collective-permute-start(f16[64,1536]{1,0:T(8,128)(2,1)S(1)} %get-tuple-element.22), channel_id=1, source_target_pairs={{0,8},{4,12},{8,0},{12,4},{1,9},{5,13},{9,1},{13,5},{2,10},{6,14},... | collective-permute-start | bytes 589832 | tf_op jit(solution)/shard_map/ppermute | solution.py:9
  76.0 14.0 %collective-permute-start.22 = (f16[64,1536]{1,0:T(8,128)(2,1)S(1)}, f16[64,1536]{1,0:T(8,128)(2,1)S(1)}, u32[]{:S(2)}, u32[]{:S(2)}) collective-permute-start(f16[64,1536]{1,0:T(8,128)(2,1)S(1)} %get-tuple-element.21), channel_id=1, source_target_pairs={{0,12},{4,8},{8,4},{12,0},{1,13},{5,9},{9,5},{13,1},{2,14},{6,10},... | collective-permute-start | bytes 589832 | tf_op jit(solution)/shard_map/ppermute | solution.py:9
  112.7 3.1 %collective-permute-start.24 = (bf16[256,1536]{1,0:T(8,128)(2,1)}, bf16[256,1536]{1,0:T(8,128)(2,1)S(1)}, u32[]{:S(2)}, u32[]{:S(2)}) collective-permute-start(bf16[256,1536]{1,0:T(8,128)(2,1)} %get-tuple-element.19), channel_id=1, source_target_pairs={{0,16},{16,0},{1,17},{17,1},{2,18},{18,2},{3,19},{19,3},{4,20},{20... | collective-permute-start | bytes 2359304 | tf_op jit(solution)/shard_map/ppermute | solution.py:9
  117.4 16.3 %collective-permute-start.25 = (bf16[192,1536]{1,0:T(8,128)(2,1)S(1)}, bf16[192,1536]{1,0:T(8,128)(2,1)S(1)}, u32[]{:S(2)}, u32[]{:S(2)}) collective-permute-start(bf16[192,1536]{1,0:T(8,128)(2,1)S(1)} %get-tuple-element.15), channel_id=1, source_target_pairs={{0,1},{1,0},{2,3},{3,2},{4,5},{5,4},{6,7},{7,6},{8,9},{9,8},{10,11... | collective-permute-start | bytes 1769480 | tf_op jit(solution)/shard_map/ppermute | solution.py:9
  119.0 27.7 %collective-permute-start.26 = (bf16[192,1536]{1,0:T(8,128)(2,1)S(1)}, bf16[192,1536]{1,0:T(8,128)(2,1)S(1)}, u32[]{:S(2)}, u32[]{:S(2)}) collective-permute-start(bf16[192,1536]{1,0:T(8,128)(2,1)S(1)} %get-tuple-element.17), channel_id=1, source_target_pairs={{0,2},{1,3},{2,0},{3,1},{4,6},{5,7},{6,4},{7,5},{8,10},{9,11},{10,... | collective-permute-start | bytes 1769480 | tf_op jit(solution)/shard_map/ppermute | solution.py:9
  120.5 26.2 %collective-permute-start.27 = (bf16[192,1536]{1,0:T(8,128)(2,1)S(1)}, bf16[192,1536]{1,0:T(8,128)(2,1)S(1)}, u32[]{:S(2)}, u32[]{:S(2)}) collective-permute-start(bf16[192,1536]{1,0:T(8,128)(2,1)S(1)} %get-tuple-element.16), channel_id=1, source_target_pairs={{0,3},{1,2},{2,1},{3,0},{4,7},{5,6},{6,5},{7,4},{8,11},{9,10},{10,... | collective-permute-start | bytes 1769480 | tf_op jit(solution)/shard_map/ppermute | solution.py:9
  (7 other events, 49.0 us)

commit v2 on v1

v2 whole, which is shorter than its diff:
```python
import jax
import jax.numpy as jnp
from jax import lax
from jax.experimental import pallas as pl
from jax.experimental.pallas import tpu as pltpu
from jax.sharding import PartitionSpec as P


def hop(block, axis, distance):
    route = [(i, i ^ distance) for i in range(lax.axis_size(axis))]
    return lax.ppermute(block, axis, route)


def rounded(values):
    return lax.reduce_precision(values, 8, 7)


def part(array, axis, count, index):
    size = array.shape[axis] // count
    return lax.dynamic_slice_in_dim(array, index * size, size, axis)


def everyone(own, axis):
    return [own] + [hop(own, axis, k) for k in range(1, lax.axis_size(axis))]


def pieces(own, axis):
    count, rows = lax.axis_size(axis), own.shape[0]
    if count != 4 or rows % 32:
        return [((k, 0), block) for k, block in enumerate(everyone(own, axis))]
    near, side = hop(own, axis, 1), hop(own, axis, 2)
    half = rows // 2
    far_top = hop(near[:half], axis, 2)
    far_bottom = hop(side[half:], axis, 1)
    return [((0, 0), own), ((1, 0), near), ((2, 0), side), ((3, 0), far_top), ((3, half), far_bottom)]


def in_order(blocks, place, size, count):
    whole = jnp.zeros((count * size,) + blocks[0][1].shape[1:], blocks[0][1].dtype)
    for (k, row), block in blocks:
        whole = lax.dynamic_update_slice_in_dim(whole, block, (place ^ k) * size + row, 0)
    return whole


VMEM = pl.BlockSpec(memory_space=pltpu.VMEM)


def pack(attended, latents, gating, weight, positions, grps, dps):
    length, depth = attended.shape
    size = weight.shape[0]
    width, rows = latents.shape[1] // dps, length // grps
    half = width // grps
    strip = length * half // depth

    def kernel(attended_ref, latents_ref, gating_ref, weight_ref, positions_ref, *outs):
        grp, dp = lax.axis_index("grp"), lax.axis_index("dp")
        row = pl.ds(pl.multiple_of(grp * rows, 16), rows)
        for k in range(dps):
            column = pl.ds(pl.multiple_of((dp ^ k) * width, 128), width)
            outs[k][:, :depth] = attended_ref[row, :]
            outs[k][:, depth:] = latents_ref[row, column]
            outs[dps + k][...] = gating_ref[:, column]
        outs[-1][:size, :] = weight_ref[...]
        if size % 16 == 0:
            column = pl.ds(pl.multiple_of(dp * width + grp * half, 128), half)
            for i in range(length // strip):
                lines = positions_ref[i * strip : (i + 1) * strip, column]
                outs[-1][size:, i * half : (i + 1) * half] = lines

    bf16, f32 = jnp.bfloat16, jnp.float32
    packed = pl.pallas_call(
        kernel,
        out_shape=[jax.ShapeDtypeStruct((rows, depth + width), bf16)] * dps
        + [jax.ShapeDtypeStruct((1, width), f32)] * dps
        + [jax.ShapeDtypeStruct((size + strip, depth), bf16)],
        in_specs=[VMEM] * 5,
        out_specs=[VMEM] * (2 * dps + 1),
        name="pack",
    )(attended, latents, gating, weight, positions)
    return list(packed[:dps]), list(packed[dps:-1]), packed[-1]


def generate(aligned, messages, gates, position, gain, own_weight, twin_weight, spots, size):
    clips, parts = len(messages), len(spots)
    rows, width = position.shape
    depth = own_weight[0].shape[1]
    channels = width

    def kernel(*refs):
        message_refs, refs = refs[:clips], refs[clips:]
        gate_refs, refs = refs[:clips], refs[clips:]
        position_ref, gain_ref, refs = refs[0], refs[1], refs[2:]
        own_refs, twin_refs, refs = refs[:parts], refs[parts : 2 * parts], refs[2 * parts :]
        out_ref, critic_ref, tokens_ref, gates_ref, square_ref, *refs = refs
        block_refs, (maker_ref, high_ref, low_ref) = refs[:clips], refs[clips:]
        grp, dp = lax.axis_index("grp"), lax.axis_index("dp")
        seq = lax.axis_index("seq") if aligned else 0

        def fill(first_refs, second_refs):
            for i, (k, row) in enumerate(spots):
                count = min(size - row, own_refs[i].shape[0])
                here = pl.ds(pl.multiple_of((seq ^ k) * size + row, 16), count)
                maker_ref[here, :] = first_refs[i][:count, :]
                critic_ref[here, :] = second_refs[i][:count, :]

        @pl.when(grp == 0)
        def _():
            fill(own_refs, twin_refs)

        @pl.when(grp != 0)
        def _():
            fill(twin_refs, own_refs)

        for k in range(clips):
            here = pl.ds(pl.multiple_of((dp ^ k) * rows, 16), rows)
            tokens_ref[here, :] = message_refs[k][:rows, :depth]
        projected = lax.dot_general(
            tokens_ref[...],
            maker_ref[...],
            (((1,), (1,)), ((), ())),
            preferred_element_type=jnp.float32,
        )
        out_ref[...] = projected.reshape(clips, rows, channels)
        for k in range(clips):
            gate = gate_refs[k][...]
            gates_ref[dp ^ k] = gate
            latents = message_refs[k][:rows, depth:].astype(jnp.float32)
            fake = (latents + gate * out_ref[dp ^ k]).astype(jnp.bfloat16)
            values = fake.astype(jnp.float32) + position_ref[...]
            out_ref[dp ^ k] = values
            sums = values[:, :128] * values[:, :128]
            for i in range(128, channels, 128):
                sums = sums + values[:, i : i + 128] * values[:, i : i + 128]
            square_ref[dp ^ k] = jnp.sum(jnp.transpose(sums), axis=0, keepdims=True)
            mean = jnp.sum(sums, axis=1, keepdims=True) / channels
            scaled = values * lax.rsqrt(mean + 1e-06) * gain_ref[...]
            high = scaled.astype(jnp.bfloat16)
            high_ref[k * rows : (k + 1) * rows] = high
            low = scaled - high.astype(jnp.float32)
            low_ref[k * rows : (k + 1) * rows] = low.astype(jnp.bfloat16)
        partial = jnp.dot(high_ref[...], critic_ref[...], preferred_element_type=jnp.float32)
        partial = partial + jnp.dot(
            low_ref[...], critic_ref[...], preferred_element_type=jnp.float32
        )
        for k in range(clips):
            block_refs[k][...] = partial[k * rows : (k + 1) * rows].astype(block_refs[k].dtype)

    return pl.pallas_call(
        kernel,
        out_shape=[
            jax.ShapeDtypeStruct((clips, rows, channels), jnp.float32),
            jax.ShapeDtypeStruct((width, depth), jnp.bfloat16),
            jax.ShapeDtypeStruct((clips * rows, depth), jnp.bfloat16),
            jax.ShapeDtypeStruct((clips, 1, channels), jnp.float32),
            jax.ShapeDtypeStruct((clips, 1, rows), jnp.float32),
        ]
        + [jax.ShapeDtypeStruct((rows, depth), jnp.float32) for _ in range(clips)],
        in_specs=[VMEM] * (2 * clips + 2 + 2 * parts),
        out_specs=[VMEM] * (5 + clips),
        scratch_shapes=[
            pltpu.VMEM((width, depth), jnp.bfloat16),
            pltpu.VMEM((clips * rows, width), jnp.bfloat16),
            pltpu.VMEM((clips * rows, width), jnp.bfloat16),
        ],
        cost_estimate=pl.CostEstimate(
            flops=2 * clips * rows * depth * width,
            bytes_accessed=2 * depth * (width + clips * rows) + 8 * clips * rows * width,
            transcendentals=0,
        ),
        name="generate",
    )(*messages, *gates, position, gain[None, :], *own_weight, *twin_weight)


def shards(
    latents, attended, gating, weights, critic_position, critic_gain, critic_head, token_order
):
    bf16, f16, f32 = jnp.bfloat16, jnp.float16, jnp.float32
    length, model_width = latents.shape[1:]
    feature_width = attended.shape[2]
    dps, seqs, grps = lax.axis_size("dp"), lax.axis_size("seq"), lax.axis_size("grp")
    width = model_width // dps
    rows = length // grps
    grp, dp, seq = lax.axis_index("grp"), lax.axis_index("dp"), lax.axis_index("seq")
    first = grp == 0

    size = weights.shape[1]
    half = width // grps
    strip = length * half // feature_width

    messages, gates, own = pack(
        attended[0], latents[0], gating, weights[0], critic_position, grps, dps
    )
    messages = messages[:1] + [hop(messages[k], "dp", k) for k in range(1, dps)]
    gates = gates[:1] + [hop(gates[k], "dp", k) for k in range(1, dps)]

    if size % 16:
        columns = part(part(critic_position, 1, dps, dp), 1, grps, grp)
        lines = [columns[i : i + strip] for i in range(0, length, strip)]
        own = jnp.concatenate([weights[0], jnp.concatenate(lines, axis=1)], axis=0)
    found = pieces(own, "seq")
    if size % 16 == 0:
        spots, blocks = [spot for spot, _ in found], [block for _, block in found]
    else:
        whole = in_order([(spot, block[:size]) for spot, block in found], seq, size, seqs)
        spots, blocks = [(0, 0)], [whole]
    twins = [hop(block, "grp", 1) for block in blocks]

    column_rows = jnp.zeros((seqs * length, half), bf16)
    for (k, row), block in found:
        if row + block.shape[0] > size:
            lines = block[size - row :]
            lines = [lines[:, i : i + half] for i in range(0, feature_width, half)]
            column_rows = lax.dynamic_update_slice_in_dim(
                column_rows, jnp.concatenate(lines, axis=0), (seq ^ k) * length, 0
            )
    wanted = seq * length + jnp.arange(length, dtype=jnp.int32)
    picks = (token_order[None, :] == wanted[:, None]).astype(bf16)
    placed = jnp.dot(picks, column_rows, preferred_element_type=f32).astype(bf16)
    mine = part(placed, 0, grps, grp)
    brought = hop(part(placed, 0, grps, 1 - grp), "grp", 1)
    position = jnp.concatenate(
        [jnp.where(first, mine, brought), jnp.where(first, brought, mine)], axis=1
    ).astype(f32)
    gain = part(critic_gain, 0, dps, dp)

    critic_in, critic_weight, attended_all, gates, square, *terms = generate(
        size % 16 == 0,
        messages,
        gates,
        position,
        gain,
        blocks,
        twins,
        spots,
        size if size % 16 == 0 else width,
    )

    for k in range(1, dps):
        term = terms[k].astype(f16)
        terms[k] = hop(term, "dp", k)
    squares = everyone(square.reshape(dps, rows), "dp")
    factor = lax.rsqrt(sum(squares) / model_width + 1e-06)
    own_factor = part(factor, 0, dps, dp)
    hidden = sum(
        term.astype(f32)
        * (jnp.sqrt(part(block, 0, dps, dp) / width + 1e-06) * own_factor).reshape(rows, 1)
        for term, block in zip(terms, squares)
    )
    factor = factor[..., None]
    normed = (critic_in * factor * gain).astype(bf16).reshape(-1, width)
    scores, slope_of = jax.vjp(
        lambda v: jnp.sum(jax.nn.gelu(v, approximate=True) * critic_head, axis=-1), hidden
    )
    hidden_grad = slope_of(-jax.nn.sigmoid(-scores))[0].astype(bf16)
    dots = jnp.sum(hidden_grad.astype(f32) * hidden, axis=-1, keepdims=True)
    high = rounded(dots)
    low = rounded(dots - high)
    lane = lax.broadcasted_iota(jnp.int32, (rows, 128), 1)
    tail = jnp.where(lane == 0, high, jnp.where(lane == 1, low, 0.0)).astype(bf16)
    gathered = lax.all_gather(
        jnp.concatenate([hidden_grad, tail], axis=1), "dp", axis=0, tiled=True
    )
    hidden_grads = gathered[:, :feature_width]
    tails = gathered[:, feature_width : feature_width + 2].astype(f32)
    dots_all = jnp.sum(tails, axis=-1).reshape(dps, rows, 1)
    normed_grad = jnp.einsum("th,dh->td", hidden_grads, critic_weight, preferred_element_type=f32)
    normed_grad = normed_grad.reshape(dps, rows, width)
    input_grad = gain * normed_grad * factor - critic_in * (
        factor * factor * dots_all / model_width
    )
    maker_grad = (gates * rounded(input_grad)).astype(bf16).reshape(-1, width)

    right_brought = hop(jnp.where(first, hidden_grads, attended_all), "grp", 1)
    left_brought = hop(jnp.where(first, normed, maker_grad), "grp", 1)
    left = jnp.concatenate([jnp.where(first, maker_grad, normed), left_brought], axis=0)
    right = jnp.concatenate([jnp.where(first, attended_all, hidden_grads), right_brought], axis=0)
    total = jnp.einsum("td,th->dh", left, right, preferred_element_type=f32)
    blocks = [part(total, 0, seqs, seq ^ k) for k in range(seqs)]
    blocks = lax.optimization_barrier(blocks[:1] + [block.astype(bf16) for block in blocks[1:]])
    summed = blocks[0]
    for k in range(1, seqs):
        summed = summed + hop(blocks[k], "seq", k).astype(f32)
    return summed[None]


def solution(mesh):
    return jax.shard_map(
        shards,
        mesh=mesh,
        in_specs=(
            P("dp", "seq", None),
            P("dp", "seq", None),
            P("dp", None),
            P("grp", ("dp", "seq"), None),
            P("seq", None),
            P(),
            P(),
            P(),
        ),
        out_specs=P("grp", ("dp", "seq"), None),
        check_vma=False,
    )
```

time: 148 us -> 147 us (level)
  Pallas kernels: 0 us -> 11 us
  waiting for transfers between devices: 72.2 us -> 62.1 us
  starting transfers between devices: 37 us -> 35.2 us
  matrix products: 4.07 us -> 2.5 us
    pallas_call x0 -> x2, Pallas kernels: none -> 11 us  [the longest x1 7.94 us: generate(): pl.pallas_call(kernel, out_shape=[jax.ShapeDtypeStruct((clips, rows, chan...]
    ppermute x28 -> x27, waiting for transfers between devices: 72.2 us -> 62.1 us  [hop(): return lax.ppermute(block, axis, route)]
    dynamic_update_slice x16 -> x0, local copies, waits for them, and re-layouts: 3.69 us -> none  [in_order(): whole = lax.dynamic_update_slice_in_dim(whole, block, (place ^ k) * size, 0)]
    dynamic_update_slice x5 -> x4, other arithmetic: 3.28 us -> 0.11 us  [shards(): lax.dynamic_update_slice_in_dim(column_rows, jnp.concatenate(lines, axis=...]
    convert_element_type x3, other arithmetic: 0.47 us -> 3.05 us  [shards(): term = terms[k].astype(f16)]
    unnamed x6 -> x45, local copies, waits for them, and re-layouts: 0.02 us -> 2.36 us
    ppermute x28 -> x27, starting transfers between devices: 37 us -> 35.2 us  [hop(): return lax.ppermute(block, axis, route)]
    slice x0 -> x6, local copies, waits for them, and re-layouts: none -> 1.61 us  [the longest x4 0.83 us: shards(): lines = [lines[:, i:i + half] for i in range(0, feature_width, half)]]
  transfers between devices with their start and end apart: 28 -> 27, of which waited for: 13 -> 10; matrix products, arithmetic and copies ran while one was open for 6% -> 6% of each run, Pallas kernels for 0% -> 0%
where the time goes in v2:
time: 147 us; the launch traced here: 146 us
  waiting for transfers between devices  62.1 us (42%)
  starting transfers between devices  35.2 us (24%)
  blocking collectives  20.1 us (14%)
  Pallas kernels  11 us (7%)
  other arithmetic  8.77 us (6%)
  local copies, waits for them, and re-layouts  6.39 us (4%)
  matrix products  2.5 us (2%)
    ppermute x27, waiting for transfers between devices, hop(): return lax.ppermute(block, axis, route)  62.1 us
    ppermute x27, starting transfers between devices, hop(): return lax.ppermute(block, axis, route)  35.2 us
    all_gather x1, blocking collectives, shards(): lax.all_gather(jnp.concatenate([hidden_grad, tail], axis=1), 'dp', axis=0...  20.1 us
    pallas_call x1, Pallas kernels, generate(): pl.pallas_call(kernel, out_shape=[jax.ShapeDtypeStruct((clips, rows, chan...  7.94 us
    convert_element_type x3, other arithmetic, shards(): term = terms[k].astype(f16)  3.05 us
    pallas_call x1, Pallas kernels, pack(): pl.pallas_call(kernel, out_shape=[jax.ShapeDtypeStruct((rows, depth + wid...  3.02 us
  transfers between devices with their start and end apart: 27, of which 10 were waited for; matrix products, arithmetic and copies ran while one was open for 6% of the time, Pallas kernels for 0%

profile of v2, /device:TPU:0, one launch (start us, length us, event | category | flops | bytes accessed | tf_op | source)
XLA Modules:
  0.0 146.4 jit_solution(11553648235374546108)
XLA Ops:
  0.0 3.0 %pack.1 = (bf16[64,2304]{1,0:T(8,128)(2,1)}, bf16[64,2304]{1,0:T(8,128)(2,1)}, bf16[64,2304]{1,0:T(8,128)(2,1)}, bf16[64,2304]{1,0:T(8,128)(2,1)}, f32[1,768]{1,...) custom-call(bf16[128,1536]{1,0:T(8,128)(2,1)} %bitcast.29, ...), custom_call_target="tpu_custom_call" | custom-call | tf_op jit(solution)/shard_map/pack/pallas_call | solution.py:71
  3.0 3.0 %collective-permute-start.7 = (bf16[224,1536]{1,0:T(8,128)(2,1)}, bf16[224,1536]{1,0:T(8,128)(2,1)S(1)}, u32[]{:S(2)}, u32[]{:S(2)}) collective-permute-start(bf16[224,1536]{1,0:T(8,128)(2,1)} %get-tuple-element.35.refs_10_), channel_id=1, source_target_pairs={{0,2},{1,3},{2,0},{3,1},{4,6},{5,7},{6,4},{7,5},{8,10},{9,11},{10,... | collective-permute-start | bytes 2064392 | tf_op jit(solution)/shard_map/ppermute | solution.py:11
  6.0 1.5 %collective-permute-start.6 = (bf16[224,1536]{1,0:T(8,128)(2,1)}, bf16[224,1536]{1,0:T(8,128)(2,1)S(1)}, u32[]{:S(2)}, u32[]{:S(2)}) collective-permute-start(bf16[224,1536]{1,0:T(8,128)(2,1)} %get-tuple-element.35.refs_10_), channel_id=1, source_target_pairs={{0,1},{1,0},{2,3},{3,2},{4,5},{5,4},{6,7},{7,6},{8,9},{9,8},{10,11... | collective-permute-start | bytes 2064392 | tf_op jit(solution)/shard_map/ppermute | solution.py:11
  7.5 1.6 %collective-permute-start = (bf16[64,2304]{1,0:T(8,128)(2,1)}, bf16[64,2304]{1,0:T(8,128)(2,1)}, u32[]{:S(2)}, u32[]{:S(2)}) collective-permute-start(bf16[64,2304]{1,0:T(8,128)(2,1)} %get-tuple-element.28), channel_id=1, source_target_pairs={{0,4},{4,0},{8,12},{12,8},{1,5},{5,1},{9,13},{13,9},{2,6},{6,2},{1... | collective-permute-start | bytes 884744 | tf_op jit(solution)/shard_map/ppermute | solution.py:11
  9.1 2.6 %collective-permute-start.1 = (bf16[64,2304]{1,0:T(8,128)(2,1)}, bf16[64,2304]{1,0:T(8,128)(2,1)}, u32[]{:S(2)}, u32[]{:S(2)}) collective-permute-start(bf16[64,2304]{1,0:T(8,128)(2,1)} %get-tuple-element.29), channel_id=1, source_target_pairs={{0,8},{4,12},{8,0},{12,4},{1,9},{5,13},{9,1},{13,5},{2,10},{6,14},... | collective-permute-start | bytes 884744 | tf_op jit(solution)/shard_map/ppermute | solution.py:11
  13.0 8.6 %collective-permute-done.7.refs_12_ = bf16[224,1536]{1,0:T(8,128)(2,1)S(1)} collective-permute-done((bf16[224,1536]{1,0:T(8,128)(2,1)}, bf16[224,1536]{1,0:T(8,128)(2,1)S(1)}, u32[]{:S(2)}, u32[]{:S(2)}) %collective-permute-start.7) | collective-permute-done | bytes 688160 | tf_op jit(solution)/shard_map/ppermute | solution.py:11
  21.7 2.8 %collective-permute-start.4 = (f32[1,768]{1,0:T(1,128)}, f32[1,768]{1,0:T(1,128)S(1)}, u32[]{:S(2)}, u32[]{:S(2)}) collective-permute-start(f32[1,768]{1,0:T(1,128)} %get-tuple-element.33), channel_id=1, source_target_pairs={{0,8},{4,12},{8,0},{12,4},{1,9},{5,13},{9,1},{13,5},{2,10},{6,14},... | collective-permute-start | bytes 9224 | tf_op jit(solution)/shard_map/ppermute | solution.py:11
  24.5 1.6 %collective-permute-start.8 = (bf16[112,1536]{1,0:T(8,128)(2,1)S(1)}, bf16[112,1536]{1,0:T(8,128)(2,1)S(1)}, u32[]{:S(2)}, u32[]{:S(2)}) collective-permute-start(bf16[112,1536]{1,0:T(8,128)(2,1)S(1)} %slice.108), channel_id=1, source_target_pairs={{0,1},{1,0},{2,3},{3,2},{4,5},{5,4},{6,7},{7,6},{8,9},{9,8},{10,11... | collective-permute-start | bytes 1032200 | tf_op jit(solution)/shard_map/ppermute | solution.py:11
  26.9 6.4 %collective-permute-done.8.refs_14_ = bf16[112,1536]{1,0:T(8,128)(2,1)S(1)} collective-permute-done((bf16[112,1536]{1,0:T(8,128)(2,1)S(1)}, bf16[112,1536]{1,0:T(8,128)(2,1)S(1)}, u32[]{:S(2)}, u32[]{:S(2)}) %collective-permute-start.8) | collective-permute-done | bytes 344096 | tf_op jit(solution)/shard_map/ppermute | solution.py:11
  33.4 2.1 %collective-permute-start.5 = (f32[1,768]{1,0:T(1,128)S(1)}, f32[1,768]{1,0:T(1,128)S(1)}, u32[]{:S(2)}, u32[]{:S(2)}) collective-permute-start(f32[1,768]{1,0:T(1,128)S(1)} %copy-done.21), channel_id=1, source_target_pairs={{0,12},{4,8},{8,4},{12,0},{1,13},{5,9},{9,5},{13,1},{2,14},{6,10},... | collective-permute-start | bytes 9224 | tf_op jit(solution)/shard_map/ppermute | solution.py:11
  35.7 1.7 %collective-permute-start.2 = (bf16[64,2304]{1,0:T(8,128)(2,1)S(1)}, bf16[64,2304]{1,0:T(8,128)(2,1)S(1)}, u32[]{:S(2)}, u32[]{:S(2)}) collective-permute-start(bf16[64,2304]{1,0:T(8,128)(2,1)S(1)} %copy-done.20), channel_id=1, source_target_pairs={{0,12},{4,8},{8,4},{12,0},{1,13},{5,9},{9,5},{13,1},{2,14},{6,10},... | collective-permute-start | bytes 884744 | tf_op jit(solution)/shard_map/ppermute | solution.py:11
  38.9 1.5 %collective-permute-start.10 = (bf16[112,1536]{1,0:T(8,128)(2,1)}, bf16[112,1536]{1,0:T(8,128)(2,1)}, u32[]{:S(2)}, u32[]{:S(2)}) collective-permute-start(bf16[112,1536]{1,0:T(8,128)(2,1)} %slice.113), channel_id=1, source_target_pairs={{0,2},{1,3},{2,0},{3,1},{4,6},{5,7},{6,4},{7,5},{8,10},{9,11},{10,... | collective-permute-start | bytes 1032200 | tf_op jit(solution)/shard_map/ppermute | solution.py:11
  41.8 5.2 %collective-permute-done.2.refs_3_ = bf16[64,2304]{1,0:T(8,128)(2,1)S(1)} collective-permute-done((bf16[64,2304]{1,0:T(8,128)(2,1)S(1)}, bf16[64,2304]{1,0:T(8,128)(2,1)S(1)}, u32[]{:S(2)}, u32[]{:S(2)}) %collective-permute-start.2) | collective-permute-done | bytes 294944 | tf_op jit(solution)/shard_map/ppermute | solution.py:11
  52.6 7.9 %generate.1 = (f32[4,64,768]{2,1,0:T(8,128)}, bf16[768,1536]{1,0:T(8,128)(2,1)}, bf16[256,1536]{1,0:T(8,128)(2,1)}, f32[4,1,768]{2,1,0:T(1,128)}, f32[4,1,64]{2,...) custom-call(bf16[64,2304]{1,0:T(8,128)(2,1)} %get-tuple-element.27.refs_0_, ...), custom_call_target="tpu_custom_call" | custom-call | flops 603979776 | bytes 4718592 | tf_op jit(solution)/shard_map/generate/pallas_call | solution.py:148
  60.6 4.2 %collective-permute-start.16 = (f32[4,64]{1,0:T(4,128)}, f32[4,64]{1,0:T(4,128)S(1)}, u32[]{:S(2)}, u32[]{:S(2)}) collective-permute-start(f32[4,64]{1,0:T(4,128)} %bitcast.33), channel_id=1, source_target_pairs={{0,4},{4,0},{8,12},{12,8},{1,5},{5,1},{9,13},{13,9},{2,6},{6,2},{1... | collective-permute-start | bytes 3080 | tf_op jit(solution)/shard_map/ppermute | solution.py:11
  70.4 2.2 %collective-permute-start.20 = (f16[64,1536]{1,0:T(8,128)(2,1)S(1)}, f16[64,1536]{1,0:T(8,128)(2,1)S(1)}, u32[]{:S(2)}, u32[]{:S(2)}) collective-permute-start(f16[64,1536]{1,0:T(8,128)(2,1)S(1)} %convert_element_type.65), channel_id=1, source_target_pairs={{0,8},{4,12},{8,0},{12,4},{1,9},{5,13},{9,1},{13,5},{2,10},{6,14},... | collective-permute-start | bytes 589832 | tf_op jit(solution)/shard_map/ppermute | solution.py:11
  75.2 2.9 %collective-permute-done.19 = f16[64,1536]{1,0:T(8,128)(2,1)S(1)} collective-permute-done((f16[64,1536]{1,0:T(8,128)(2,1)S(1)}, f16[64,1536]{1,0:T(8,128)(2,1)S(1)}, u32[]{:S(2)}, u32[]{:S(2)}) %collective-permute-start.19) | collective-permute-done | bytes 196640 | tf_op jit(solution)/shard_map/ppermute | solution.py:11
  78.1 9.5 %collective-permute-done.20 = f16[64,1536]{1,0:T(8,128)(2,1)S(1)} collective-permute-done((f16[64,1536]{1,0:T(8,128)(2,1)S(1)}, f16[64,1536]{1,0:T(8,128)(2,1)S(1)}, u32[]{:S(2)}, u32[]{:S(2)}) %collective-permute-start.20) | collective-permute-done | bytes 196640 | tf_op jit(solution)/shard_map/ppermute | solution.py:11
  88.6 20.1 %all_gather.3 = bf16[256,1664]{1,0:T(8,128)(2,1)S(1)} all-gather(bf16[64,1664]{1,0:T(8,128)(2,1)S(1)} %pad_maximum_fusion), channel_id=1, replica_groups=mesh['grp'=2,'dp'=4,'seq'=4] {'dp'}, dimensions={0}, use_global_device_ids=true | all-gather | bytes 1064960 | tf_op jit(solution)/shard_map/all_gather | solution.py:260
  112.1 1.9 %collective-permute-done.22 = bf16[256,768]{1,0:T(8,128)(2,1)S(1)} collective-permute-done((bf16[256,768]{1,0:T(8,128)(2,1)S(1)}, bf16[256,768]{1,0:T(8,128)(2,1)S(1)}, u32[]{:S(2)}, u32[]{:S(2)}) %collective-permute-start.22) | collective-permute-done | bytes 393248 | tf_op jit(solution)/shard_map/ppermute | solution.py:11
  115.8 1.6 %collective-permute-start.24 = (bf16[192,1536]{1,0:T(8,128)(2,1)S(1)}, bf16[192,1536]{1,0:T(8,128)(2,1)S(1)}, u32[]{:S(2)}, u32[]{:S(2)}) collective-permute-start(bf16[192,1536]{1,0:T(8,128)(2,1)S(1)} %get-tuple-element.46), channel_id=1, source_target_pairs={{0,1},{1,0},{2,3},{3,2},{4,5},{5,4},{6,7},{7,6},{8,9},{9,8},{10,11... | collective-permute-start | bytes 1769480 | tf_op jit(solution)/shard_map/ppermute | solution.py:11
  117.3 1.5 %collective-permute-start.25 = (bf16[192,1536]{1,0:T(8,128)(2,1)S(1)}, bf16[192,1536]{1,0:T(8,128)(2,1)S(1)}, u32[]{:S(2)}, u32[]{:S(2)}) collective-permute-start(bf16[192,1536]{1,0:T(8,128)(2,1)S(1)} %get-tuple-element.47), channel_id=1, source_target_pairs={{0,2},{1,3},{2,0},{3,1},{4,6},{5,7},{6,4},{7,5},{8,10},{9,11},{10,... | collective-permute-start | bytes 1769480 | tf_op jit(solution)/shard_map/ppermute | solution.py:11
  119.3 12.7 %collective-permute-done.24 = bf16[192,1536]{1,0:T(8,128)(2,1)S(1)} collective-permute-done((bf16[192,1536]{1,0:T(8,128)(2,1)S(1)}, bf16[192,1536]{1,0:T(8,128)(2,1)S(1)}, u32[]{:S(2)}, u32[]{:S(2)}) %collective-permute-start.24) | collective-permute-done | bytes 589856 | tf_op jit(solution)/shard_map/ppermute | solution.py:11
  132.0 13.0 %collective-permute-done.25 = bf16[192,1536]{1,0:T(8,128)(2,1)S(1)} collective-permute-done((bf16[192,1536]{1,0:T(8,128)(2,1)S(1)}, bf16[192,1536]{1,0:T(8,128)(2,1)S(1)}, u32[]{:S(2)}, u32[]{:S(2)}) %collective-permute-start.25) | collective-permute-done | bytes 589856 | tf_op jit(solution)/shard_map/ppermute | solution.py:11
  (120 shorter events, 26.8 us)
Async XLA Ops:
  3.0 18.6 %collective-permute-start.7 = (bf16[224,1536]{1,0:T(8,128)(2,1)}, bf16[224,1536]{1,0:T(8,128)(2,1)S(1)}, u32[]{:S(2)}, u32[]{:S(2)}) collective-permute-start(bf16[224,1536]{1,0:T(8,128)(2,1)} %get-tuple-element.35.refs_10_), channel_id=1, source_target_pairs={{0,2},{1,3},{2,0},{3,1},{4,6},{5,7},{6,4},{7,5},{8,10},{9,11},{10,... | collective-permute-start | bytes 2064392 | tf_op jit(solution)/shard_map/ppermute | solution.py:11
  6.0 18.5 %collective-permute-start.6 = (bf16[224,1536]{1,0:T(8,128)(2,1)}, bf16[224,1536]{1,0:T(8,128)(2,1)S(1)}, u32[]{:S(2)}, u32[]{:S(2)}) collective-permute-start(bf16[224,1536]{1,0:T(8,128)(2,1)} %get-tuple-element.35.refs_10_), channel_id=1, source_target_pairs={{0,1},{1,0},{2,3},{3,2},{4,5},{5,4},{6,7},{7,6},{8,9},{9,8},{10,11... | collective-permute-start | bytes 2064392 | tf_op jit(solution)/shard_map/ppermute | solution.py:11
  7.5 32.9 %collective-permute-start = (bf16[64,2304]{1,0:T(8,128)(2,1)}, bf16[64,2304]{1,0:T(8,128)(2,1)}, u32[]{:S(2)}, u32[]{:S(2)}) collective-permute-start(bf16[64,2304]{1,0:T(8,128)(2,1)} %get-tuple-element.28), channel_id=1, source_target_pairs={{0,4},{4,0},{8,12},{12,8},{1,5},{5,1},{9,13},{13,9},{2,6},{6,2},{1... | collective-permute-start | bytes 884744 | tf_op jit(solution)/shard_map/ppermute | solution.py:11
  9.1 31.3 %collective-permute-start.1 = (bf16[64,2304]{1,0:T(8,128)(2,1)}, bf16[64,2304]{1,0:T(8,128)(2,1)}, u32[]{:S(2)}, u32[]{:S(2)}) collective-permute-start(bf16[64,2304]{1,0:T(8,128)(2,1)} %get-tuple-element.29), channel_id=1, source_target_pairs={{0,8},{4,12},{8,0},{12,4},{1,9},{5,13},{9,1},{13,5},{2,10},{6,14},... | collective-permute-start | bytes 884744 | tf_op jit(solution)/shard_map/ppermute | solution.py:11
  11.7 23.9 %collective-permute-start.3 = (f32[1,768]{1,0:T(1,128)}, f32[1,768]{1,0:T(1,128)S(1)}, u32[]{:S(2)}, u32[]{:S(2)}) collective-permute-start(f32[1,768]{1,0:T(1,128)} %get-tuple-element.32), channel_id=1, source_target_pairs={{0,4},{4,0},{8,12},{12,8},{1,5},{5,1},{9,13},{13,9},{2,6},{6,2},{1... | collective-permute-start | bytes 9224 | tf_op jit(solution)/shard_map/ppermute | solution.py:11
  21.7 14.0 %collective-permute-start.4 = (f32[1,768]{1,0:T(1,128)}, f32[1,768]{1,0:T(1,128)S(1)}, u32[]{:S(2)}, u32[]{:S(2)}) collective-permute-start(f32[1,768]{1,0:T(1,128)} %get-tuple-element.33), channel_id=1, source_target_pairs={{0,8},{4,12},{8,0},{12,4},{1,9},{5,13},{9,1},{13,5},{2,10},{6,14},... | collective-permute-start | bytes 9224 | tf_op jit(solution)/shard_map/ppermute | solution.py:11
  24.5 8.8 %collective-permute-start.8 = (bf16[112,1536]{1,0:T(8,128)(2,1)S(1)}, bf16[112,1536]{1,0:T(8,128)(2,1)S(1)}, u32[]{:S(2)}, u32[]{:S(2)}) collective-permute-start(bf16[112,1536]{1,0:T(8,128)(2,1)S(1)} %slice.108), channel_id=1, source_target_pairs={{0,1},{1,0},{2,3},{3,2},{4,5},{5,4},{6,7},{7,6},{8,9},{9,8},{10,11... | collective-permute-start | bytes 1032200 | tf_op jit(solution)/shard_map/ppermute | solution.py:11
  33.4 5.5 %collective-permute-start.5 = (f32[1,768]{1,0:T(1,128)S(1)}, f32[1,768]{1,0:T(1,128)S(1)}, u32[]{:S(2)}, u32[]{:S(2)}) collective-permute-start(f32[1,768]{1,0:T(1,128)S(1)} %copy-done.21), channel_id=1, source_target_pairs={{0,12},{4,8},{8,4},{12,0},{1,13},{5,9},{9,5},{13,1},{2,14},{6,10},... | collective-permute-start | bytes 9224 | tf_op jit(solution)/shard_map/ppermute | solution.py:11
  35.6 15.7 %collective-permute-start.11 = (bf16[224,1536]{1,0:T(8,128)(2,1)S(1)}, bf16[224,1536]{1,0:T(8,128)(2,1)S(1)}, u32[]{:S(2)}, u32[]{:S(2)}) collective-permute-start(bf16[224,1536]{1,0:T(8,128)(2,1)S(1)} %copy-done.3), channel_id=1, source_target_pairs={{0,16},{16,0},{1,17},{17,1},{2,18},{18,2},{3,19},{19,3},{4,20},{20... | collective-permute-start | bytes 2064392 | tf_op jit(solution)/shard_map/ppermute | solution.py:11
  35.7 11.3 %collective-permute-start.2 = (bf16[64,2304]{1,0:T(8,128)(2,1)S(1)}, bf16[64,2304]{1,0:T(8,128)(2,1)S(1)}, u32[]{:S(2)}, u32[]{:S(2)}) collective-permute-start(bf16[64,2304]{1,0:T(8,128)(2,1)S(1)} %copy-done.20), channel_id=1, source_target_pairs={{0,12},{4,8},{8,4},{12,0},{1,13},{5,9},{9,5},{13,1},{2,14},{6,10},... | collective-permute-start | bytes 884744 | tf_op jit(solution)/shard_map/ppermute | solution.py:11
  38.9 10.3 %collective-permute-start.10 = (bf16[112,1536]{1,0:T(8,128)(2,1)}, bf16[112,1536]{1,0:T(8,128)(2,1)}, u32[]{:S(2)}, u32[]{:S(2)}) collective-permute-start(bf16[112,1536]{1,0:T(8,128)(2,1)} %slice.113), channel_id=1, source_target_pairs={{0,2},{1,3},{2,0},{3,1},{4,6},{5,7},{6,4},{7,5},{8,10},{9,11},{10,... | collective-permute-start | bytes 1032200 | tf_op jit(solution)/shard_map/ppermute | solution.py:11
  40.4 11.2 %collective-permute-start.12 = (bf16[224,1536]{1,0:T(8,128)(2,1)S(1)}, bf16[224,1536]{1,0:T(8,128)(2,1)S(1)}, u32[]{:S(2)}, u32[]{:S(2)}) collective-permute-start(bf16[224,1536]{1,0:T(8,128)(2,1)S(1)} %collective-permute-done.6.refs_11_), channel_id=1, source_target_pairs={{0,16},{16,0},{1,17},{17,1},{2,18},{18,2},{3,19},{19,3},{4,20},{20... | collective-permute-start | bytes 2064392 | tf_op jit(solution)/shard_map/ppermute | solution.py:11
  40.4 11.2 %collective-permute-start.13 = (bf16[224,1536]{1,0:T(8,128)(2,1)S(1)}, bf16[224,1536]{1,0:T(8,128)(2,1)}, u32[]{:S(2)}, u32[]{:S(2)}) collective-permute-start(bf16[224,1536]{1,0:T(8,128)(2,1)S(1)} %collective-permute-done.7.refs_12_), channel_id=1, source_target_pairs={{0,16},{16,0},{1,17},{17,1},{2,18},{18,2},{3,19},{19,3},{4,20},{20... | collective-permute-start | bytes 2064392 | tf_op jit(solution)/shard_map/ppermute | solution.py:11
  49.1 2.1 %collective-permute-start.15 = (bf16[112,1536]{1,0:T(8,128)(2,1)}, bf16[112,1536]{1,0:T(8,128)(2,1)S(1)}, u32[]{:S(2)}, u32[]{:S(2)}) collective-permute-start(bf16[112,1536]{1,0:T(8,128)(2,1)} %copy-done.7), channel_id=1, source_target_pairs={{0,16},{16,0},{1,17},{17,1},{2,18},{18,2},{3,19},{19,3},{4,20},{20... | collective-permute-start | bytes 1032200 | tf_op jit(solution)/shard_map/ppermute | solution.py:11
  60.6 13.1 %collective-permute-start.16 = (f32[4,64]{1,0:T(4,128)}, f32[4,64]{1,0:T(4,128)S(1)}, u32[]{:S(2)}, u32[]{:S(2)}) collective-permute-start(f32[4,64]{1,0:T(4,128)} %bitcast.33), channel_id=1, source_target_pairs={{0,4},{4,0},{8,12},{12,8},{1,5},{5,1},{9,13},{13,9},{2,6},{6,2},{1... | collective-permute-start | bytes 3080 | tf_op jit(solution)/shard_map/ppermute | solution.py:11
  64.8 10.3 %collective-permute-start.17 = (f32[4,64]{1,0:T(4,128)}, f32[4,64]{1,0:T(4,128)S(1)}, u32[]{:S(2)}, u32[]{:S(2)}) collective-permute-start(f32[4,64]{1,0:T(4,128)} %bitcast.34), channel_id=1, source_target_pairs={{0,8},{4,12},{8,0},{12,4},{1,9},{5,13},{9,1},{13,5},{2,10},{6,14},... | collective-permute-start | bytes 3080 | tf_op jit(solution)/shard_map/ppermute | solution.py:11
  66.1 9.1 %collective-permute-start.18 = (f32[4,64]{1,0:T(4,128)}, f32[4,64]{1,0:T(4,128)S(1)}, u32[]{:S(2)}, u32[]{:S(2)}) collective-permute-start(f32[4,64]{1,0:T(4,128)} %bitcast.35), channel_id=1, source_target_pairs={{0,12},{4,8},{8,4},{12,0},{1,13},{5,9},{9,5},{13,1},{2,14},{6,10},... | collective-permute-start | bytes 3080 | tf_op jit(solution)/shard_map/ppermute | solution.py:11
  68.5 9.6 %collective-permute-start.19 = (f16[64,1536]{1,0:T(8,128)(2,1)S(1)}, f16[64,1536]{1,0:T(8,128)(2,1)S(1)}, u32[]{:S(2)}, u32[]{:S(2)}) collective-permute-start(f16[64,1536]{1,0:T(8,128)(2,1)S(1)} %convert_element_type.63), channel_id=1, source_target_pairs={{0,4},{4,0},{8,12},{12,8},{1,5},{5,1},{9,13},{13,9},{2,6},{6,2},{1... | collective-permute-start | bytes 589832 | tf_op jit(solution)/shard_map/ppermute | solution.py:11
  70.4 17.2 %collective-permute-start.20 = (f16[64,1536]{1,0:T(8,128)(2,1)S(1)}, f16[64,1536]{1,0:T(8,128)(2,1)S(1)}, u32[]{:S(2)}, u32[]{:S(2)}) collective-permute-start(f16[64,1536]{1,0:T(8,128)(2,1)S(1)} %convert_element_type.65), channel_id=1, source_target_pairs={{0,8},{4,12},{8,0},{12,4},{1,9},{5,13},{9,1},{13,5},{2,10},{6,14},... | collective-permute-start | bytes 589832 | tf_op jit(solution)/shard_map/ppermute | solution.py:11
  73.7 13.9 %collective-permute-start.21 = (f16[64,1536]{1,0:T(8,128)(2,1)S(1)}, f16[64,1536]{1,0:T(8,128)(2,1)S(1)}, u32[]{:S(2)}, u32[]{:S(2)}) collective-permute-start(f16[64,1536]{1,0:T(8,128)(2,1)S(1)} %convert_element_type.67), channel_id=1, source_target_pairs={{0,12},{4,8},{8,4},{12,0},{1,13},{5,9},{9,5},{13,1},{2,14},{6,10},... | collective-permute-start | bytes 589832 | tf_op jit(solution)/shard_map/ppermute | solution.py:11
  111.0 3.1 %collective-permute-start.23 = (bf16[256,1536]{1,0:T(8,128)(2,1)}, bf16[256,1536]{1,0:T(8,128)(2,1)S(1)}, u32[]{:S(2)}, u32[]{:S(2)}) collective-permute-start(bf16[256,1536]{1,0:T(8,128)(2,1)} %get-tuple-element.61), channel_id=1, source_target_pairs={{0,16},{16,0},{1,17},{17,1},{2,18},{18,2},{3,19},{19,3},{4,20},{20... | collective-permute-start | bytes 2359304 | tf_op jit(solution)/shard_map/ppermute | solution.py:11
  115.8 16.3 %collective-permute-start.24 = (bf16[192,1536]{1,0:T(8,128)(2,1)S(1)}, bf16[192,1536]{1,0:T(8,128)(2,1)S(1)}, u32[]{:S(2)}, u32[]{:S(2)}) collective-permute-start(bf16[192,1536]{1,0:T(8,128)(2,1)S(1)} %get-tuple-element.46), channel_id=1, source_target_pairs={{0,1},{1,0},{2,3},{3,2},{4,5},{5,4},{6,7},{7,6},{8,9},{9,8},{10,11... | collective-permute-start | bytes 1769480 | tf_op jit(solution)/shard_map/ppermute | solution.py:11
  117.3 27.7 %collective-permute-start.25 = (bf16[192,1536]{1,0:T(8,128)(2,1)S(1)}, bf16[192,1536]{1,0:T(8,128)(2,1)S(1)}, u32[]{:S(2)}, u32[]{:S(2)}) collective-permute-start(bf16[192,1536]{1,0:T(8,128)(2,1)S(1)} %get-tuple-element.47), channel_id=1, source_target_pairs={{0,2},{1,3},{2,0},{3,1},{4,6},{5,7},{6,4},{7,5},{8,10},{9,11},{10,... | collective-permute-start | bytes 1769480 | tf_op jit(solution)/shard_map/ppermute | solution.py:11
  118.8 26.2 %collective-permute-start.26 = (bf16[192,1536]{1,0:T(8,128)(2,1)S(1)}, bf16[192,1536]{1,0:T(8,128)(2,1)S(1)}, u32[]{:S(2)}, u32[]{:S(2)}) collective-permute-start(bf16[192,1536]{1,0:T(8,128)(2,1)S(1)} %get-tuple-element.48), channel_id=1, source_target_pairs={{0,3},{1,2},{2,1},{3,0},{4,7},{5,6},{6,5},{7,4},{8,11},{9,10},{10,... | collective-permute-start | bytes 1769480 | tf_op jit(solution)/shard_map/ppermute | solution.py:11
  (25 other events, 328.3 us)

commit v3 on v2

--- a/solution.py
+++ b/solution.py
@@ -80,19 +80,21 @@
     return list(packed[:dps]), list(packed[dps:-1]), packed[-1]
 
 
-def generate(aligned, messages, gates, position, gain, own_weight, twin_weight, spots, size):
+def generate(aligned, messages, gates, picks, gain, own_weight, twin_weight, spots, size, tables):
     clips, parts = len(messages), len(spots)
-    rows, width = position.shape
+    rows, lines = picks.shape
     depth = own_weight[0].shape[1]
-    channels = width
+    channels = width = messages[0].shape[1] - depth
+    half = width // 2
 
     def kernel(*refs):
         message_refs, refs = refs[:clips], refs[clips:]
         gate_refs, refs = refs[:clips], refs[clips:]
-        position_ref, gain_ref, refs = refs[0], refs[1], refs[2:]
+        picks_ref, gain_ref, refs = refs[0], refs[1], refs[2:]
         own_refs, twin_refs, refs = refs[:parts], refs[parts : 2 * parts], refs[2 * parts :]
+        given_refs, refs = refs[: len(tables)], refs[len(tables) :]
         out_ref, critic_ref, tokens_ref, gates_ref, square_ref, *refs = refs
-        block_refs, (maker_ref, high_ref, low_ref) = refs[:clips], refs[clips:]
+        block_refs, (maker_ref, high_ref, low_ref, table_ref) = refs[:clips], refs[clips:]
         grp, dp = lax.axis_index("grp"), lax.axis_index("dp")
         seq = lax.axis_index("seq") if aligned else 0
 
@@ -111,6 +113,23 @@
         def _():
             fill(twin_refs, own_refs)
 
+        places = []
+        for side, piece_refs in enumerate((own_refs, twin_refs)):
+            if tables:
+                table = given_refs[side][...]
+            else:
+                for i, (k, row) in enumerate(spots):
+                    start, strip = size - row, piece_refs[i].shape[0] - size + row
+                    for j in range(depth // half if strip > 0 else 0):
+                        at = (k * (depth // half) + j) * strip
+                        block = piece_refs[i][start:, j * half : (j + 1) * half]
+                        table_ref[at : at + strip, :] = block
+                table = table_ref[...]
+            places.append(jnp.dot(picks_ref[...], table, preferred_element_type=jnp.float32))
+        position = jnp.concatenate(
+            [jnp.where(grp == 0, *places), jnp.where(grp == 0, *reversed(places))], axis=1
+        )
+        gain_row = gain_ref[:, pl.ds(pl.multiple_of(dp * width, 128), width)]
         for k in range(clips):
             here = pl.ds(pl.multiple_of((dp ^ k) * rows, 16), rows)
             tokens_ref[here, :] = message_refs[k][:rows, :depth]
@@ -126,14 +145,14 @@
             gates_ref[dp ^ k] = gate
             latents = message_refs[k][:rows, depth:].astype(jnp.float32)
             fake = (latents + gate * out_ref[dp ^ k]).astype(jnp.bfloat16)
-            values = fake.astype(jnp.float32) + position_ref[...]
+            values = fake.astype(jnp.float32) + position
             out_ref[dp ^ k] = values
             sums = values[:, :128] * values[:, :128]
             for i in range(128, channels, 128):
                 sums = sums + values[:, i : i + 128] * values[:, i : i + 128]
             square_ref[dp ^ k] = jnp.sum(jnp.transpose(sums), axis=0, keepdims=True)
             mean = jnp.sum(sums, axis=1, keepdims=True) / channels
-            scaled = values * lax.rsqrt(mean + 1e-06) * gain_ref[...]
+            scaled = values * lax.rsqrt(mean + 1e-06) * gain_row
             high = scaled.astype(jnp.bfloat16)
             high_ref[k * rows : (k + 1) * rows] = high
             low = scaled - high.astype(jnp.float32)
@@ -155,12 +174,13 @@
             jax.ShapeDtypeStruct((clips, 1, rows), jnp.float32),
         ]
         + [jax.ShapeDtypeStruct((rows, depth), jnp.float32) for _ in range(clips)],
-        in_specs=[VMEM] * (2 * clips + 2 + 2 * parts),
+        in_specs=[VMEM] * (2 * clips + 2 + 2 * parts + len(tables)),
         out_specs=[VMEM] * (5 + clips),
         scratch_shapes=[
             pltpu.VMEM((width, depth), jnp.bfloat16),
             pltpu.VMEM((clips * rows, width), jnp.bfloat16),
             pltpu.VMEM((clips * rows, width), jnp.bfloat16),
+            pltpu.VMEM((lines, half), jnp.bfloat16),
         ],
         cost_estimate=pl.CostEstimate(
             flops=2 * clips * rows * depth * width,
@@ -168,7 +188,7 @@
             transcendentals=0,
         ),
         name="generate",
-    )(*messages, *gates, position, gain[None, :], *own_weight, *twin_weight)
+    )(*messages, *gates, picks, gain[None, :], *own_weight, *twin_weight, *tables)
 
 
 def shards(
@@ -205,34 +225,29 @@
         spots, blocks = [(0, 0)], [whole]
     twins = [hop(block, "grp", 1) for block in blocks]
 
-    column_rows = jnp.zeros((seqs * length, half), bf16)
-    for (k, row), block in found:
-        if row + block.shape[0] > size:
-            lines = block[size - row :]
-            lines = [lines[:, i : i + half] for i in range(0, feature_width, half)]
-            column_rows = lax.dynamic_update_slice_in_dim(
-                column_rows, jnp.concatenate(lines, axis=0), (seq ^ k) * length, 0
-            )
-    wanted = seq * length + jnp.arange(length, dtype=jnp.int32)
-    picks = (token_order[None, :] == wanted[:, None]).astype(bf16)
-    placed = jnp.dot(picks, column_rows, preferred_element_type=f32).astype(bf16)
-    mine = part(placed, 0, grps, grp)
-    brought = hop(part(placed, 0, grps, 1 - grp), "grp", 1)
-    position = jnp.concatenate(
-        [jnp.where(first, mine, brought), jnp.where(first, brought, mine)], axis=1
-    ).astype(f32)
+    tables = []
+    if size % 16:
+        lines = [block[size - row :] for (_, row), block in found if row + block.shape[0] > size]
+        table = jnp.concatenate(
+            [line[:, i : i + half] for line in lines for i in range(0, feature_width, half)]
+        )
+        tables = [table, hop(table, "grp", 1)]
+    order = jnp.concatenate([part(token_order, 0, seqs, seq ^ k) for k in range(seqs)])
+    wanted = seq * length + grp * rows + jnp.arange(rows, dtype=jnp.int32)
+    picks = (order[None, :] == wanted[:, None]).astype(bf16)
     gain = part(critic_gain, 0, dps, dp)
 
     critic_in, critic_weight, attended_all, gates, square, *terms = generate(
         size % 16 == 0,
         messages,
         gates,
-        position,
-        gain,
+        picks,
+        critic_gain,
         blocks,
         twins,
         spots,
         size if size % 16 == 0 else width,
+        tables,
     )
 
     for k in range(1, dps):

time: 147 us -> 142 us (0.966)
  starting transfers between devices: 35.2 us -> 31.9 us
    ppermute x27 -> x26, starting transfers between devices: 35.2 us -> 31.9 us  [hop(): return lax.ppermute(block, axis, route)]
    ppermute x27 -> x26, waiting for transfers between devices: 62.1 us -> 62.6 us  [hop(): return lax.ppermute(block, axis, route)]
  transfers between devices with their start and end apart: 27 -> 26, of which waited for: 10 -> 11; matrix products, arithmetic and copies ran while one was open for 6% -> 5% of each run, Pallas kernels for 0% -> 0%
where the time goes in v3:
time: 142 us; the launch traced here: 141 us
  waiting for transfers between devices  62.6 us (44%)
  starting transfers between devices  31.9 us (22%)
  blocking collectives  20.1 us (14%)
  Pallas kernels  11.1 us (8%)
  other arithmetic  7.87 us (6%)
  local copies, waits for them, and re-layouts  5.04 us (4%)
  matrix products  2.23 us (2%)
    ppermute x26, waiting for transfers between devices, hop(): return lax.ppermute(block, axis, route)  62.6 us
    ppermute x26, starting transfers between devices, hop(): return lax.ppermute(block, axis, route)  31.9 us
    all_gather x1, blocking collectives, shards(): lax.all_gather(jnp.concatenate([hidden_grad, tail], axis=1), 'dp', axis=0...  20.1 us
    pallas_call x1, Pallas kernels, generate(): pl.pallas_call(kernel, out_shape=[jax.ShapeDtypeStruct((clips, rows, chan...  8.13 us
    convert_element_type x3, other arithmetic, shards(): term = terms[k].astype(f16)  3.05 us
    pallas_call x1, Pallas kernels, pack(): pl.pallas_call(kernel, out_shape=[jax.ShapeDtypeStruct((rows, depth + wid...  3 us
  transfers between devices with their start and end apart: 26, of which 11 were waited for; matrix products, arithmetic and copies ran while one was open for 5% of the time, Pallas kernels for 0%

profile of v3, /device:TPU:0, one launch (start us, length us, event | category | flops | bytes accessed | tf_op | source)
XLA Modules:
  0.0 141.2 jit_solution(12854605326736654355)
XLA Ops:
  0.0 3.0 %pack.1 = (bf16[64,2304]{1,0:T(8,128)(2,1)}, bf16[64,2304]{1,0:T(8,128)(2,1)}, bf16[64,2304]{1,0:T(8,128)(2,1)}, bf16[64,2304]{1,0:T(8,128)(2,1)}, f32[1,768]{1,...) custom-call(bf16[128,1536]{1,0:T(8,128)(2,1)} %bitcast.29, ...), custom_call_target="tpu_custom_call" | custom-call | tf_op jit(solution)/shard_map/pack/pallas_call | solution.py:71
  3.0 3.0 %collective-permute-start.6 = (bf16[224,1536]{1,0:T(8,128)(2,1)}, bf16[224,1536]{1,0:T(8,128)(2,1)S(1)}, u32[]{:S(2)}, u32[]{:S(2)}) collective-permute-start(bf16[224,1536]{1,0:T(8,128)(2,1)} %get-tuple-element.35.refs_10_), channel_id=1, source_target_pairs={{0,1},{1,0},{2,3},{3,2},{4,5},{5,4},{6,7},{7,6},{8,9},{9,8},{10,11... | collective-permute-start | bytes 2064392 | tf_op jit(solution)/shard_map/ppermute | solution.py:11
  6.0 1.5 %collective-permute-start.7 = (bf16[224,1536]{1,0:T(8,128)(2,1)}, bf16[224,1536]{1,0:T(8,128)(2,1)S(1)}, u32[]{:S(2)}, u32[]{:S(2)}) collective-permute-start(bf16[224,1536]{1,0:T(8,128)(2,1)} %get-tuple-element.35.refs_10_), channel_id=1, source_target_pairs={{0,2},{1,3},{2,0},{3,1},{4,6},{5,7},{6,4},{7,5},{8,10},{9,11},{10,... | collective-permute-start | bytes 2064392 | tf_op jit(solution)/shard_map/ppermute | solution.py:11
  7.5 1.6 %collective-permute-start.3 = (f32[1,768]{1,0:T(1,128)}, f32[1,768]{1,0:T(1,128)S(1)}, u32[]{:S(2)}, u32[]{:S(2)}) collective-permute-start(f32[1,768]{1,0:T(1,128)} %get-tuple-element.32), channel_id=1, source_target_pairs={{0,4},{4,0},{8,12},{12,8},{1,5},{5,1},{9,13},{13,9},{2,6},{6,2},{1... | collective-permute-start | bytes 9224 | tf_op jit(solution)/shard_map/ppermute | solution.py:11
  9.5 2.6 %collective-permute-start.1 = (bf16[64,2304]{1,0:T(8,128)(2,1)}, bf16[64,2304]{1,0:T(8,128)(2,1)S(1)}, u32[]{:S(2)}, u32[]{:S(2)}) collective-permute-start(bf16[64,2304]{1,0:T(8,128)(2,1)} %get-tuple-element.29), channel_id=1, source_target_pairs={{0,8},{4,12},{8,0},{12,4},{1,9},{5,13},{9,1},{13,5},{2,10},{6,14},... | collective-permute-start | bytes 884744 | tf_op jit(solution)/shard_map/ppermute | solution.py:11
  12.1 2.8 %collective-permute-start.2 = (bf16[64,2304]{1,0:T(8,128)(2,1)}, bf16[64,2304]{1,0:T(8,128)(2,1)S(1)}, u32[]{:S(2)}, u32[]{:S(2)}) collective-permute-start(bf16[64,2304]{1,0:T(8,128)(2,1)} %get-tuple-element.30), channel_id=1, source_target_pairs={{0,12},{4,8},{8,4},{12,0},{1,13},{5,9},{9,5},{13,1},{2,14},{6,10},... | collective-permute-start | bytes 884744 | tf_op jit(solution)/shard_map/ppermute | solution.py:11
  14.9 6.7 %collective-permute-done.6.refs_11_ = bf16[224,1536]{1,0:T(8,128)(2,1)S(1)} collective-permute-done((bf16[224,1536]{1,0:T(8,128)(2,1)}, bf16[224,1536]{1,0:T(8,128)(2,1)S(1)}, u32[]{:S(2)}, u32[]{:S(2)}) %collective-permute-start.6) | collective-permute-done | bytes 688160 | tf_op jit(solution)/shard_map/ppermute | solution.py:11
  21.6 2.8 %collective-permute-start.4 = (f32[1,768]{1,0:T(1,128)}, f32[1,768]{1,0:T(1,128)S(1)}, u32[]{:S(2)}, u32[]{:S(2)}) collective-permute-start(f32[1,768]{1,0:T(1,128)} %get-tuple-element.33), channel_id=1, source_target_pairs={{0,8},{4,12},{8,0},{12,4},{1,9},{5,13},{9,1},{13,5},{2,10},{6,14},... | collective-permute-start | bytes 9224 | tf_op jit(solution)/shard_map/ppermute | solution.py:11
  24.5 2.2 %collective-permute-start.5 = (f32[1,768]{1,0:T(1,128)}, f32[1,768]{1,0:T(1,128)S(1)}, u32[]{:S(2)}, u32[]{:S(2)}) collective-permute-start(f32[1,768]{1,0:T(1,128)} %get-tuple-element.34), channel_id=1, source_target_pairs={{0,12},{4,8},{8,4},{12,0},{1,13},{5,9},{9,5},{13,1},{2,14},{6,10},... | collective-permute-start | bytes 9224 | tf_op jit(solution)/shard_map/ppermute | solution.py:11
  28.2 9.3 %collective-permute-done.4.refs_6_ = f32[1,768]{1,0:T(1,128)S(1)} collective-permute-done((f32[1,768]{1,0:T(1,128)}, f32[1,768]{1,0:T(1,128)S(1)}, u32[]{:S(2)}, u32[]{:S(2)}) %collective-permute-start.4) | collective-permute-done | bytes 3104 | tf_op jit(solution)/shard_map/ppermute | solution.py:11
  40.1 5.2 %collective-permute-done.8.refs_13_ = bf16[112,1536]{1,0:T(8,128)(2,1)} collective-permute-done((bf16[112,1536]{1,0:T(8,128)(2,1)}, bf16[112,1536]{1,0:T(8,128)(2,1)}, u32[]{:S(2)}, u32[]{:S(2)}) %collective-permute-start.8) | collective-permute-done | bytes 344096 | tf_op jit(solution)/shard_map/ppermute | solution.py:11
  48.9 8.1 %generate.1 = (f32[4,64,768]{2,1,0:T(8,128)}, bf16[768,1536]{1,0:T(8,128)(2,1)}, bf16[256,1536]{1,0:T(8,128)(2,1)}, f32[4,1,768]{2,1,0:T(1,128)}, f32[4,1,64]{2,...) custom-call(bf16[64,2304]{1,0:T(8,128)(2,1)} %get-tuple-element.27.refs_0_, ...), custom_call_target="tpu_custom_call" | custom-call | flops 603979776 | bytes 4718592 | tf_op jit(solution)/shard_map/generate/pallas_call | solution.py:167
  57.1 1.3 collective-permute-start.15
  58.4 3.0 %collective-permute-start.16 = (f32[4,64]{1,0:T(4,128)}, f32[4,64]{1,0:T(4,128)S(1)}, u32[]{:S(2)}, u32[]{:S(2)}) collective-permute-start(f32[4,64]{1,0:T(4,128)} %bitcast.35), channel_id=1, source_target_pairs={{0,8},{4,12},{8,0},{12,4},{1,9},{5,13},{9,1},{13,5},{2,10},{6,14},... | collective-permute-start | bytes 3080 | tf_op jit(solution)/shard_map/ppermute | solution.py:11
  64.9 3.9 %collective-permute-start.19 = (f16[64,1536]{1,0:T(8,128)(2,1)S(1)}, f16[64,1536]{1,0:T(8,128)(2,1)S(1)}, u32[]{:S(2)}, u32[]{:S(2)}) collective-permute-start(f16[64,1536]{1,0:T(8,128)(2,1)S(1)} %convert_element_type.60), channel_id=1, source_target_pairs={{0,8},{4,12},{8,0},{12,4},{1,9},{5,13},{9,1},{13,5},{2,10},{6,14},... | collective-permute-start | bytes 589832 | tf_op jit(solution)/shard_map/ppermute | solution.py:11
  70.1 2.1 %collective-permute-done.18 = f16[64,1536]{1,0:T(8,128)(2,1)S(1)} collective-permute-done((f16[64,1536]{1,0:T(8,128)(2,1)S(1)}, f16[64,1536]{1,0:T(8,128)(2,1)S(1)}, u32[]{:S(2)}, u32[]{:S(2)}) %collective-permute-start.18) | collective-permute-done | bytes 196640 | tf_op jit(solution)/shard_map/ppermute | solution.py:11
  72.2 10.6 %collective-permute-done.19 = f16[64,1536]{1,0:T(8,128)(2,1)S(1)} collective-permute-done((f16[64,1536]{1,0:T(8,128)(2,1)S(1)}, f16[64,1536]{1,0:T(8,128)(2,1)S(1)}, u32[]{:S(2)}, u32[]{:S(2)}) %collective-permute-start.19) | collective-permute-done | bytes 196640 | tf_op jit(solution)/shard_map/ppermute | solution.py:11
  83.9 20.1 %all_gather.3 = bf16[256,1664]{1,0:T(8,128)(2,1)S(1)} all-gather(bf16[64,1664]{1,0:T(8,128)(2,1)S(1)} %pad_maximum_fusion), channel_id=1, replica_groups=mesh['grp'=2,'dp'=4,'seq'=4] {'dp'}, dimensions={0}, use_global_device_ids=true | all-gather | bytes 1064960 | tf_op jit(solution)/shard_map/all_gather | solution.py:275
  107.4 1.9 %collective-permute-done.21 = bf16[256,768]{1,0:T(8,128)(2,1)S(1)} collective-permute-done((bf16[256,768]{1,0:T(8,128)(2,1)S(1)}, bf16[256,768]{1,0:T(8,128)(2,1)S(1)}, u32[]{:S(2)}, u32[]{:S(2)}) %collective-permute-start.21) | collective-permute-done | bytes 393248 | tf_op jit(solution)/shard_map/ppermute | solution.py:11
  109.3 1.4 %fusion = f32[768,1536]{1,0:T(8,128)S(1)} fusion(bf16[256,1536]{1,0:T(8,128)(2,1)S(1)} %collective-permute-done.22, bf16[256,1536]{1,0:T(8,128)(2,1)S(1)} %get-tuple-element.60, bf16[256,768]{1,0:T(8,128)(2,1)S(1)} %collective-permute-done.21, bf16[256,768]{1,0:T(8,128)(2,1)S(1)} %bitcast.31), kind=kOutput, calls=%fused_computation | convolution fusion | flops 1212678144 | bytes 7077888 | tf_op jit(solution)/shard_map/td,th->dh/dot_general | solution.py:292
  112.9 1.7 %collective-permute-start.25 = (bf16[192,1536]{1,0:T(8,128)(2,1)S(1)}, bf16[192,1536]{1,0:T(8,128)(2,1)S(1)}, u32[]{:S(2)}, u32[]{:S(2)}) collective-permute-start(bf16[192,1536]{1,0:T(8,128)(2,1)S(1)} %get-tuple-element.48), channel_id=1, source_target_pairs={{0,3},{1,2},{2,1},{3,0},{4,7},{5,6},{6,5},{7,4},{8,11},{9,10},{10,... | collective-permute-start | bytes 1769480 | tf_op jit(solution)/shard_map/ppermute | solution.py:11
  114.6 12.7 %collective-permute-done.23 = bf16[192,1536]{1,0:T(8,128)(2,1)S(1)} collective-permute-done((bf16[192,1536]{1,0:T(8,128)(2,1)S(1)}, bf16[192,1536]{1,0:T(8,128)(2,1)S(1)}, u32[]{:S(2)}, u32[]{:S(2)}) %collective-permute-start.23) | collective-permute-done | bytes 589856 | tf_op jit(solution)/shard_map/ppermute | solution.py:11
  127.3 12.5 %collective-permute-done.25 = bf16[192,1536]{1,0:T(8,128)(2,1)S(1)} collective-permute-done((bf16[192,1536]{1,0:T(8,128)(2,1)S(1)}, bf16[192,1536]{1,0:T(8,128)(2,1)S(1)}, u32[]{:S(2)}, u32[]{:S(2)}) %collective-permute-start.25) | collective-permute-done | bytes 589856 | tf_op jit(solution)/shard_map/ppermute | solution.py:11
  139.8 1.4 add_bitcast_fusion
  (101 shorter events, 19.3 us)
Async XLA Ops:
  3.0 18.6 %collective-permute-start.6 = (bf16[224,1536]{1,0:T(8,128)(2,1)}, bf16[224,1536]{1,0:T(8,128)(2,1)S(1)}, u32[]{:S(2)}, u32[]{:S(2)}) collective-permute-start(bf16[224,1536]{1,0:T(8,128)(2,1)} %get-tuple-element.35.refs_10_), channel_id=1, source_target_pairs={{0,1},{1,0},{2,3},{3,2},{4,5},{5,4},{6,7},{7,6},{8,9},{9,8},{10,11... | collective-permute-start | bytes 2064392 | tf_op jit(solution)/shard_map/ppermute | solution.py:11
  6.0 18.5 %collective-permute-start.7 = (bf16[224,1536]{1,0:T(8,128)(2,1)}, bf16[224,1536]{1,0:T(8,128)(2,1)S(1)}, u32[]{:S(2)}, u32[]{:S(2)}) collective-permute-start(bf16[224,1536]{1,0:T(8,128)(2,1)} %get-tuple-element.35.refs_10_), channel_id=1, source_target_pairs={{0,2},{1,3},{2,0},{3,1},{4,6},{5,7},{6,4},{7,5},{8,10},{9,11},{10,... | collective-permute-start | bytes 2064392 | tf_op jit(solution)/shard_map/ppermute | solution.py:11
  7.5 4.6 %collective-permute-start.3 = (f32[1,768]{1,0:T(1,128)}, f32[1,768]{1,0:T(1,128)S(1)}, u32[]{:S(2)}, u32[]{:S(2)}) collective-permute-start(f32[1,768]{1,0:T(1,128)} %get-tuple-element.32), channel_id=1, source_target_pairs={{0,4},{4,0},{8,12},{12,8},{1,5},{5,1},{9,13},{13,9},{2,6},{6,2},{1... | collective-permute-start | bytes 9224 | tf_op jit(solution)/shard_map/ppermute | solution.py:11
  9.1 29.4 %collective-permute-start = (bf16[64,2304]{1,0:T(8,128)(2,1)}, bf16[64,2304]{1,0:T(8,128)(2,1)S(1)}, u32[]{:S(2)}, u32[]{:S(2)}) collective-permute-start(bf16[64,2304]{1,0:T(8,128)(2,1)} %get-tuple-element.28), channel_id=1, source_target_pairs={{0,4},{4,0},{8,12},{12,8},{1,5},{5,1},{9,13},{13,9},{2,6},{6,2},{1... | collective-permute-start | bytes 884744 | tf_op jit(solution)/shard_map/ppermute | solution.py:11
  9.5 29.0 %collective-permute-start.1 = (bf16[64,2304]{1,0:T(8,128)(2,1)}, bf16[64,2304]{1,0:T(8,128)(2,1)S(1)}, u32[]{:S(2)}, u32[]{:S(2)}) collective-permute-start(bf16[64,2304]{1,0:T(8,128)(2,1)} %get-tuple-element.29), channel_id=1, source_target_pairs={{0,8},{4,12},{8,0},{12,4},{1,9},{5,13},{9,1},{13,5},{2,10},{6,14},... | collective-permute-start | bytes 884744 | tf_op jit(solution)/shard_map/ppermute | solution.py:11
  12.1 27.1 %collective-permute-start.2 = (bf16[64,2304]{1,0:T(8,128)(2,1)}, bf16[64,2304]{1,0:T(8,128)(2,1)S(1)}, u32[]{:S(2)}, u32[]{:S(2)}) collective-permute-start(bf16[64,2304]{1,0:T(8,128)(2,1)} %get-tuple-element.30), channel_id=1, source_target_pairs={{0,12},{4,8},{8,4},{12,0},{1,13},{5,9},{9,5},{13,1},{2,14},{6,10},... | collective-permute-start | bytes 884744 | tf_op jit(solution)/shard_map/ppermute | solution.py:11
  21.6 15.9 %collective-permute-start.4 = (f32[1,768]{1,0:T(1,128)}, f32[1,768]{1,0:T(1,128)S(1)}, u32[]{:S(2)}, u32[]{:S(2)}) collective-permute-start(f32[1,768]{1,0:T(1,128)} %get-tuple-element.33), channel_id=1, source_target_pairs={{0,8},{4,12},{8,0},{12,4},{1,9},{5,13},{9,1},{13,5},{2,10},{6,14},... | collective-permute-start | bytes 9224 | tf_op jit(solution)/shard_map/ppermute | solution.py:11
  24.5 13.5 %collective-permute-start.5 = (f32[1,768]{1,0:T(1,128)}, f32[1,768]{1,0:T(1,128)S(1)}, u32[]{:S(2)}, u32[]{:S(2)}) collective-permute-start(f32[1,768]{1,0:T(1,128)} %get-tuple-element.34), channel_id=1, source_target_pairs={{0,12},{4,8},{8,4},{12,0},{1,13},{5,9},{9,5},{13,1},{2,14},{6,10},... | collective-permute-start | bytes 9224 | tf_op jit(solution)/shard_map/ppermute | solution.py:11
  37.5 7.9 %collective-permute-start.8 = (bf16[112,1536]{1,0:T(8,128)(2,1)}, bf16[112,1536]{1,0:T(8,128)(2,1)}, u32[]{:S(2)}, u32[]{:S(2)}) collective-permute-start(bf16[112,1536]{1,0:T(8,128)(2,1)} %slice.16), channel_id=1, source_target_pairs={{0,2},{1,3},{2,0},{3,1},{4,6},{5,7},{6,4},{7,5},{8,10},{9,11},{10,... | collective-permute-start | bytes 1032200 | tf_op jit(solution)/shard_map/ppermute | solution.py:11
  38.0 7.6 %collective-permute-start.9 = (bf16[112,1536]{1,0:T(8,128)(2,1)}, bf16[112,1536]{1,0:T(8,128)(2,1)}, u32[]{:S(2)}, u32[]{:S(2)}) collective-permute-start(bf16[112,1536]{1,0:T(8,128)(2,1)} %slice.17), channel_id=1, source_target_pairs={{0,1},{1,0},{2,3},{3,2},{4,5},{5,4},{6,7},{7,6},{8,9},{9,8},{10,11... | collective-permute-start | bytes 1032200 | tf_op jit(solution)/shard_map/ppermute | solution.py:11
  38.5 8.1 %collective-permute-start.10 = (bf16[224,1536]{1,0:T(8,128)(2,1)}, bf16[224,1536]{1,0:T(8,128)(2,1)S(1)}, u32[]{:S(2)}, u32[]{:S(2)}) collective-permute-start(bf16[224,1536]{1,0:T(8,128)(2,1)} %get-tuple-element.35.refs_10_), channel_id=1, source_target_pairs={{0,16},{16,0},{1,17},{17,1},{2,18},{18,2},{3,19},{19,3},{4,20},{20... | collective-permute-start | bytes 2064392 | tf_op jit(solution)/shard_map/ppermute | solution.py:11
  38.5 9.3 %collective-permute-start.11 = (bf16[224,1536]{1,0:T(8,128)(2,1)S(1)}, bf16[224,1536]{1,0:T(8,128)(2,1)S(1)}, u32[]{:S(2)}, u32[]{:S(2)}) collective-permute-start(bf16[224,1536]{1,0:T(8,128)(2,1)S(1)} %collective-permute-done.6.refs_11_), channel_id=1, source_target_pairs={{0,16},{16,0},{1,17},{17,1},{2,18},{18,2},{3,19},{19,3},{4,20},{20... | collective-permute-start | bytes 2064392 | tf_op jit(solution)/shard_map/ppermute | solution.py:11
  39.3 8.5 %collective-permute-start.12 = (bf16[224,1536]{1,0:T(8,128)(2,1)S(1)}, bf16[224,1536]{1,0:T(8,128)(2,1)S(1)}, u32[]{:S(2)}, u32[]{:S(2)}) collective-permute-start(bf16[224,1536]{1,0:T(8,128)(2,1)S(1)} %collective-permute-done.7.refs_12_), channel_id=1, source_target_pairs={{0,16},{16,0},{1,17},{17,1},{2,18},{18,2},{3,19},{19,3},{4,20},{20... | collective-permute-start | bytes 2064392 | tf_op jit(solution)/shard_map/ppermute | solution.py:11
  45.6 2.3 %collective-permute-start.14 = (bf16[112,1536]{1,0:T(8,128)(2,1)}, bf16[112,1536]{1,0:T(8,128)(2,1)}, u32[]{:S(2)}, u32[]{:S(2)}) collective-permute-start(bf16[112,1536]{1,0:T(8,128)(2,1)} %collective-permute-done.9.refs_14_), channel_id=1, source_target_pairs={{0,16},{16,0},{1,17},{17,1},{2,18},{18,2},{3,19},{19,3},{4,20},{20... | collective-permute-start | bytes 1032200 | tf_op jit(solution)/shard_map/ppermute | solution.py:11
  57.1 12.7 %collective-permute-start.15 = (f32[4,64]{1,0:T(4,128)}, f32[4,64]{1,0:T(4,128)S(1)}, u32[]{:S(2)}, u32[]{:S(2)}) collective-permute-start(f32[4,64]{1,0:T(4,128)} %bitcast.34), channel_id=1, source_target_pairs={{0,4},{4,0},{8,12},{12,8},{1,5},{5,1},{9,13},{13,9},{2,6},{6,2},{1... | collective-permute-start | bytes 3080 | tf_op jit(solution)/shard_map/ppermute | solution.py:11
  58.4 11.6 %collective-permute-start.16 = (f32[4,64]{1,0:T(4,128)}, f32[4,64]{1,0:T(4,128)S(1)}, u32[]{:S(2)}, u32[]{:S(2)}) collective-permute-start(f32[4,64]{1,0:T(4,128)} %bitcast.35), channel_id=1, source_target_pairs={{0,8},{4,12},{8,0},{12,4},{1,9},{5,13},{9,1},{13,5},{2,10},{6,14},... | collective-permute-start | bytes 3080 | tf_op jit(solution)/shard_map/ppermute | solution.py:11
  61.5 8.5 %collective-permute-start.17 = (f32[4,64]{1,0:T(4,128)}, f32[4,64]{1,0:T(4,128)S(1)}, u32[]{:S(2)}, u32[]{:S(2)}) collective-permute-start(f32[4,64]{1,0:T(4,128)} %bitcast.36), channel_id=1, source_target_pairs={{0,12},{4,8},{8,4},{12,0},{1,13},{5,9},{9,5},{13,1},{2,14},{6,10},... | collective-permute-start | bytes 3080 | tf_op jit(solution)/shard_map/ppermute | solution.py:11
  63.3 8.9 %collective-permute-start.18 = (f16[64,1536]{1,0:T(8,128)(2,1)S(1)}, f16[64,1536]{1,0:T(8,128)(2,1)S(1)}, u32[]{:S(2)}, u32[]{:S(2)}) collective-permute-start(f16[64,1536]{1,0:T(8,128)(2,1)S(1)} %convert_element_type.58), channel_id=1, source_target_pairs={{0,4},{4,0},{8,12},{12,8},{1,5},{5,1},{9,13},{13,9},{2,6},{6,2},{1... | collective-permute-start | bytes 589832 | tf_op jit(solution)/shard_map/ppermute | solution.py:11
  64.9 17.9 %collective-permute-start.19 = (f16[64,1536]{1,0:T(8,128)(2,1)S(1)}, f16[64,1536]{1,0:T(8,128)(2,1)S(1)}, u32[]{:S(2)}, u32[]{:S(2)}) collective-permute-start(f16[64,1536]{1,0:T(8,128)(2,1)S(1)} %convert_element_type.60), channel_id=1, source_target_pairs={{0,8},{4,12},{8,0},{12,4},{1,9},{5,13},{9,1},{13,5},{2,10},{6,14},... | collective-permute-start | bytes 589832 | tf_op jit(solution)/shard_map/ppermute | solution.py:11
  69.8 13.0 %collective-permute-start.20 = (f16[64,1536]{1,0:T(8,128)(2,1)S(1)}, f16[64,1536]{1,0:T(8,128)(2,1)S(1)}, u32[]{:S(2)}, u32[]{:S(2)}) collective-permute-start(f16[64,1536]{1,0:T(8,128)(2,1)S(1)} %convert_element_type.62), channel_id=1, source_target_pairs={{0,12},{4,8},{8,4},{12,0},{1,13},{5,9},{9,5},{13,1},{2,14},{6,10},... | collective-permute-start | bytes 589832 | tf_op jit(solution)/shard_map/ppermute | solution.py:11
  106.3 3.1 %collective-permute-start.22 = (bf16[256,1536]{1,0:T(8,128)(2,1)}, bf16[256,1536]{1,0:T(8,128)(2,1)S(1)}, u32[]{:S(2)}, u32[]{:S(2)}) collective-permute-start(bf16[256,1536]{1,0:T(8,128)(2,1)} %get-tuple-element.61), channel_id=1, source_target_pairs={{0,16},{16,0},{1,17},{17,1},{2,18},{18,2},{3,19},{19,3},{4,20},{20... | collective-permute-start | bytes 2359304 | tf_op jit(solution)/shard_map/ppermute | solution.py:11
  111.1 16.3 %collective-permute-start.23 = (bf16[192,1536]{1,0:T(8,128)(2,1)S(1)}, bf16[192,1536]{1,0:T(8,128)(2,1)S(1)}, u32[]{:S(2)}, u32[]{:S(2)}) collective-permute-start(bf16[192,1536]{1,0:T(8,128)(2,1)S(1)} %get-tuple-element.46), channel_id=1, source_target_pairs={{0,1},{1,0},{2,3},{3,2},{4,5},{5,4},{6,7},{7,6},{8,9},{9,8},{10,11... | collective-permute-start | bytes 1769480 | tf_op jit(solution)/shard_map/ppermute | solution.py:11
  111.7 15.7 %collective-permute-start.24 = (bf16[192,1536]{1,0:T(8,128)(2,1)S(1)}, bf16[192,1536]{1,0:T(8,128)(2,1)S(1)}, u32[]{:S(2)}, u32[]{:S(2)}) collective-permute-start(bf16[192,1536]{1,0:T(8,128)(2,1)S(1)} %get-tuple-element.47), channel_id=1, source_target_pairs={{0,2},{1,3},{2,0},{3,1},{4,6},{5,7},{6,4},{7,5},{8,10},{9,11},{10,... | collective-permute-start | bytes 1769480 | tf_op jit(solution)/shard_map/ppermute | solution.py:11
  112.9 26.9 %collective-permute-start.25 = (bf16[192,1536]{1,0:T(8,128)(2,1)S(1)}, bf16[192,1536]{1,0:T(8,128)(2,1)S(1)}, u32[]{:S(2)}, u32[]{:S(2)}) collective-permute-start(bf16[192,1536]{1,0:T(8,128)(2,1)S(1)} %get-tuple-element.48), channel_id=1, source_target_pairs={{0,3},{1,2},{2,1},{3,0},{4,7},{5,6},{6,5},{7,4},{8,11},{9,10},{10,... | collective-permute-start | bytes 1769480 | tf_op jit(solution)/shard_map/ppermute | solution.py:11
  (21 other events, 256.4 us)

commit v4 on v3

--- a/solution.py
+++ b/solution.py
@@ -191,6 +191,33 @@
     )(*messages, *gates, picks, gain[None, :], *own_weight, *twin_weight, *tables)
 
 
+def reduce_blocks(total, axis, place):
+    bf16, f32 = jnp.bfloat16, jnp.float32
+    count = lax.axis_size(axis)
+    rows = total.shape[0] // count
+    if count != 4 or rows % 32:
+        blocks = [part(total, 0, count, place ^ k) for k in range(count)]
+        blocks = lax.optimization_barrier(blocks[:1] + [block.astype(bf16) for block in blocks[1:]])
+        got = [hop(blocks[k], axis, k).astype(f32) for k in range(1, count)]
+        return sum(got, blocks[0])
+    ways, half = ((1, 2), (2, 1)), rows // 2
+    kept, sent = [], []
+    for side, (one, two) in enumerate(ways):
+        own, first, second, far = (
+            part(total, 0, 2 * count, 2 * (place ^ k) + side) for k in (0, one, two, 3)
+        )
+        sent.append(jnp.concatenate([first.astype(bf16), far.astype(bf16)]))
+        kept.append((own, second))
+    kept, sent = lax.optimization_barrier((kept, sent))
+    got = [hop(sent[i], axis, ways[i][0]) for i in (0, 1)]
+    passed = [(kept[i][1] + got[i][half:].astype(f32)).astype(bf16) for i in (0, 1)]
+    passed = lax.optimization_barrier(passed)
+    last = [hop(passed[i], axis, ways[i][1]) for i in (0, 1)]
+    return jnp.concatenate(
+        [kept[i][0] + got[i][:half].astype(f32) + last[i].astype(f32) for i in (0, 1)]
+    )
+
+
 def shards(
     latents, attended, gating, weights, critic_position, critic_gain, critic_head, token_order
 ):
@@ -290,12 +317,7 @@
     left = jnp.concatenate([jnp.where(first, maker_grad, normed), left_brought], axis=0)
     right = jnp.concatenate([jnp.where(first, attended_all, hidden_grads), right_brought], axis=0)
     total = jnp.einsum("td,th->dh", left, right, preferred_element_type=f32)
-    blocks = [part(total, 0, seqs, seq ^ k) for k in range(seqs)]
-    blocks = lax.optimization_barrier(blocks[:1] + [block.astype(bf16) for block in blocks[1:]])
-    summed = blocks[0]
-    for k in range(1, seqs):
-        summed = summed + hop(blocks[k], "seq", k).astype(f32)
-    return summed[None]
+    return reduce_blocks(total, "seq", seq)[None]
 
 
 def solution(mesh):

time: 142 us -> 138 us (0.972)
  waiting for transfers between devices: 62.6 us -> 58.9 us
    ppermute x26 -> x27, waiting for transfers between devices: 62.6 us -> 58.9 us  [hop(): return lax.ppermute(block, axis, route)]
    ppermute x26 -> x27, starting transfers between devices: 31.9 us -> 31.6 us  [hop(): return lax.ppermute(block, axis, route)]
  transfers between devices with their start and end apart: 26 -> 27, of which waited for: 11 -> 13; matrix products, arithmetic and copies ran while one was open for 5% -> 5% of each run, Pallas kernels for 0% -> 0%
where the time goes in v4:
time: 138 us; the launch traced here: 137 us
  waiting for transfers between devices  58.9 us (43%)
  starting transfers between devices  31.6 us (23%)
  blocking collectives  20.1 us (15%)
  Pallas kernels  11.1 us (8%)
  other arithmetic  8.03 us (6%)
  local copies, waits for them, and re-layouts  5.01 us (4%)
  matrix products  2.24 us (2%)
    ppermute x27, waiting for transfers between devices, hop(): return lax.ppermute(block, axis, route)  58.9 us
    ppermute x27, starting transfers between devices, hop(): return lax.ppermute(block, axis, route)  31.6 us
    all_gather x1, blocking collectives, shards(): lax.all_gather(jnp.concatenate([hidden_grad, tail], axis=1), 'dp', axis=0...  20.1 us
    pallas_call x1, Pallas kernels, generate(): pl.pallas_call(kernel, out_shape=[jax.ShapeDtypeStruct((clips, rows, chan...  8.12 us
    convert_element_type x3, other arithmetic, shards(): term = terms[k].astype(f16)  3.05 us
    pallas_call x1, Pallas kernels, pack(): pl.pallas_call(kernel, out_shape=[jax.ShapeDtypeStruct((rows, depth + wid...  3.01 us
  transfers between devices with their start and end apart: 27, of which 13 were waited for; matrix products, arithmetic and copies ran while one was open for 5% of the time, Pallas kernels for 0%

profile of v4, /device:TPU:0, one launch (start us, length us, event | category | flops | bytes accessed | tf_op | source)
XLA Modules:
  0.0 137.3 jit_solution(12259546633049205701)
XLA Ops:
  0.0 3.0 %pack.1 = (bf16[64,2304]{1,0:T(8,128)(2,1)}, bf16[64,2304]{1,0:T(8,128)(2,1)}, bf16[64,2304]{1,0:T(8,128)(2,1)}, bf16[64,2304]{1,0:T(8,128)(2,1)}, f32[1,768]{1,...) custom-call(bf16[128,1536]{1,0:T(8,128)(2,1)} %bitcast.29, ...), custom_call_target="tpu_custom_call" | custom-call | tf_op jit(solution)/shard_map/pack/pallas_call | solution.py:71
  3.0 3.0 %collective-permute-start.6 = (bf16[224,1536]{1,0:T(8,128)(2,1)}, bf16[224,1536]{1,0:T(8,128)(2,1)S(1)}, u32[]{:S(2)}, u32[]{:S(2)}) collective-permute-start(bf16[224,1536]{1,0:T(8,128)(2,1)} %get-tuple-element.39.refs_10_), channel_id=1, source_target_pairs={{0,1},{1,0},{2,3},{3,2},{4,5},{5,4},{6,7},{7,6},{8,9},{9,8},{10,11... | collective-permute-start | bytes 2064392 | tf_op jit(solution)/shard_map/ppermute | solution.py:11
  6.0 1.5 %collective-permute-start.7 = (bf16[224,1536]{1,0:T(8,128)(2,1)}, bf16[224,1536]{1,0:T(8,128)(2,1)S(1)}, u32[]{:S(2)}, u32[]{:S(2)}) collective-permute-start(bf16[224,1536]{1,0:T(8,128)(2,1)} %get-tuple-element.39.refs_10_), channel_id=1, source_target_pairs={{0,2},{1,3},{2,0},{3,1},{4,6},{5,7},{6,4},{7,5},{8,10},{9,11},{10,... | collective-permute-start | bytes 2064392 | tf_op jit(solution)/shard_map/ppermute | solution.py:11
  7.5 1.6 %collective-permute-start.3 = (f32[1,768]{1,0:T(1,128)}, f32[1,768]{1,0:T(1,128)S(1)}, u32[]{:S(2)}, u32[]{:S(2)}) collective-permute-start(f32[1,768]{1,0:T(1,128)} %get-tuple-element.36), channel_id=1, source_target_pairs={{0,4},{4,0},{8,12},{12,8},{1,5},{5,1},{9,13},{13,9},{2,6},{6,2},{1... | collective-permute-start | bytes 9224 | tf_op jit(solution)/shard_map/ppermute | solution.py:11
  9.5 2.6 %collective-permute-start.1 = (bf16[64,2304]{1,0:T(8,128)(2,1)}, bf16[64,2304]{1,0:T(8,128)(2,1)S(1)}, u32[]{:S(2)}, u32[]{:S(2)}) collective-permute-start(bf16[64,2304]{1,0:T(8,128)(2,1)} %get-tuple-element.33), channel_id=1, source_target_pairs={{0,8},{4,12},{8,0},{12,4},{1,9},{5,13},{9,1},{13,5},{2,10},{6,14},... | collective-permute-start | bytes 884744 | tf_op jit(solution)/shard_map/ppermute | solution.py:11
  12.1 2.8 %collective-permute-start.2 = (bf16[64,2304]{1,0:T(8,128)(2,1)}, bf16[64,2304]{1,0:T(8,128)(2,1)S(1)}, u32[]{:S(2)}, u32[]{:S(2)}) collective-permute-start(bf16[64,2304]{1,0:T(8,128)(2,1)} %get-tuple-element.34), channel_id=1, source_target_pairs={{0,12},{4,8},{8,4},{12,0},{1,13},{5,9},{9,5},{13,1},{2,14},{6,10},... | collective-permute-start | bytes 884744 | tf_op jit(solution)/shard_map/ppermute | solution.py:11
  14.9 6.7 %collective-permute-done.6.refs_11_ = bf16[224,1536]{1,0:T(8,128)(2,1)S(1)} collective-permute-done((bf16[224,1536]{1,0:T(8,128)(2,1)}, bf16[224,1536]{1,0:T(8,128)(2,1)S(1)}, u32[]{:S(2)}, u32[]{:S(2)}) %collective-permute-start.6) | collective-permute-done | bytes 688160 | tf_op jit(solution)/shard_map/ppermute | solution.py:11
  21.6 2.8 %collective-permute-start.4 = (f32[1,768]{1,0:T(1,128)}, f32[1,768]{1,0:T(1,128)S(1)}, u32[]{:S(2)}, u32[]{:S(2)}) collective-permute-start(f32[1,768]{1,0:T(1,128)} %get-tuple-element.37), channel_id=1, source_target_pairs={{0,8},{4,12},{8,0},{12,4},{1,9},{5,13},{9,1},{13,5},{2,10},{6,14},... | collective-permute-start | bytes 9224 | tf_op jit(solution)/shard_map/ppermute | solution.py:11
  24.5 2.2 %collective-permute-start.5 = (f32[1,768]{1,0:T(1,128)}, f32[1,768]{1,0:T(1,128)S(1)}, u32[]{:S(2)}, u32[]{:S(2)}) collective-permute-start(f32[1,768]{1,0:T(1,128)} %get-tuple-element.38), channel_id=1, source_target_pairs={{0,12},{4,8},{8,4},{12,0},{1,13},{5,9},{9,5},{13,1},{2,14},{6,10},... | collective-permute-start | bytes 9224 | tf_op jit(solution)/shard_map/ppermute | solution.py:11
  28.2 9.3 %collective-permute-done.4.refs_6_ = f32[1,768]{1,0:T(1,128)S(1)} collective-permute-done((f32[1,768]{1,0:T(1,128)}, f32[1,768]{1,0:T(1,128)S(1)}, u32[]{:S(2)}, u32[]{:S(2)}) %collective-permute-start.4) | collective-permute-done | bytes 3104 | tf_op jit(solution)/shard_map/ppermute | solution.py:11
  40.1 5.2 %collective-permute-done.8.refs_13_ = bf16[112,1536]{1,0:T(8,128)(2,1)} collective-permute-done((bf16[112,1536]{1,0:T(8,128)(2,1)}, bf16[112,1536]{1,0:T(8,128)(2,1)}, u32[]{:S(2)}, u32[]{:S(2)}) %collective-permute-start.8) | collective-permute-done | bytes 344096 | tf_op jit(solution)/shard_map/ppermute | solution.py:11
  48.9 8.1 %generate.1 = (f32[4,64,768]{2,1,0:T(8,128)}, bf16[768,1536]{1,0:T(8,128)(2,1)}, bf16[256,1536]{1,0:T(8,128)(2,1)}, f32[4,1,768]{2,1,0:T(1,128)}, f32[4,1,64]{2,...) custom-call(bf16[64,2304]{1,0:T(8,128)(2,1)} %get-tuple-element.31.refs_0_, ...), custom_call_target="tpu_custom_call" | custom-call | flops 603979776 | bytes 4718592 | tf_op jit(solution)/shard_map/generate/pallas_call | solution.py:167
  57.1 1.3 collective-permute-start.15
  58.4 3.0 %collective-permute-start.16 = (f32[4,64]{1,0:T(4,128)}, f32[4,64]{1,0:T(4,128)S(1)}, u32[]{:S(2)}, u32[]{:S(2)}) collective-permute-start(f32[4,64]{1,0:T(4,128)} %bitcast.35), channel_id=1, source_target_pairs={{0,8},{4,12},{8,0},{12,4},{1,9},{5,13},{9,1},{13,5},{2,10},{6,14},... | collective-permute-start | bytes 3080 | tf_op jit(solution)/shard_map/ppermute | solution.py:11
  64.9 3.9 %collective-permute-start.19 = (f16[64,1536]{1,0:T(8,128)(2,1)S(1)}, f16[64,1536]{1,0:T(8,128)(2,1)S(1)}, u32[]{:S(2)}, u32[]{:S(2)}) collective-permute-start(f16[64,1536]{1,0:T(8,128)(2,1)S(1)} %convert_element_type.78), channel_id=1, source_target_pairs={{0,8},{4,12},{8,0},{12,4},{1,9},{5,13},{9,1},{13,5},{2,10},{6,14},... | collective-permute-start | bytes 589832 | tf_op jit(solution)/shard_map/ppermute | solution.py:11
  70.1 2.2 %collective-permute-done.18 = f16[64,1536]{1,0:T(8,128)(2,1)S(1)} collective-permute-done((f16[64,1536]{1,0:T(8,128)(2,1)S(1)}, f16[64,1536]{1,0:T(8,128)(2,1)S(1)}, u32[]{:S(2)}, u32[]{:S(2)}) %collective-permute-start.18) | collective-permute-done | bytes 196640 | tf_op jit(solution)/shard_map/ppermute | solution.py:11
  72.2 10.6 %collective-permute-done.19 = f16[64,1536]{1,0:T(8,128)(2,1)S(1)} collective-permute-done((f16[64,1536]{1,0:T(8,128)(2,1)S(1)}, f16[64,1536]{1,0:T(8,128)(2,1)S(1)}, u32[]{:S(2)}, u32[]{:S(2)}) %collective-permute-start.19) | collective-permute-done | bytes 196640 | tf_op jit(solution)/shard_map/ppermute | solution.py:11
  83.9 20.1 %all_gather.3 = bf16[256,1664]{1,0:T(8,128)(2,1)S(1)} all-gather(bf16[64,1664]{1,0:T(8,128)(2,1)S(1)} %pad_maximum_fusion.2), channel_id=1, replica_groups=mesh['grp'=2,'dp'=4,'seq'=4] {'dp'}, dimensions={0}, use_global_device_ids=true | all-gather | bytes 1064960 | tf_op jit(solution)/shard_map/all_gather | solution.py:302
  107.4 1.9 %collective-permute-done.21 = bf16[256,768]{1,0:T(8,128)(2,1)S(1)} collective-permute-done((bf16[256,768]{1,0:T(8,128)(2,1)S(1)}, bf16[256,768]{1,0:T(8,128)(2,1)S(1)}, u32[]{:S(2)}, u32[]{:S(2)}) %collective-permute-start.21) | collective-permute-done | bytes 393248 | tf_op jit(solution)/shard_map/ppermute | solution.py:11
  109.3 1.4 %fusion = f32[768,1536]{1,0:T(8,128)S(1)} fusion(bf16[256,1536]{1,0:T(8,128)(2,1)S(1)} %collective-permute-done.22, bf16[256,1536]{1,0:T(8,128)(2,1)S(1)} %get-tuple-element.73, bf16[256,768]{1,0:T(8,128)(2,1)S(1)} %collective-permute-done.21, bf16[256,768]{1,0:T(8,128)(2,1)S(1)} %bitcast.31), kind=kOutput, calls=%fused_computation | convolution fusion | flops 1212678144 | bytes 7077888 | tf_op jit(solution)/shard_map/td,th->dh/dot_general | solution.py:319
  111.2 1.3 collective-permute-start.24
  113.0 13.6 %collective-permute-done.24 = bf16[192,1536]{1,0:T(8,128)(2,1)S(1)} collective-permute-done((bf16[192,1536]{1,0:T(8,128)(2,1)S(1)}, bf16[192,1536]{1,0:T(8,128)(2,1)S(1)}, u32[]{:S(2)}, u32[]{:S(2)}) %collective-permute-start.24) | collective-permute-done | bytes 589856 | tf_op jit(solution)/shard_map/ppermute | solution.py:11
  129.0 6.6 %collective-permute-done.25 = bf16[96,1536]{1,0:T(8,128)(2,1)S(1)} collective-permute-done((bf16[96,1536]{1,0:T(8,128)(2,1)S(1)}, bf16[96,1536]{1,0:T(8,128)(2,1)S(1)}, u32[]{:S(2)}, u32[]{:S(2)}) %collective-permute-start.25) | collective-permute-done | bytes 294944 | tf_op jit(solution)/shard_map/ppermute | solution.py:11
  136.2 1.1 maximum_bitcast_fusion
  (109 shorter events, 21.1 us)
Async XLA Ops:
  3.0 18.6 %collective-permute-start.6 = (bf16[224,1536]{1,0:T(8,128)(2,1)}, bf16[224,1536]{1,0:T(8,128)(2,1)S(1)}, u32[]{:S(2)}, u32[]{:S(2)}) collective-permute-start(bf16[224,1536]{1,0:T(8,128)(2,1)} %get-tuple-element.39.refs_10_), channel_id=1, source_target_pairs={{0,1},{1,0},{2,3},{3,2},{4,5},{5,4},{6,7},{7,6},{8,9},{9,8},{10,11... | collective-permute-start | bytes 2064392 | tf_op jit(solution)/shard_map/ppermute | solution.py:11
  6.0 18.5 %collective-permute-start.7 = (bf16[224,1536]{1,0:T(8,128)(2,1)}, bf16[224,1536]{1,0:T(8,128)(2,1)S(1)}, u32[]{:S(2)}, u32[]{:S(2)}) collective-permute-start(bf16[224,1536]{1,0:T(8,128)(2,1)} %get-tuple-element.39.refs_10_), channel_id=1, source_target_pairs={{0,2},{1,3},{2,0},{3,1},{4,6},{5,7},{6,4},{7,5},{8,10},{9,11},{10,... | collective-permute-start | bytes 2064392 | tf_op jit(solution)/shard_map/ppermute | solution.py:11
  7.5 4.6 %collective-permute-start.3 = (f32[1,768]{1,0:T(1,128)}, f32[1,768]{1,0:T(1,128)S(1)}, u32[]{:S(2)}, u32[]{:S(2)}) collective-permute-start(f32[1,768]{1,0:T(1,128)} %get-tuple-element.36), channel_id=1, source_target_pairs={{0,4},{4,0},{8,12},{12,8},{1,5},{5,1},{9,13},{13,9},{2,6},{6,2},{1... | collective-permute-start | bytes 9224 | tf_op jit(solution)/shard_map/ppermute | solution.py:11
  9.1 29.4 %collective-permute-start = (bf16[64,2304]{1,0:T(8,128)(2,1)}, bf16[64,2304]{1,0:T(8,128)(2,1)S(1)}, u32[]{:S(2)}, u32[]{:S(2)}) collective-permute-start(bf16[64,2304]{1,0:T(8,128)(2,1)} %get-tuple-element.32), channel_id=1, source_target_pairs={{0,4},{4,0},{8,12},{12,8},{1,5},{5,1},{9,13},{13,9},{2,6},{6,2},{1... | collective-permute-start | bytes 884744 | tf_op jit(solution)/shard_map/ppermute | solution.py:11
  9.5 29.0 %collective-permute-start.1 = (bf16[64,2304]{1,0:T(8,128)(2,1)}, bf16[64,2304]{1,0:T(8,128)(2,1)S(1)}, u32[]{:S(2)}, u32[]{:S(2)}) collective-permute-start(bf16[64,2304]{1,0:T(8,128)(2,1)} %get-tuple-element.33), channel_id=1, source_target_pairs={{0,8},{4,12},{8,0},{12,4},{1,9},{5,13},{9,1},{13,5},{2,10},{6,14},... | collective-permute-start | bytes 884744 | tf_op jit(solution)/shard_map/ppermute | solution.py:11
  12.1 27.1 %collective-permute-start.2 = (bf16[64,2304]{1,0:T(8,128)(2,1)}, bf16[64,2304]{1,0:T(8,128)(2,1)S(1)}, u32[]{:S(2)}, u32[]{:S(2)}) collective-permute-start(bf16[64,2304]{1,0:T(8,128)(2,1)} %get-tuple-element.34), channel_id=1, source_target_pairs={{0,12},{4,8},{8,4},{12,0},{1,13},{5,9},{9,5},{13,1},{2,14},{6,10},... | collective-permute-start | bytes 884744 | tf_op jit(solution)/shard_map/ppermute | solution.py:11
  21.6 15.9 %collective-permute-start.4 = (f32[1,768]{1,0:T(1,128)}, f32[1,768]{1,0:T(1,128)S(1)}, u32[]{:S(2)}, u32[]{:S(2)}) collective-permute-start(f32[1,768]{1,0:T(1,128)} %get-tuple-element.37), channel_id=1, source_target_pairs={{0,8},{4,12},{8,0},{12,4},{1,9},{5,13},{9,1},{13,5},{2,10},{6,14},... | collective-permute-start | bytes 9224 | tf_op jit(solution)/shard_map/ppermute | solution.py:11
  24.5 13.5 %collective-permute-start.5 = (f32[1,768]{1,0:T(1,128)}, f32[1,768]{1,0:T(1,128)S(1)}, u32[]{:S(2)}, u32[]{:S(2)}) collective-permute-start(f32[1,768]{1,0:T(1,128)} %get-tuple-element.38), channel_id=1, source_target_pairs={{0,12},{4,8},{8,4},{12,0},{1,13},{5,9},{9,5},{13,1},{2,14},{6,10},... | collective-permute-start | bytes 9224 | tf_op jit(solution)/shard_map/ppermute | solution.py:11
  37.5 7.9 %collective-permute-start.8 = (bf16[112,1536]{1,0:T(8,128)(2,1)}, bf16[112,1536]{1,0:T(8,128)(2,1)}, u32[]{:S(2)}, u32[]{:S(2)}) collective-permute-start(bf16[112,1536]{1,0:T(8,128)(2,1)} %slice.32), channel_id=1, source_target_pairs={{0,2},{1,3},{2,0},{3,1},{4,6},{5,7},{6,4},{7,5},{8,10},{9,11},{10,... | collective-permute-start | bytes 1032200 | tf_op jit(solution)/shard_map/ppermute | solution.py:11
  38.0 7.6 %collective-permute-start.9 = (bf16[112,1536]{1,0:T(8,128)(2,1)}, bf16[112,1536]{1,0:T(8,128)(2,1)}, u32[]{:S(2)}, u32[]{:S(2)}) collective-permute-start(bf16[112,1536]{1,0:T(8,128)(2,1)} %slice.33), channel_id=1, source_target_pairs={{0,1},{1,0},{2,3},{3,2},{4,5},{5,4},{6,7},{7,6},{8,9},{9,8},{10,11... | collective-permute-start | bytes 1032200 | tf_op jit(solution)/shard_map/ppermute | solution.py:11
  38.5 8.1 %collective-permute-start.10 = (bf16[224,1536]{1,0:T(8,128)(2,1)}, bf16[224,1536]{1,0:T(8,128)(2,1)S(1)}, u32[]{:S(2)}, u32[]{:S(2)}) collective-permute-start(bf16[224,1536]{1,0:T(8,128)(2,1)} %get-tuple-element.39.refs_10_), channel_id=1, source_target_pairs={{0,16},{16,0},{1,17},{17,1},{2,18},{18,2},{3,19},{19,3},{4,20},{20... | collective-permute-start | bytes 2064392 | tf_op jit(solution)/shard_map/ppermute | solution.py:11
  38.5 9.3 %collective-permute-start.11 = (bf16[224,1536]{1,0:T(8,128)(2,1)S(1)}, bf16[224,1536]{1,0:T(8,128)(2,1)S(1)}, u32[]{:S(2)}, u32[]{:S(2)}) collective-permute-start(bf16[224,1536]{1,0:T(8,128)(2,1)S(1)} %collective-permute-done.6.refs_11_), channel_id=1, source_target_pairs={{0,16},{16,0},{1,17},{17,1},{2,18},{18,2},{3,19},{19,3},{4,20},{20... | collective-permute-start | bytes 2064392 | tf_op jit(solution)/shard_map/ppermute | solution.py:11
  39.3 8.5 %collective-permute-start.12 = (bf16[224,1536]{1,0:T(8,128)(2,1)S(1)}, bf16[224,1536]{1,0:T(8,128)(2,1)S(1)}, u32[]{:S(2)}, u32[]{:S(2)}) collective-permute-start(bf16[224,1536]{1,0:T(8,128)(2,1)S(1)} %collective-permute-done.7.refs_12_), channel_id=1, source_target_pairs={{0,16},{16,0},{1,17},{17,1},{2,18},{18,2},{3,19},{19,3},{4,20},{20... | collective-permute-start | bytes 2064392 | tf_op jit(solution)/shard_map/ppermute | solution.py:11
  57.1 12.7 %collective-permute-start.15 = (f32[4,64]{1,0:T(4,128)}, f32[4,64]{1,0:T(4,128)S(1)}, u32[]{:S(2)}, u32[]{:S(2)}) collective-permute-start(f32[4,64]{1,0:T(4,128)} %bitcast.34), channel_id=1, source_target_pairs={{0,4},{4,0},{8,12},{12,8},{1,5},{5,1},{9,13},{13,9},{2,6},{6,2},{1... | collective-permute-start | bytes 3080 | tf_op jit(solution)/shard_map/ppermute | solution.py:11
  58.4 11.6 %collective-permute-start.16 = (f32[4,64]{1,0:T(4,128)}, f32[4,64]{1,0:T(4,128)S(1)}, u32[]{:S(2)}, u32[]{:S(2)}) collective-permute-start(f32[4,64]{1,0:T(4,128)} %bitcast.35), channel_id=1, source_target_pairs={{0,8},{4,12},{8,0},{12,4},{1,9},{5,13},{9,1},{13,5},{2,10},{6,14},... | collective-permute-start | bytes 3080 | tf_op jit(solution)/shard_map/ppermute | solution.py:11
  61.5 8.5 %collective-permute-start.17 = (f32[4,64]{1,0:T(4,128)}, f32[4,64]{1,0:T(4,128)S(1)}, u32[]{:S(2)}, u32[]{:S(2)}) collective-permute-start(f32[4,64]{1,0:T(4,128)} %bitcast.36), channel_id=1, source_target_pairs={{0,12},{4,8},{8,4},{12,0},{1,13},{5,9},{9,5},{13,1},{2,14},{6,10},... | collective-permute-start | bytes 3080 | tf_op jit(solution)/shard_map/ppermute | solution.py:11
  63.3 8.9 %collective-permute-start.18 = (f16[64,1536]{1,0:T(8,128)(2,1)S(1)}, f16[64,1536]{1,0:T(8,128)(2,1)S(1)}, u32[]{:S(2)}, u32[]{:S(2)}) collective-permute-start(f16[64,1536]{1,0:T(8,128)(2,1)S(1)} %convert_element_type.76), channel_id=1, source_target_pairs={{0,4},{4,0},{8,12},{12,8},{1,5},{5,1},{9,13},{13,9},{2,6},{6,2},{1... | collective-permute-start | bytes 589832 | tf_op jit(solution)/shard_map/ppermute | solution.py:11
  64.9 18.0 %collective-permute-start.19 = (f16[64,1536]{1,0:T(8,128)(2,1)S(1)}, f16[64,1536]{1,0:T(8,128)(2,1)S(1)}, u32[]{:S(2)}, u32[]{:S(2)}) collective-permute-start(f16[64,1536]{1,0:T(8,128)(2,1)S(1)} %convert_element_type.78), channel_id=1, source_target_pairs={{0,8},{4,12},{8,0},{12,4},{1,9},{5,13},{9,1},{13,5},{2,10},{6,14},... | collective-permute-start | bytes 589832 | tf_op jit(solution)/shard_map/ppermute | solution.py:11
  69.8 13.0 %collective-permute-start.20 = (f16[64,1536]{1,0:T(8,128)(2,1)S(1)}, f16[64,1536]{1,0:T(8,128)(2,1)S(1)}, u32[]{:S(2)}, u32[]{:S(2)}) collective-permute-start(f16[64,1536]{1,0:T(8,128)(2,1)S(1)} %convert_element_type.80), channel_id=1, source_target_pairs={{0,12},{4,8},{8,4},{12,0},{1,13},{5,9},{9,5},{13,1},{2,14},{6,10},... | collective-permute-start | bytes 589832 | tf_op jit(solution)/shard_map/ppermute | solution.py:11
  106.3 3.1 %collective-permute-start.22 = (bf16[256,1536]{1,0:T(8,128)(2,1)}, bf16[256,1536]{1,0:T(8,128)(2,1)S(1)}, u32[]{:S(2)}, u32[]{:S(2)}) collective-permute-start(bf16[256,1536]{1,0:T(8,128)(2,1)} %get-tuple-element.74), channel_id=1, source_target_pairs={{0,16},{16,0},{1,17},{17,1},{2,18},{18,2},{3,19},{19,3},{4,20},{20... | collective-permute-start | bytes 2359304 | tf_op jit(solution)/shard_map/ppermute | solution.py:11
  111.2 15.4 %collective-permute-start.24 = (bf16[192,1536]{1,0:T(8,128)(2,1)S(1)}, bf16[192,1536]{1,0:T(8,128)(2,1)S(1)}, u32[]{:S(2)}, u32[]{:S(2)}) collective-permute-start(bf16[192,1536]{1,0:T(8,128)(2,1)S(1)} %pad_maximum_fusion.1), channel_id=1, source_target_pairs={{0,2},{1,3},{2,0},{3,1},{4,6},{5,7},{6,4},{7,5},{8,10},{9,11},{10,... | collective-permute-start | bytes 1769480 | tf_op jit(solution)/shard_map/ppermute | solution.py:11
  112.5 15.1 %collective-permute-start.23 = (bf16[192,1536]{1,0:T(8,128)(2,1)S(1)}, bf16[192,1536]{1,0:T(8,128)(2,1)S(1)}, u32[]{:S(2)}, u32[]{:S(2)}) collective-permute-start(bf16[192,1536]{1,0:T(8,128)(2,1)S(1)} %pad_maximum_fusion), channel_id=1, source_target_pairs={{0,1},{1,0},{2,3},{3,2},{4,5},{5,4},{6,7},{7,6},{8,9},{9,8},{10,11... | collective-permute-start | bytes 1769480 | tf_op jit(solution)/shard_map/ppermute | solution.py:11
  127.7 8.0 %collective-permute-start.25 = (bf16[96,1536]{1,0:T(8,128)(2,1)S(1)}, bf16[96,1536]{1,0:T(8,128)(2,1)S(1)}, u32[]{:S(2)}, u32[]{:S(2)}) collective-permute-start(bf16[96,1536]{1,0:T(8,128)(2,1)S(1)} %add_convert_fusion.1), channel_id=1, source_target_pairs={{0,2},{1,3},{2,0},{3,1},{4,6},{5,7},{6,4},{7,5},{8,10},{9,11},{10,... | collective-permute-start | bytes 884744 | tf_op jit(solution)/shard_map/ppermute | solution.py:11
  128.5 7.6 %collective-permute-start.26 = (bf16[96,1536]{1,0:T(8,128)(2,1)S(1)}, bf16[96,1536]{1,0:T(8,128)(2,1)S(1)}, u32[]{:S(2)}, u32[]{:S(2)}) collective-permute-start(bf16[96,1536]{1,0:T(8,128)(2,1)S(1)} %add_convert_fusion), channel_id=1, source_target_pairs={{0,1},{1,0},{2,3},{3,2},{4,5},{5,4},{6,7},{7,6},{8,9},{9,8},{10,11... | collective-permute-start | bytes 884744 | tf_op jit(solution)/shard_map/ppermute | solution.py:11
  (22 other events, 258.6 us)

commit v5 on v4

--- a/solution.py
+++ b/solution.py
@@ -52,20 +52,29 @@
     half = width // grps
     strip = length * half // depth
 
-    def kernel(attended_ref, latents_ref, gating_ref, weight_ref, positions_ref, *outs):
+    def kernel(attended_ref, latents_ref, gating_ref, weight_ref, positions_ref, *refs):
+        outs, sems = refs[:-1], refs[-1]
         grp, dp = lax.axis_index("grp"), lax.axis_index("dp")
         row = pl.ds(pl.multiple_of(grp * rows, 16), rows)
-        for k in range(dps):
-            column = pl.ds(pl.multiple_of((dp ^ k) * width, 128), width)
-            outs[k][:, :depth] = attended_ref[row, :]
-            outs[k][:, depth:] = latents_ref[row, column]
-            outs[dps + k][...] = gating_ref[:, column]
-        outs[-1][:size, :] = weight_ref[...]
+        moves = [(weight_ref, outs[-1].at[:size])]
         if size % 16 == 0:
             column = pl.ds(pl.multiple_of(dp * width + grp * half, 128), half)
             for i in range(length // strip):
-                lines = positions_ref[i * strip : (i + 1) * strip, column]
-                outs[-1][size:, i * half : (i + 1) * half] = lines
+                lines = positions_ref.at[i * strip : (i + 1) * strip, column]
+                moves.append((lines, outs[-1].at[size:, i * half : (i + 1) * half]))
+        for k in range(dps):
+            column = pl.ds(pl.multiple_of((dp ^ k) * width, 128), width)
+            moves.append((attended_ref.at[row, :], outs[k].at[:, :depth]))
+            moves.append((latents_ref.at[row, column], outs[k].at[:, depth:]))
+            moves.append((gating_ref.at[:, column], outs[dps + k]))
+        copies = [
+            pltpu.make_async_copy(source, target, sems.at[i])
+            for i, (source, target) in enumerate(moves)
+        ]
+        for copy in copies:
+            copy.start()
+        for copy in copies:
+            copy.wait()
 
     bf16, f32 = jnp.bfloat16, jnp.float32
     packed = pl.pallas_call(
@@ -73,8 +82,9 @@
         out_shape=[jax.ShapeDtypeStruct((rows, depth + width), bf16)] * dps
         + [jax.ShapeDtypeStruct((1, width), f32)] * dps
         + [jax.ShapeDtypeStruct((size + strip, depth), bf16)],
-        in_specs=[VMEM] * 5,
+        in_specs=[pl.BlockSpec(memory_space=pltpu.HBM)] * 5,
         out_specs=[VMEM] * (2 * dps + 1),
+        scratch_shapes=[pltpu.SemaphoreType.DMA((3 * dps + 1 + length // strip,))],
         name="pack",
     )(attended, latents, gating, weight, positions)
     return list(packed[:dps]), list(packed[dps:-1]), packed[-1]
@@ -94,7 +104,7 @@
         own_refs, twin_refs, refs = refs[:parts], refs[parts : 2 * parts], refs[2 * parts :]
         given_refs, refs = refs[: len(tables)], refs[len(tables) :]
         out_ref, critic_ref, tokens_ref, gates_ref, square_ref, *refs = refs
-        block_refs, (maker_ref, high_ref, low_ref, table_ref) = refs[:clips], refs[clips:]
+        block_refs, (maker_ref, terms_ref, table_ref) = refs[:clips], refs[clips:]
         grp, dp = lax.axis_index("grp"), lax.axis_index("dp")
         seq = lax.axis_index("seq") if aligned else 0
 
@@ -154,13 +164,11 @@
             mean = jnp.sum(sums, axis=1, keepdims=True) / channels
             scaled = values * lax.rsqrt(mean + 1e-06) * gain_row
             high = scaled.astype(jnp.bfloat16)
-            high_ref[k * rows : (k + 1) * rows] = high
+            terms_ref[k * rows : (k + 1) * rows] = high
             low = scaled - high.astype(jnp.float32)
-            low_ref[k * rows : (k + 1) * rows] = low.astype(jnp.bfloat16)
-        partial = jnp.dot(high_ref[...], critic_ref[...], preferred_element_type=jnp.float32)
-        partial = partial + jnp.dot(
-            low_ref[...], critic_ref[...], preferred_element_type=jnp.float32
-        )
+            terms_ref[(clips + k) * rows : (clips + k + 1) * rows] = low.astype(jnp.bfloat16)
+        both = jnp.dot(terms_ref[...], critic_ref[...], preferred_element_type=jnp.float32)
+        partial = both[: clips * rows] + both[clips * rows :]
         for k in range(clips):
             block_refs[k][...] = partial[k * rows : (k + 1) * rows].astype(block_refs[k].dtype)
 
@@ -178,8 +186,7 @@
         out_specs=[VMEM] * (5 + clips),
         scratch_shapes=[
             pltpu.VMEM((width, depth), jnp.bfloat16),
-            pltpu.VMEM((clips * rows, width), jnp.bfloat16),
-            pltpu.VMEM((clips * rows, width), jnp.bfloat16),
+            pltpu.VMEM((2 * clips * rows, width), jnp.bfloat16),
             pltpu.VMEM((lines, half), jnp.bfloat16),
         ],
         cost_estimate=pl.CostEstimate(
@@ -187,6 +194,7 @@
             bytes_accessed=2 * depth * (width + clips * rows) + 8 * clips * rows * width,
             transcendentals=0,
         ),
+        compiler_params=pltpu.CompilerParams(vmem_limit_bytes=49 * 2**20),
         name="generate",
     )(*messages, *gates, picks, gain[None, :], *own_weight, *twin_weight, *tables)
 

time: 138 us -> 137 us (level)
  local copies, waits for them, and re-layouts: 5.01 us -> 11.4 us
  other arithmetic: 8.03 us -> 4.41 us
  Pallas kernels: 11.1 us -> 9.05 us
    unnamed x39 -> x37, local copies, waits for them, and re-layouts: 2.26 us -> 9.05 us
    convert_element_type x3, other arithmetic: 3.05 us -> 0.07 us  [shards(): term = terms[k].astype(f16)]
    pallas_call x1, Pallas kernels: 8.12 us -> 5.95 us  [generate(): pl.pallas_call(kernel, out_shape=[jax.ShapeDtypeStruct((clips, rows, chan...]
  transfers between devices with their start and end apart: 27 -> 27, of which waited for: 13 -> 14; matrix products, arithmetic and copies ran while one was open for 5% -> 2% of each run, Pallas kernels for 0% -> 0%
where the time goes in v5:
time: 137 us
  waiting for transfers between devices  58.7 us (43%)
  starting transfers between devices  30.9 us (23%)
  blocking collectives  20 us (15%)
  local copies, waits for them, and re-layouts  11.4 us (8%)
  Pallas kernels  9.05 us (7%)
  other arithmetic  4.41 us (3%)
  matrix products  2.23 us (2%)
    ppermute x27, waiting for transfers between devices, hop(): return lax.ppermute(block, axis, route)  58.7 us
    ppermute x27, starting transfers between devices, hop(): return lax.ppermute(block, axis, route)  30.9 us
    all_gather x1, blocking collectives, shards(): lax.all_gather(jnp.concatenate([hidden_grad, tail], axis=1), 'dp', axis=0...  20 us
    unnamed x37, local copies, waits for them, and re-layouts  9.05 us
    pallas_call x1, Pallas kernels, generate(): pl.pallas_call(kernel, out_shape=[jax.ShapeDtypeStruct((clips, rows, chan...  5.95 us
    pallas_call x1, Pallas kernels, pack(): pl.pallas_call(kernel, out_shape=[jax.ShapeDtypeStruct((rows, depth + wid...  3.1 us
  transfers between devices with their start and end apart: 27, of which 14 were waited for; matrix products, arithmetic and copies ran while one was open for 2% of the time, Pallas kernels for 0%

profile of v5, /device:TPU:0, one launch (start us, length us, event | category | flops | bytes accessed | tf_op | source)
XLA Modules:
  0.0 136.9 jit_solution(7242607536643383415)
XLA Ops:
  0.0 3.1 %pack.1 = (bf16[64,2304]{1,0:T(8,128)(2,1)}, bf16[64,2304]{1,0:T(8,128)(2,1)}, bf16[64,2304]{1,0:T(8,128)(2,1)}, bf16[64,2304]{1,0:T(8,128)(2,1)}, f32[1,768]{1,...) custom-call(bf16[128,1536]{1,0:T(8,128)(2,1)} %bitcast.34, ...), custom_call_target="tpu_custom_call" | custom-call | tf_op jit(solution)/shard_map/pack/pallas_call | solution.py:80
  3.1 3.0 %collective-permute-start.6 = (bf16[224,1536]{1,0:T(8,128)(2,1)}, bf16[224,1536]{1,0:T(8,128)(2,1)S(1)}, u32[]{:S(2)}, u32[]{:S(2)}) collective-permute-start(bf16[224,1536]{1,0:T(8,128)(2,1)} %get-tuple-element.39.refs_10_), channel_id=1, source_target_pairs={{0,1},{1,0},{2,3},{3,2},{4,5},{5,4},{6,7},{7,6},{8,9},{9,8},{10,11... | collective-permute-start | bytes 2064392 | tf_op jit(solution)/shard_map/ppermute | solution.py:11
  6.2 1.5 %collective-permute-start.7 = (bf16[224,1536]{1,0:T(8,128)(2,1)}, bf16[224,1536]{1,0:T(8,128)(2,1)}, u32[]{:S(2)}, u32[]{:S(2)}) collective-permute-start(bf16[224,1536]{1,0:T(8,128)(2,1)} %get-tuple-element.39.refs_10_), channel_id=1, source_target_pairs={{0,2},{1,3},{2,0},{3,1},{4,6},{5,7},{6,4},{7,5},{8,10},{9,11},{10,... | collective-permute-start | bytes 2064392 | tf_op jit(solution)/shard_map/ppermute | solution.py:11
  7.7 1.6 %collective-permute-start.3 = (f32[1,768]{1,0:T(1,128)}, f32[1,768]{1,0:T(1,128)S(1)}, u32[]{:S(2)}, u32[]{:S(2)}) collective-permute-start(f32[1,768]{1,0:T(1,128)} %get-tuple-element.36), channel_id=1, source_target_pairs={{0,4},{4,0},{8,12},{12,8},{1,5},{5,1},{9,13},{13,9},{2,6},{6,2},{1... | collective-permute-start | bytes 9224 | tf_op jit(solution)/shard_map/ppermute | solution.py:11
  9.7 2.6 %collective-permute-start.1 = (bf16[64,2304]{1,0:T(8,128)(2,1)}, bf16[64,2304]{1,0:T(8,128)(2,1)S(1)}, u32[]{:S(2)}, u32[]{:S(2)}) collective-permute-start(bf16[64,2304]{1,0:T(8,128)(2,1)} %get-tuple-element.33), channel_id=1, source_target_pairs={{0,8},{4,12},{8,0},{12,4},{1,9},{5,13},{9,1},{13,5},{2,10},{6,14},... | collective-permute-start | bytes 884744 | tf_op jit(solution)/shard_map/ppermute | solution.py:11
  12.3 2.8 %collective-permute-start.2 = (bf16[64,2304]{1,0:T(8,128)(2,1)}, bf16[64,2304]{1,0:T(8,128)(2,1)S(1)}, u32[]{:S(2)}, u32[]{:S(2)}) collective-permute-start(bf16[64,2304]{1,0:T(8,128)(2,1)} %get-tuple-element.34), channel_id=1, source_target_pairs={{0,12},{4,8},{8,4},{12,0},{1,13},{5,9},{9,5},{13,1},{2,14},{6,10},... | collective-permute-start | bytes 884744 | tf_op jit(solution)/shard_map/ppermute | solution.py:11
  15.1 6.5 %collective-permute-done.6.refs_11_ = bf16[224,1536]{1,0:T(8,128)(2,1)S(1)} collective-permute-done((bf16[224,1536]{1,0:T(8,128)(2,1)}, bf16[224,1536]{1,0:T(8,128)(2,1)S(1)}, u32[]{:S(2)}, u32[]{:S(2)}) %collective-permute-start.6) | collective-permute-done | bytes 688160 | tf_op jit(solution)/shard_map/ppermute | solution.py:11
  21.6 2.8 %collective-permute-start.4 = (f32[1,768]{1,0:T(1,128)}, f32[1,768]{1,0:T(1,128)S(1)}, u32[]{:S(2)}, u32[]{:S(2)}) collective-permute-start(f32[1,768]{1,0:T(1,128)} %get-tuple-element.37), channel_id=1, source_target_pairs={{0,8},{4,12},{8,0},{12,4},{1,9},{5,13},{9,1},{13,5},{2,10},{6,14},... | collective-permute-start | bytes 9224 | tf_op jit(solution)/shard_map/ppermute | solution.py:11
  24.4 2.3 %collective-permute-start.5 = (f32[1,768]{1,0:T(1,128)}, f32[1,768]{1,0:T(1,128)S(1)}, u32[]{:S(2)}, u32[]{:S(2)}) collective-permute-start(f32[1,768]{1,0:T(1,128)} %get-tuple-element.38), channel_id=1, source_target_pairs={{0,12},{4,8},{8,4},{12,0},{1,13},{5,9},{9,5},{13,1},{2,14},{6,10},... | collective-permute-start | bytes 9224 | tf_op jit(solution)/shard_map/ppermute | solution.py:11
  26.8 1.7 %slice.33 = bf16[112,1536]{1,0:T(8,128)(2,1)} slice(bf16[224,1536]{1,0:T(8,128)(2,1)} %collective-permute-done.7.refs_12_), slice={[112:224], [0:1536]} | slice | bytes 688128 | tf_op jit(solution)/shard_map/slice | solution.py:34
  28.5 9.0 %collective-permute-done.4.refs_6_ = f32[1,768]{1,0:T(1,128)S(1)} collective-permute-done((f32[1,768]{1,0:T(1,128)}, f32[1,768]{1,0:T(1,128)S(1)}, u32[]{:S(2)}, u32[]{:S(2)}) %collective-permute-start.4) | collective-permute-done | bytes 3104 | tf_op jit(solution)/shard_map/ppermute | solution.py:11
  41.3 3.6 %collective-permute-done.8.refs_13_ = bf16[112,1536]{1,0:T(8,128)(2,1)S(1)} collective-permute-done((bf16[112,1536]{1,0:T(8,128)(2,1)S(1)}, bf16[112,1536]{1,0:T(8,128)(2,1)S(1)}, u32[]{:S(2)}, u32[]{:S(2)}) %collective-permute-start.8) | collective-permute-done | bytes 344096 | tf_op jit(solution)/shard_map/ppermute | solution.py:11
  53.4 5.9 %generate.1 = (f32[4,64,768]{2,1,0:T(8,128)}, bf16[768,1536]{1,0:T(8,128)(2,1)}, bf16[256,1536]{1,0:T(8,128)(2,1)}, f32[4,1,768]{2,1,0:T(1,128)S(1)}, f32[4,1,64...) custom-call(bf16[64,2304]{1,0:T(8,128)(2,1)S(1)} %copy-done.3, ...), custom_call_target="tpu_custom_call" | custom-call | flops 603979776 | bytes 4718592 | tf_op jit(solution)/shard_map/generate/pallas_call | solution.py:175
  59.4 1.2 collective-permute-start.15
  60.6 3.0 %collective-permute-start.16 = (f32[4,64]{1,0:T(4,128)S(1)}, f32[4,64]{1,0:T(4,128)S(1)}, u32[]{:S(2)}, u32[]{:S(2)}) collective-permute-start(f32[4,64]{1,0:T(4,128)S(1)} %bitcast.28), channel_id=1, source_target_pairs={{0,8},{4,12},{8,0},{12,4},{1,9},{5,13},{9,1},{13,5},{2,10},{6,14},... | collective-permute-start | bytes 3080 | tf_op jit(solution)/shard_map/ppermute | solution.py:11
  64.5 3.8 %collective-permute-start.19 = (f16[64,1536]{1,0:T(8,128)(2,1)S(1)}, f16[64,1536]{1,0:T(8,128)(2,1)S(1)}, u32[]{:S(2)}, u32[]{:S(2)}) collective-permute-start(f16[64,1536]{1,0:T(8,128)(2,1)S(1)} %convert_element_type.78), channel_id=1, source_target_pairs={{0,8},{4,12},{8,0},{12,4},{1,9},{5,13},{9,1},{13,5},{2,10},{6,14},... | collective-permute-start | bytes 589832 | tf_op jit(solution)/shard_map/ppermute | solution.py:11
  69.1 4.5 %collective-permute-done.18 = f16[64,1536]{1,0:T(8,128)(2,1)S(1)} collective-permute-done((f16[64,1536]{1,0:T(8,128)(2,1)S(1)}, f16[64,1536]{1,0:T(8,128)(2,1)S(1)}, u32[]{:S(2)}, u32[]{:S(2)}) %collective-permute-start.18) | collective-permute-done | bytes 196640 | tf_op jit(solution)/shard_map/ppermute | solution.py:11
  73.6 8.9 %collective-permute-done.19 = f16[64,1536]{1,0:T(8,128)(2,1)S(1)} collective-permute-done((f16[64,1536]{1,0:T(8,128)(2,1)S(1)}, f16[64,1536]{1,0:T(8,128)(2,1)S(1)}, u32[]{:S(2)}, u32[]{:S(2)}) %collective-permute-start.19) | collective-permute-done | bytes 196640 | tf_op jit(solution)/shard_map/ppermute | solution.py:11
  83.5 20.0 %all_gather.3 = bf16[256,1664]{1,0:T(8,128)(2,1)S(1)} all-gather(bf16[64,1664]{1,0:T(8,128)(2,1)S(1)} %pad_maximum_fusion.2), channel_id=1, replica_groups=mesh['grp'=2,'dp'=4,'seq'=4] {'dp'}, dimensions={0}, use_global_device_ids=true | all-gather | bytes 1064960 | tf_op jit(solution)/shard_map/all_gather | solution.py:310
  106.9 1.9 %collective-permute-done.21 = bf16[256,768]{1,0:T(8,128)(2,1)S(1)} collective-permute-done((bf16[256,768]{1,0:T(8,128)(2,1)S(1)}, bf16[256,768]{1,0:T(8,128)(2,1)S(1)}, u32[]{:S(2)}, u32[]{:S(2)}) %collective-permute-start.21) | collective-permute-done | bytes 393248 | tf_op jit(solution)/shard_map/ppermute | solution.py:11
  108.8 1.4 %fusion = f32[768,1536]{1,0:T(8,128)S(1)} fusion(bf16[256,1536]{1,0:T(8,128)(2,1)S(1)} %collective-permute-done.22, bf16[256,1536]{1,0:T(8,128)(2,1)S(1)} %get-tuple-element.73, bf16[256,768]{1,0:T(8,128)(2,1)S(1)} %collective-permute-done.21, bf16[256,768]{1,0:T(8,128)(2,1)S(1)} %bitcast.36), kind=kOutput, calls=%fused_computation | convolution fusion | flops 1212678144 | bytes 7077888 | tf_op jit(solution)/shard_map/td,th->dh/dot_general | solution.py:327
  110.7 1.5 %collective-permute-start.24 = (bf16[192,1536]{1,0:T(8,128)(2,1)S(1)}, bf16[192,1536]{1,0:T(8,128)(2,1)S(1)}, u32[]{:S(2)}, u32[]{:S(2)}) collective-permute-start(bf16[192,1536]{1,0:T(8,128)(2,1)S(1)} %pad_maximum_fusion.1), channel_id=1, source_target_pairs={{0,2},{1,3},{2,0},{3,1},{4,6},{5,7},{6,4},{7,5},{8,10},{9,11},{10,... | collective-permute-start | bytes 1769480 | tf_op jit(solution)/shard_map/ppermute | solution.py:11
  112.7 13.4 %collective-permute-done.24 = bf16[192,1536]{1,0:T(8,128)(2,1)S(1)} collective-permute-done((bf16[192,1536]{1,0:T(8,128)(2,1)S(1)}, bf16[192,1536]{1,0:T(8,128)(2,1)S(1)}, u32[]{:S(2)}, u32[]{:S(2)}) %collective-permute-start.24) | collective-permute-done | bytes 589856 | tf_op jit(solution)/shard_map/ppermute | solution.py:11
  128.5 6.8 %collective-permute-done.25 = bf16[96,1536]{1,0:T(8,128)(2,1)S(1)} collective-permute-done((bf16[96,1536]{1,0:T(8,128)(2,1)S(1)}, bf16[96,1536]{1,0:T(8,128)(2,1)S(1)}, u32[]{:S(2)}, u32[]{:S(2)}) %collective-permute-start.25) | collective-permute-done | bytes 294944 | tf_op jit(solution)/shard_map/ppermute | solution.py:11
  (107 shorter events, 23.7 us)
Async XLA Ops:
  3.1 18.5 %collective-permute-start.6 = (bf16[224,1536]{1,0:T(8,128)(2,1)}, bf16[224,1536]{1,0:T(8,128)(2,1)S(1)}, u32[]{:S(2)}, u32[]{:S(2)}) collective-permute-start(bf16[224,1536]{1,0:T(8,128)(2,1)} %get-tuple-element.39.refs_10_), channel_id=1, source_target_pairs={{0,1},{1,0},{2,3},{3,2},{4,5},{5,4},{6,7},{7,6},{8,9},{9,8},{10,11... | collective-permute-start | bytes 2064392 | tf_op jit(solution)/shard_map/ppermute | solution.py:11
  6.2 18.3 %collective-permute-start.7 = (bf16[224,1536]{1,0:T(8,128)(2,1)}, bf16[224,1536]{1,0:T(8,128)(2,1)}, u32[]{:S(2)}, u32[]{:S(2)}) collective-permute-start(bf16[224,1536]{1,0:T(8,128)(2,1)} %get-tuple-element.39.refs_10_), channel_id=1, source_target_pairs={{0,2},{1,3},{2,0},{3,1},{4,6},{5,7},{6,4},{7,5},{8,10},{9,11},{10,... | collective-permute-start | bytes 2064392 | tf_op jit(solution)/shard_map/ppermute | solution.py:11
  7.7 4.6 %collective-permute-start.3 = (f32[1,768]{1,0:T(1,128)}, f32[1,768]{1,0:T(1,128)S(1)}, u32[]{:S(2)}, u32[]{:S(2)}) collective-permute-start(f32[1,768]{1,0:T(1,128)} %get-tuple-element.36), channel_id=1, source_target_pairs={{0,4},{4,0},{8,12},{12,8},{1,5},{5,1},{9,13},{13,9},{2,6},{6,2},{1... | collective-permute-start | bytes 9224 | tf_op jit(solution)/shard_map/ppermute | solution.py:11
  9.2 29.2 %collective-permute-start = (bf16[64,2304]{1,0:T(8,128)(2,1)}, bf16[64,2304]{1,0:T(8,128)(2,1)S(1)}, u32[]{:S(2)}, u32[]{:S(2)}) collective-permute-start(bf16[64,2304]{1,0:T(8,128)(2,1)} %get-tuple-element.32), channel_id=1, source_target_pairs={{0,4},{4,0},{8,12},{12,8},{1,5},{5,1},{9,13},{13,9},{2,6},{6,2},{1... | collective-permute-start | bytes 884744 | tf_op jit(solution)/shard_map/ppermute | solution.py:11
  9.7 29.5 %collective-permute-start.1 = (bf16[64,2304]{1,0:T(8,128)(2,1)}, bf16[64,2304]{1,0:T(8,128)(2,1)S(1)}, u32[]{:S(2)}, u32[]{:S(2)}) collective-permute-start(bf16[64,2304]{1,0:T(8,128)(2,1)} %get-tuple-element.33), channel_id=1, source_target_pairs={{0,8},{4,12},{8,0},{12,4},{1,9},{5,13},{9,1},{13,5},{2,10},{6,14},... | collective-permute-start | bytes 884744 | tf_op jit(solution)/shard_map/ppermute | solution.py:11
  12.3 28.2 %collective-permute-start.2 = (bf16[64,2304]{1,0:T(8,128)(2,1)}, bf16[64,2304]{1,0:T(8,128)(2,1)S(1)}, u32[]{:S(2)}, u32[]{:S(2)}) collective-permute-start(bf16[64,2304]{1,0:T(8,128)(2,1)} %get-tuple-element.34), channel_id=1, source_target_pairs={{0,12},{4,8},{8,4},{12,0},{1,13},{5,9},{9,5},{13,1},{2,14},{6,10},... | collective-permute-start | bytes 884744 | tf_op jit(solution)/shard_map/ppermute | solution.py:11
  21.6 15.9 %collective-permute-start.4 = (f32[1,768]{1,0:T(1,128)}, f32[1,768]{1,0:T(1,128)S(1)}, u32[]{:S(2)}, u32[]{:S(2)}) collective-permute-start(f32[1,768]{1,0:T(1,128)} %get-tuple-element.37), channel_id=1, source_target_pairs={{0,8},{4,12},{8,0},{12,4},{1,9},{5,13},{9,1},{13,5},{2,10},{6,14},... | collective-permute-start | bytes 9224 | tf_op jit(solution)/shard_map/ppermute | solution.py:11
  24.4 13.6 %collective-permute-start.5 = (f32[1,768]{1,0:T(1,128)}, f32[1,768]{1,0:T(1,128)S(1)}, u32[]{:S(2)}, u32[]{:S(2)}) collective-permute-start(f32[1,768]{1,0:T(1,128)} %get-tuple-element.38), channel_id=1, source_target_pairs={{0,12},{4,8},{8,4},{12,0},{1,13},{5,9},{9,5},{13,1},{2,14},{6,10},... | collective-permute-start | bytes 9224 | tf_op jit(solution)/shard_map/ppermute | solution.py:11
  37.5 7.4 %collective-permute-start.8 = (bf16[112,1536]{1,0:T(8,128)(2,1)S(1)}, bf16[112,1536]{1,0:T(8,128)(2,1)S(1)}, u32[]{:S(2)}, u32[]{:S(2)}) collective-permute-start(bf16[112,1536]{1,0:T(8,128)(2,1)S(1)} %slice.32), channel_id=1, source_target_pairs={{0,2},{1,3},{2,0},{3,1},{4,6},{5,7},{6,4},{7,5},{8,10},{9,11},{10,... | collective-permute-start | bytes 1032200 | tf_op jit(solution)/shard_map/ppermute | solution.py:11
  38.0 7.5 %collective-permute-start.9 = (bf16[112,1536]{1,0:T(8,128)(2,1)}, bf16[112,1536]{1,0:T(8,128)(2,1)S(1)}, u32[]{:S(2)}, u32[]{:S(2)}) collective-permute-start(bf16[112,1536]{1,0:T(8,128)(2,1)} %slice.33), channel_id=1, source_target_pairs={{0,1},{1,0},{2,3},{3,2},{4,5},{5,4},{6,7},{7,6},{8,9},{9,8},{10,11... | collective-permute-start | bytes 1032200 | tf_op jit(solution)/shard_map/ppermute | solution.py:11
  39.2 6.4 %collective-permute-start.10 = (bf16[224,1536]{1,0:T(8,128)(2,1)}, bf16[224,1536]{1,0:T(8,128)(2,1)}, u32[]{:S(2)}, u32[]{:S(2)}) collective-permute-start(bf16[224,1536]{1,0:T(8,128)(2,1)} %get-tuple-element.39.refs_10_), channel_id=1, source_target_pairs={{0,16},{16,0},{1,17},{17,1},{2,18},{18,2},{3,19},{19,3},{4,20},{20... | collective-permute-start | bytes 2064392 | tf_op jit(solution)/shard_map/ppermute | solution.py:11
  39.9 7.9 %collective-permute-start.11 = (bf16[224,1536]{1,0:T(8,128)(2,1)S(1)}, bf16[224,1536]{1,0:T(8,128)(2,1)}, u32[]{:S(2)}, u32[]{:S(2)}) collective-permute-start(bf16[224,1536]{1,0:T(8,128)(2,1)S(1)} %collective-permute-done.6.refs_11_), channel_id=1, source_target_pairs={{0,16},{16,0},{1,17},{17,1},{2,18},{18,2},{3,19},{19,3},{4,20},{20... | collective-permute-start | bytes 2064392 | tf_op jit(solution)/shard_map/ppermute | solution.py:11
  41.2 6.7 %collective-permute-start.12 = (bf16[224,1536]{1,0:T(8,128)(2,1)}, bf16[224,1536]{1,0:T(8,128)(2,1)}, u32[]{:S(2)}, u32[]{:S(2)}) collective-permute-start(bf16[224,1536]{1,0:T(8,128)(2,1)} %collective-permute-done.7.refs_12_), channel_id=1, source_target_pairs={{0,16},{16,0},{1,17},{17,1},{2,18},{18,2},{3,19},{19,3},{4,20},{20... | collective-permute-start | bytes 2064392 | tf_op jit(solution)/shard_map/ppermute | solution.py:11
  59.4 9.0 %collective-permute-start.15 = (f32[4,64]{1,0:T(4,128)S(1)}, f32[4,64]{1,0:T(4,128)S(1)}, u32[]{:S(2)}, u32[]{:S(2)}) collective-permute-start(f32[4,64]{1,0:T(4,128)S(1)} %bitcast.27), channel_id=1, source_target_pairs={{0,4},{4,0},{8,12},{12,8},{1,5},{5,1},{9,13},{13,9},{2,6},{6,2},{1... | collective-permute-start | bytes 3080 | tf_op jit(solution)/shard_map/ppermute | solution.py:11
  60.6 7.9 %collective-permute-start.16 = (f32[4,64]{1,0:T(4,128)S(1)}, f32[4,64]{1,0:T(4,128)S(1)}, u32[]{:S(2)}, u32[]{:S(2)}) collective-permute-start(f32[4,64]{1,0:T(4,128)S(1)} %bitcast.28), channel_id=1, source_target_pairs={{0,8},{4,12},{8,0},{12,4},{1,9},{5,13},{9,1},{13,5},{2,10},{6,14},... | collective-permute-start | bytes 3080 | tf_op jit(solution)/shard_map/ppermute | solution.py:11
  63.7 5.4 %collective-permute-start.17 = (f32[4,64]{1,0:T(4,128)S(1)}, f32[4,64]{1,0:T(4,128)S(1)}, u32[]{:S(2)}, u32[]{:S(2)}) collective-permute-start(f32[4,64]{1,0:T(4,128)S(1)} %bitcast.29), channel_id=1, source_target_pairs={{0,12},{4,8},{8,4},{12,0},{1,13},{5,9},{9,5},{13,1},{2,14},{6,10},... | collective-permute-start | bytes 3080 | tf_op jit(solution)/shard_map/ppermute | solution.py:11
  63.9 9.7 %collective-permute-start.18 = (f16[64,1536]{1,0:T(8,128)(2,1)S(1)}, f16[64,1536]{1,0:T(8,128)(2,1)S(1)}, u32[]{:S(2)}, u32[]{:S(2)}) collective-permute-start(f16[64,1536]{1,0:T(8,128)(2,1)S(1)} %convert_element_type.76), channel_id=1, source_target_pairs={{0,4},{4,0},{8,12},{12,8},{1,5},{5,1},{9,13},{13,9},{2,6},{6,2},{1... | collective-permute-start | bytes 589832 | tf_op jit(solution)/shard_map/ppermute | solution.py:11
  64.5 18.0 %collective-permute-start.19 = (f16[64,1536]{1,0:T(8,128)(2,1)S(1)}, f16[64,1536]{1,0:T(8,128)(2,1)S(1)}, u32[]{:S(2)}, u32[]{:S(2)}) collective-permute-start(f16[64,1536]{1,0:T(8,128)(2,1)S(1)} %convert_element_type.78), channel_id=1, source_target_pairs={{0,8},{4,12},{8,0},{12,4},{1,9},{5,13},{9,1},{13,5},{2,10},{6,14},... | collective-permute-start | bytes 589832 | tf_op jit(solution)/shard_map/ppermute | solution.py:11
  68.3 14.1 %collective-permute-start.20 = (f16[64,1536]{1,0:T(8,128)(2,1)S(1)}, f16[64,1536]{1,0:T(8,128)(2,1)S(1)}, u32[]{:S(2)}, u32[]{:S(2)}) collective-permute-start(f16[64,1536]{1,0:T(8,128)(2,1)S(1)} %convert_element_type.80), channel_id=1, source_target_pairs={{0,12},{4,8},{8,4},{12,0},{1,13},{5,9},{9,5},{13,1},{2,14},{6,10},... | collective-permute-start | bytes 589832 | tf_op jit(solution)/shard_map/ppermute | solution.py:11
  105.7 3.1 %collective-permute-start.22 = (bf16[256,1536]{1,0:T(8,128)(2,1)}, bf16[256,1536]{1,0:T(8,128)(2,1)S(1)}, u32[]{:S(2)}, u32[]{:S(2)}) collective-permute-start(bf16[256,1536]{1,0:T(8,128)(2,1)} %get-tuple-element.74), channel_id=1, source_target_pairs={{0,16},{16,0},{1,17},{17,1},{2,18},{18,2},{3,19},{19,3},{4,20},{20... | collective-permute-start | bytes 2359304 | tf_op jit(solution)/shard_map/ppermute | solution.py:11
  110.7 15.4 %collective-permute-start.24 = (bf16[192,1536]{1,0:T(8,128)(2,1)S(1)}, bf16[192,1536]{1,0:T(8,128)(2,1)S(1)}, u32[]{:S(2)}, u32[]{:S(2)}) collective-permute-start(bf16[192,1536]{1,0:T(8,128)(2,1)S(1)} %pad_maximum_fusion.1), channel_id=1, source_target_pairs={{0,2},{1,3},{2,0},{3,1},{4,6},{5,7},{6,4},{7,5},{8,10},{9,11},{10,... | collective-permute-start | bytes 1769480 | tf_op jit(solution)/shard_map/ppermute | solution.py:11
  112.2 15.1 %collective-permute-start.23 = (bf16[192,1536]{1,0:T(8,128)(2,1)S(1)}, bf16[192,1536]{1,0:T(8,128)(2,1)S(1)}, u32[]{:S(2)}, u32[]{:S(2)}) collective-permute-start(bf16[192,1536]{1,0:T(8,128)(2,1)S(1)} %pad_maximum_fusion), channel_id=1, source_target_pairs={{0,1},{1,0},{2,3},{3,2},{4,5},{5,4},{6,7},{7,6},{8,9},{9,8},{10,11... | collective-permute-start | bytes 1769480 | tf_op jit(solution)/shard_map/ppermute | solution.py:11
  127.4 8.0 %collective-permute-start.25 = (bf16[96,1536]{1,0:T(8,128)(2,1)S(1)}, bf16[96,1536]{1,0:T(8,128)(2,1)S(1)}, u32[]{:S(2)}, u32[]{:S(2)}) collective-permute-start(bf16[96,1536]{1,0:T(8,128)(2,1)S(1)} %add_convert_fusion.1), channel_id=1, source_target_pairs={{0,2},{1,3},{2,0},{3,1},{4,6},{5,7},{6,4},{7,5},{8,10},{9,11},{10,... | collective-permute-start | bytes 884744 | tf_op jit(solution)/shard_map/ppermute | solution.py:11
  128.0 7.7 %collective-permute-start.26 = (bf16[96,1536]{1,0:T(8,128)(2,1)S(1)}, bf16[96,1536]{1,0:T(8,128)(2,1)S(1)}, u32[]{:S(2)}, u32[]{:S(2)}) collective-permute-start(bf16[96,1536]{1,0:T(8,128)(2,1)S(1)} %add_convert_fusion), channel_id=1, source_target_pairs={{0,1},{1,0},{2,3},{3,2},{4,5},{5,4},{6,7},{7,6},{8,9},{9,8},{10,11... | collective-permute-start | bytes 884744 | tf_op jit(solution)/shard_map/ppermute | solution.py:11
  (21 other events, 220.7 us)

commit v6 on v5

--- a/solution.py
+++ b/solution.py
@@ -25,14 +25,23 @@
 
 
 def pieces(own, axis):
-    count, rows = lax.axis_size(axis), own.shape[0]
-    if count != 4 or rows % 32:
-        return [((k, 0), block) for k, block in enumerate(everyone(own, axis))]
-    near, side = hop(own, axis, 1), hop(own, axis, 2)
-    half = rows // 2
-    far_top = hop(near[:half], axis, 2)
-    far_bottom = hop(side[half:], axis, 1)
-    return [((0, 0), own), ((1, 0), near), ((2, 0), side), ((3, 0), far_top), ((3, half), far_bottom)]
+    count = lax.axis_size(axis)
+    if count != 4 or len(own) != 2:
+        whole = own[0] if len(own) == 1 else jnp.concatenate(own, axis=0)
+        return [((k, 0), block) for k, block in enumerate(everyone(whole, axis))]
+    top, bottom = own
+    row = top.shape[0]
+    near_top, side_bottom = hop(top, axis, 1), hop(bottom, axis, 2)
+    near_bottom, side_top = hop(bottom, axis, 1), hop(top, axis, 2)
+    far_top = hop(near_top, axis, 2)
+    far_bottom = hop(side_bottom, axis, 1)
+    tops = [top, near_top, side_top, far_top]
+    bottoms = [bottom, near_bottom, side_bottom, far_bottom]
+    return [
+        ((k, first), block)
+        for k in range(4)
+        for first, block in ((0, tops[k]), (row, bottoms[k]))
+    ]
 
 
 def in_order(blocks, place, size, count):
@@ -51,17 +60,21 @@
     width, rows = latents.shape[1] // dps, length // grps
     half = width // grps
     strip = length * half // depth
+    cut = (size + strip) // 2 if size % 16 == 0 else 0
+    ends = [cut, size + strip - cut] if cut else []
 
     def kernel(attended_ref, latents_ref, gating_ref, weight_ref, positions_ref, *refs):
         outs, sems = refs[:-1], refs[-1]
         grp, dp = lax.axis_index("grp"), lax.axis_index("dp")
         row = pl.ds(pl.multiple_of(grp * rows, 16), rows)
-        moves = [(weight_ref, outs[-1].at[:size])]
+        moves = []
         if size % 16 == 0:
             column = pl.ds(pl.multiple_of(dp * width + grp * half, 128), half)
             for i in range(length // strip):
                 lines = positions_ref.at[i * strip : (i + 1) * strip, column]
-                moves.append((lines, outs[-1].at[size:, i * half : (i + 1) * half]))
+                moves.append((lines, outs[-1].at[size - cut :, i * half : (i + 1) * half]))
+            moves.append((weight_ref.at[:cut], outs[-2]))
+            moves.append((weight_ref.at[cut:], outs[-1].at[: size - cut]))
         for k in range(dps):
             column = pl.ds(pl.multiple_of((dp ^ k) * width, 128), width)
             moves.append((attended_ref.at[row, :], outs[k].at[:, :depth]))
@@ -81,13 +94,13 @@
         kernel,
         out_shape=[jax.ShapeDtypeStruct((rows, depth + width), bf16)] * dps
         + [jax.ShapeDtypeStruct((1, width), f32)] * dps
-        + [jax.ShapeDtypeStruct((size + strip, depth), bf16)],
+        + [jax.ShapeDtypeStruct((end, depth), bf16) for end in ends],
         in_specs=[pl.BlockSpec(memory_space=pltpu.HBM)] * 5,
-        out_specs=[VMEM] * (2 * dps + 1),
-        scratch_shapes=[pltpu.SemaphoreType.DMA((3 * dps + 1 + length // strip,))],
+        out_specs=[VMEM] * (2 * dps + len(ends)),
+        scratch_shapes=[pltpu.SemaphoreType.DMA((3 * dps + 2 + length // strip,))],
         name="pack",
     )(attended, latents, gating, weight, positions)
-    return list(packed[:dps]), list(packed[dps:-1]), packed[-1]
+    return list(packed[:dps]), list(packed[dps : 2 * dps]), list(packed[2 * dps :])
 
 
 def generate(aligned, messages, gates, picks, gain, own_weight, twin_weight, spots, size, tables):
@@ -194,7 +207,7 @@
             bytes_accessed=2 * depth * (width + clips * rows) + 8 * clips * rows * width,
             transcendentals=0,
         ),
-        compiler_params=pltpu.CompilerParams(vmem_limit_bytes=49 * 2**20),
+        compiler_params=pltpu.CompilerParams(vmem_limit_bytes=55 * 2**20),
         name="generate",
     )(*messages, *gates, picks, gain[None, :], *own_weight, *twin_weight, *tables)
 
@@ -251,7 +264,7 @@
     if size % 16:
         columns = part(part(critic_position, 1, dps, dp), 1, grps, grp)
         lines = [columns[i : i + strip] for i in range(0, length, strip)]
-        own = jnp.concatenate([weights[0], jnp.concatenate(lines, axis=1)], axis=0)
+        own = [jnp.concatenate([weights[0], jnp.concatenate(lines, axis=1)], axis=0)]
     found = pieces(own, "seq")
     if size % 16 == 0:
         spots, blocks = [spot for spot, _ in found], [block for _, block in found]

time: 137 us -> 139 us (1.015)
  local copies, waits for them, and re-layouts: 11.4 us -> 2.01 us
  starting transfers between devices: 30.9 us -> 38.8 us
  other arithmetic: 4.41 us -> 8.03 us
  waiting for transfers between devices: 58.7 us -> 56.8 us
    unnamed x37 -> x49, local copies, waits for them, and re-layouts: 9.05 us -> 0.72 us
    ppermute x27 -> x32, starting transfers between devices: 30.9 us -> 38.8 us  [hop(): return lax.ppermute(block, axis, route)]
    convert_element_type x3, other arithmetic: 0.07 us -> 3.05 us  [shards(): term = terms[k].astype(f16)]
    ppermute x27 -> x32, waiting for transfers between devices: 58.7 us -> 56.8 us  [hop(): return lax.ppermute(block, axis, route)]
    slice x2 -> x0, local copies, waits for them, and re-layouts: 1.76 us -> none  [the longest x1 1.74 us: pieces(): far_bottom = hop(side[half:], axis, 1)]
    pallas_call x1, Pallas kernels: 5.95 us -> 7.37 us  [generate(): pl.pallas_call(kernel, out_shape=[jax.ShapeDtypeStruct((clips, rows, chan...]
  transfers between devices with their start and end apart: 27 -> 32, of which waited for: 14 -> 13; matrix products, arithmetic and copies ran while one was open for 2% -> 4% of each run, Pallas kernels for 0% -> 0%
where the time goes in v6:
time: 139 us
  waiting for transfers between devices  56.8 us (41%)
  starting transfers between devices  38.8 us (28%)
  blocking collectives  20.1 us (14%)
  Pallas kernels  10.3 us (7%)
  other arithmetic  8.03 us (6%)
  matrix products  2.22 us (2%)
  local copies, waits for them, and re-layouts  2.01 us (1%)
    ppermute x32, waiting for transfers between devices, hop(): return lax.ppermute(block, axis, route)  56.8 us
    ppermute x32, starting transfers between devices, hop(): return lax.ppermute(block, axis, route)  38.8 us
    all_gather x1, blocking collectives, shards(): lax.all_gather(jnp.concatenate([hidden_grad, tail], axis=1), 'dp', axis=0...  20.1 us
    pallas_call x1, Pallas kernels, generate(): pl.pallas_call(kernel, out_shape=[jax.ShapeDtypeStruct((clips, rows, chan...  7.37 us
    convert_element_type x3, other arithmetic, shards(): term = terms[k].astype(f16)  3.05 us
    pallas_call x1, Pallas kernels, pack(): pl.pallas_call(kernel, out_shape=[jax.ShapeDtypeStruct((rows, depth + wid...  2.95 us
  transfers between devices with their start and end apart: 32, of which 13 were waited for; matrix products, arithmetic and copies ran while one was open for 4% of the time, Pallas kernels for 0%

profile of v6, /device:TPU:0, one launch (start us, length us, event | category | flops | bytes accessed | tf_op | source)
XLA Modules:
  0.0 138.8 jit_solution(5248511540022163406)
XLA Ops:
  0.0 2.9 %pack.1 = (bf16[64,2304]{1,0:T(8,128)(2,1)}, bf16[64,2304]{1,0:T(8,128)(2,1)}, bf16[64,2304]{1,0:T(8,128)(2,1)}, bf16[64,2304]{1,0:T(8,128)(2,1)}, f32[1,768]{1,...) custom-call(bf16[128,1536]{1,0:T(8,128)(2,1)} %bitcast.29, ...), custom_call_target="tpu_custom_call" | custom-call | tf_op jit(solution)/shard_map/pack/pallas_call | solution.py:93
  3.0 3.1 %collective-permute-start = (bf16[64,2304]{1,0:T(8,128)(2,1)}, bf16[64,2304]{1,0:T(8,128)(2,1)S(1)}, u32[]{:S(2)}, u32[]{:S(2)}) collective-permute-start(bf16[64,2304]{1,0:T(8,128)(2,1)} %get-tuple-element.33), channel_id=1, source_target_pairs={{0,4},{4,0},{8,12},{12,8},{1,5},{5,1},{9,13},{13,9},{2,6},{6,2},{1... | collective-permute-start | bytes 884744 | tf_op jit(solution)/shard_map/ppermute | solution.py:11
  6.1 2.6 %collective-permute-start.1 = (bf16[64,2304]{1,0:T(8,128)(2,1)}, bf16[64,2304]{1,0:T(8,128)(2,1)S(1)}, u32[]{:S(2)}, u32[]{:S(2)}) collective-permute-start(bf16[64,2304]{1,0:T(8,128)(2,1)} %get-tuple-element.34), channel_id=1, source_target_pairs={{0,8},{4,12},{8,0},{12,4},{1,9},{5,13},{9,1},{13,5},{2,10},{6,14},... | collective-permute-start | bytes 884744 | tf_op jit(solution)/shard_map/ppermute | solution.py:11
  9.1 3.9 %collective-permute-start.5 = (f32[1,768]{1,0:T(1,128)}, f32[1,768]{1,0:T(1,128)S(1)}, u32[]{:S(2)}, u32[]{:S(2)}) collective-permute-start(f32[1,768]{1,0:T(1,128)} %get-tuple-element.39), channel_id=1, source_target_pairs={{0,12},{4,8},{8,4},{12,0},{1,13},{5,9},{9,5},{13,1},{2,14},{6,10},... | collective-permute-start | bytes 9224 | tf_op jit(solution)/shard_map/ppermute | solution.py:11
  13.1 6.5 %collective-permute-done.3.refs_5_ = f32[1,768]{1,0:T(1,128)S(1)} collective-permute-done((f32[1,768]{1,0:T(1,128)}, f32[1,768]{1,0:T(1,128)S(1)}, u32[]{:S(2)}, u32[]{:S(2)}) %collective-permute-start.3) | collective-permute-done | bytes 3104 | tf_op jit(solution)/shard_map/ppermute | solution.py:11
  19.5 1.7 %collective-permute-start.6 = (bf16[112,1536]{1,0:T(8,128)(2,1)}, bf16[112,1536]{1,0:T(8,128)(2,1)S(1)}, u32[]{:S(2)}, u32[]{:S(2)}) collective-permute-start(bf16[112,1536]{1,0:T(8,128)(2,1)} %get-tuple-element.40.refs_10_), channel_id=1, source_target_pairs={{0,1},{1,0},{2,3},{3,2},{4,5},{5,4},{6,7},{7,6},{8,9},{9,8},{10,11... | collective-permute-start | bytes 1032200 | tf_op jit(solution)/shard_map/ppermute | solution.py:11
  22.3 1.5 %collective-permute-start.9 = (bf16[112,1536]{1,0:T(8,128)(2,1)}, bf16[112,1536]{1,0:T(8,128)(2,1)S(1)}, u32[]{:S(2)}, u32[]{:S(2)}) collective-permute-start(bf16[112,1536]{1,0:T(8,128)(2,1)} %get-tuple-element.41.refs_11_), channel_id=1, source_target_pairs={{0,2},{1,3},{2,0},{3,1},{4,6},{5,7},{6,4},{7,5},{8,10},{9,11},{10,... | collective-permute-start | bytes 1032200 | tf_op jit(solution)/shard_map/ppermute | solution.py:11
  23.8 1.5 %collective-permute-start.7 = (bf16[112,1536]{1,0:T(8,128)(2,1)}, bf16[112,1536]{1,0:T(8,128)(2,1)S(1)}, u32[]{:S(2)}, u32[]{:S(2)}) collective-permute-start(bf16[112,1536]{1,0:T(8,128)(2,1)} %get-tuple-element.41.refs_11_), channel_id=1, source_target_pairs={{0,1},{1,0},{2,3},{3,2},{4,5},{5,4},{6,7},{7,6},{8,9},{9,8},{10,11... | collective-permute-start | bytes 1032200 | tf_op jit(solution)/shard_map/ppermute | solution.py:11
  25.8 2.5 %collective-permute-start.2 = (bf16[64,2304]{1,0:T(8,128)(2,1)}, bf16[64,2304]{1,0:T(8,128)(2,1)S(1)}, u32[]{:S(2)}, u32[]{:S(2)}) collective-permute-start(bf16[64,2304]{1,0:T(8,128)(2,1)} %get-tuple-element.35), channel_id=1, source_target_pairs={{0,12},{4,8},{8,4},{12,0},{1,13},{5,9},{9,5},{13,1},{2,14},{6,10},... | collective-permute-start | bytes 884744 | tf_op jit(solution)/shard_map/ppermute | solution.py:11
  28.3 6.3 %collective-permute-done.2.refs_3_ = bf16[64,2304]{1,0:T(8,128)(2,1)S(1)} collective-permute-done((bf16[64,2304]{1,0:T(8,128)(2,1)}, bf16[64,2304]{1,0:T(8,128)(2,1)S(1)}, u32[]{:S(2)}, u32[]{:S(2)}) %collective-permute-start.2) | collective-permute-done | bytes 294944 | tf_op jit(solution)/shard_map/ppermute | solution.py:11
  35.1 1.6 %collective-permute-start.10 = (bf16[112,1536]{1,0:T(8,128)(2,1)S(1)}, bf16[112,1536]{1,0:T(8,128)(2,1)S(1)}, u32[]{:S(2)}, u32[]{:S(2)}) collective-permute-start(bf16[112,1536]{1,0:T(8,128)(2,1)S(1)} %collective-permute-done.6.refs_12_), channel_id=1, source_target_pairs={{0,2},{1,3},{2,0},{3,1},{4,6},{5,7},{6,4},{7,5},{8,10},{9,11},{10,... | collective-permute-start | bytes 1032200 | tf_op jit(solution)/shard_map/ppermute | solution.py:11
  38.6 6.5 %collective-permute-done.10.refs_16_ = bf16[112,1536]{1,0:T(8,128)(2,1)S(1)} collective-permute-done((bf16[112,1536]{1,0:T(8,128)(2,1)S(1)}, bf16[112,1536]{1,0:T(8,128)(2,1)S(1)}, u32[]{:S(2)}, u32[]{:S(2)}) %collective-permute-start.10) | collective-permute-done | bytes 344096 | tf_op jit(solution)/shard_map/ppermute | solution.py:11
  48.8 7.4 %generate.1 = (f32[4,64,768]{2,1,0:T(8,128)}, bf16[768,1536]{1,0:T(8,128)(2,1)}, bf16[256,1536]{1,0:T(8,128)(2,1)}, f32[4,1,768]{2,1,0:T(1,128)}, f32[4,1,64]{2,...) custom-call(bf16[64,2304]{1,0:T(8,128)(2,1)} %get-tuple-element.32.refs_0_, ...), custom_call_target="tpu_custom_call" | custom-call | flops 603979776 | bytes 4718592 | tf_op jit(solution)/shard_map/generate/pallas_call | solution.py:188
  56.3 5.1 %collective-permute-start.20 = (f32[4,64]{1,0:T(4,128)}, f32[4,64]{1,0:T(4,128)S(1)}, u32[]{:S(2)}, u32[]{:S(2)}) collective-permute-start(f32[4,64]{1,0:T(4,128)} %bitcast.34), channel_id=1, source_target_pairs={{0,4},{4,0},{8,12},{12,8},{1,5},{5,1},{9,13},{13,9},{2,6},{6,2},{1... | collective-permute-start | bytes 3080 | tf_op jit(solution)/shard_map/ppermute | solution.py:11
  61.7 2.2 %collective-permute-start.22 = (f32[4,64]{1,0:T(4,128)}, f32[4,64]{1,0:T(4,128)S(1)}, u32[]{:S(2)}, u32[]{:S(2)}) collective-permute-start(f32[4,64]{1,0:T(4,128)} %bitcast.36), channel_id=1, source_target_pairs={{0,12},{4,8},{8,4},{12,0},{1,13},{5,9},{9,5},{13,1},{2,14},{6,10},... | collective-permute-start | bytes 3080 | tf_op jit(solution)/shard_map/ppermute | solution.py:11
  70.0 2.2 %collective-permute-start.25 = (f16[64,1536]{1,0:T(8,128)(2,1)S(1)}, f16[64,1536]{1,0:T(8,128)(2,1)S(1)}, u32[]{:S(2)}, u32[]{:S(2)}) collective-permute-start(f16[64,1536]{1,0:T(8,128)(2,1)S(1)} %convert_element_type.80), channel_id=1, source_target_pairs={{0,12},{4,8},{8,4},{12,0},{1,13},{5,9},{9,5},{13,1},{2,14},{6,10},... | collective-permute-start | bytes 589832 | tf_op jit(solution)/shard_map/ppermute | solution.py:11
  72.3 1.9 %collective-permute-done.23 = f16[64,1536]{1,0:T(8,128)(2,1)S(1)} collective-permute-done((f16[64,1536]{1,0:T(8,128)(2,1)S(1)}, f16[64,1536]{1,0:T(8,128)(2,1)S(1)}, u32[]{:S(2)}, u32[]{:S(2)}) %collective-permute-start.23) | collective-permute-done | bytes 196640 | tf_op jit(solution)/shard_map/ppermute | solution.py:11
  74.3 10.0 %collective-permute-done.24 = f16[64,1536]{1,0:T(8,128)(2,1)S(1)} collective-permute-done((f16[64,1536]{1,0:T(8,128)(2,1)S(1)}, f16[64,1536]{1,0:T(8,128)(2,1)S(1)}, u32[]{:S(2)}, u32[]{:S(2)}) %collective-permute-start.24) | collective-permute-done | bytes 196640 | tf_op jit(solution)/shard_map/ppermute | solution.py:11
  85.3 20.1 %all_gather.3 = bf16[256,1664]{1,0:T(8,128)(2,1)S(1)} all-gather(bf16[64,1664]{1,0:T(8,128)(2,1)S(1)} %pad_maximum_fusion.2), channel_id=1, replica_groups=mesh['grp'=2,'dp'=4,'seq'=4] {'dp'}, dimensions={0}, use_global_device_ids=true | all-gather | bytes 1064960 | tf_op jit(solution)/shard_map/all_gather | solution.py:323
  108.9 1.9 %collective-permute-done.26 = bf16[256,768]{1,0:T(8,128)(2,1)S(1)} collective-permute-done((bf16[256,768]{1,0:T(8,128)(2,1)S(1)}, bf16[256,768]{1,0:T(8,128)(2,1)S(1)}, u32[]{:S(2)}, u32[]{:S(2)}) %collective-permute-start.26) | collective-permute-done | bytes 393248 | tf_op jit(solution)/shard_map/ppermute | solution.py:11
  110.8 1.4 %fusion = f32[768,1536]{1,0:T(8,128)S(1)} fusion(bf16[256,1536]{1,0:T(8,128)(2,1)S(1)} %collective-permute-done.27, bf16[256,1536]{1,0:T(8,128)(2,1)S(1)} %get-tuple-element.75, bf16[256,768]{1,0:T(8,128)(2,1)S(1)} %collective-permute-done.26, bf16[256,768]{1,0:T(8,128)(2,1)S(1)} %bitcast.31), kind=kOutput, calls=%fused_computation | convolution fusion | flops 1212678144 | bytes 7077888 | tf_op jit(solution)/shard_map/td,th->dh/dot_general | solution.py:340
  114.4 13.7 %collective-permute-done.29 = bf16[192,1536]{1,0:T(8,128)(2,1)S(1)} collective-permute-done((bf16[192,1536]{1,0:T(8,128)(2,1)S(1)}, bf16[192,1536]{1,0:T(8,128)(2,1)S(1)}, u32[]{:S(2)}, u32[]{:S(2)}) %collective-permute-start.29) | collective-permute-done | bytes 589856 | tf_op jit(solution)/shard_map/ppermute | solution.py:11
  128.3 1.7 %collective-permute-start.30 = (bf16[96,1536]{1,0:T(8,128)(2,1)S(1)}, bf16[96,1536]{1,0:T(8,128)(2,1)S(1)}, u32[]{:S(2)}, u32[]{:S(2)}) collective-permute-start(bf16[96,1536]{1,0:T(8,128)(2,1)S(1)} %add_convert_fusion.1), channel_id=1, source_target_pairs={{0,2},{1,3},{2,0},{3,1},{4,6},{5,7},{6,4},{7,5},{8,10},{9,11},{10,... | collective-permute-start | bytes 884744 | tf_op jit(solution)/shard_map/ppermute | solution.py:11
  130.9 5.6 %collective-permute-done.30 = bf16[96,1536]{1,0:T(8,128)(2,1)S(1)} collective-permute-done((bf16[96,1536]{1,0:T(8,128)(2,1)S(1)}, bf16[96,1536]{1,0:T(8,128)(2,1)S(1)}, u32[]{:S(2)}, u32[]{:S(2)}) %collective-permute-start.30) | collective-permute-done | bytes 294944 | tf_op jit(solution)/shard_map/ppermute | solution.py:11
  (127 shorter events, 24.5 us)
Async XLA Ops:
  3.0 22.3 %collective-permute-start = (bf16[64,2304]{1,0:T(8,128)(2,1)}, bf16[64,2304]{1,0:T(8,128)(2,1)S(1)}, u32[]{:S(2)}, u32[]{:S(2)}) collective-permute-start(bf16[64,2304]{1,0:T(8,128)(2,1)} %get-tuple-element.33), channel_id=1, source_target_pairs={{0,4},{4,0},{8,12},{12,8},{1,5},{5,1},{9,13},{13,9},{2,6},{6,2},{1... | collective-permute-start | bytes 884744 | tf_op jit(solution)/shard_map/ppermute | solution.py:11
  6.1 19.7 %collective-permute-start.1 = (bf16[64,2304]{1,0:T(8,128)(2,1)}, bf16[64,2304]{1,0:T(8,128)(2,1)S(1)}, u32[]{:S(2)}, u32[]{:S(2)}) collective-permute-start(bf16[64,2304]{1,0:T(8,128)(2,1)} %get-tuple-element.34), channel_id=1, source_target_pairs={{0,8},{4,12},{8,0},{12,4},{1,9},{5,13},{9,1},{13,5},{2,10},{6,14},... | collective-permute-start | bytes 884744 | tf_op jit(solution)/shard_map/ppermute | solution.py:11
  8.7 10.9 %collective-permute-start.3 = (f32[1,768]{1,0:T(1,128)}, f32[1,768]{1,0:T(1,128)S(1)}, u32[]{:S(2)}, u32[]{:S(2)}) collective-permute-start(f32[1,768]{1,0:T(1,128)} %get-tuple-element.37), channel_id=1, source_target_pairs={{0,4},{4,0},{8,12},{12,8},{1,5},{5,1},{9,13},{13,9},{2,6},{6,2},{1... | collective-permute-start | bytes 9224 | tf_op jit(solution)/shard_map/ppermute | solution.py:11
  9.1 13.1 %collective-permute-start.4 = (f32[1,768]{1,0:T(1,128)}, f32[1,768]{1,0:T(1,128)S(1)}, u32[]{:S(2)}, u32[]{:S(2)}) collective-permute-start(f32[1,768]{1,0:T(1,128)} %get-tuple-element.38), channel_id=1, source_target_pairs={{0,8},{4,12},{8,0},{12,4},{1,9},{5,13},{9,1},{13,5},{2,10},{6,14},... | collective-permute-start | bytes 9224 | tf_op jit(solution)/shard_map/ppermute | solution.py:11
  9.1 14.7 %collective-permute-start.5 = (f32[1,768]{1,0:T(1,128)}, f32[1,768]{1,0:T(1,128)S(1)}, u32[]{:S(2)}, u32[]{:S(2)}) collective-permute-start(f32[1,768]{1,0:T(1,128)} %get-tuple-element.39), channel_id=1, source_target_pairs={{0,12},{4,8},{8,4},{12,0},{1,13},{5,9},{9,5},{13,1},{2,14},{6,10},... | collective-permute-start | bytes 9224 | tf_op jit(solution)/shard_map/ppermute | solution.py:11
  19.5 15.0 %collective-permute-start.6 = (bf16[112,1536]{1,0:T(8,128)(2,1)}, bf16[112,1536]{1,0:T(8,128)(2,1)S(1)}, u32[]{:S(2)}, u32[]{:S(2)}) collective-permute-start(bf16[112,1536]{1,0:T(8,128)(2,1)} %get-tuple-element.40.refs_10_), channel_id=1, source_target_pairs={{0,1},{1,0},{2,3},{3,2},{4,5},{5,4},{6,7},{7,6},{8,9},{9,8},{10,11... | collective-permute-start | bytes 1032200 | tf_op jit(solution)/shard_map/ppermute | solution.py:11
  22.3 12.8 %collective-permute-start.9 = (bf16[112,1536]{1,0:T(8,128)(2,1)}, bf16[112,1536]{1,0:T(8,128)(2,1)S(1)}, u32[]{:S(2)}, u32[]{:S(2)}) collective-permute-start(bf16[112,1536]{1,0:T(8,128)(2,1)} %get-tuple-element.41.refs_11_), channel_id=1, source_target_pairs={{0,2},{1,3},{2,0},{3,1},{4,6},{5,7},{6,4},{7,5},{8,10},{9,11},{10,... | collective-permute-start | bytes 1032200 | tf_op jit(solution)/shard_map/ppermute | solution.py:11
  23.8 12.9 %collective-permute-start.7 = (bf16[112,1536]{1,0:T(8,128)(2,1)}, bf16[112,1536]{1,0:T(8,128)(2,1)S(1)}, u32[]{:S(2)}, u32[]{:S(2)}) collective-permute-start(bf16[112,1536]{1,0:T(8,128)(2,1)} %get-tuple-element.41.refs_11_), channel_id=1, source_target_pairs={{0,1},{1,0},{2,3},{3,2},{4,5},{5,4},{6,7},{7,6},{8,9},{9,8},{10,11... | collective-permute-start | bytes 1032200 | tf_op jit(solution)/shard_map/ppermute | solution.py:11
  25.3 12.5 %collective-permute-start.8 = (bf16[112,1536]{1,0:T(8,128)(2,1)}, bf16[112,1536]{1,0:T(8,128)(2,1)S(1)}, u32[]{:S(2)}, u32[]{:S(2)}) collective-permute-start(bf16[112,1536]{1,0:T(8,128)(2,1)} %get-tuple-element.40.refs_10_), channel_id=1, source_target_pairs={{0,2},{1,3},{2,0},{3,1},{4,6},{5,7},{6,4},{7,5},{8,10},{9,11},{10,... | collective-permute-start | bytes 1032200 | tf_op jit(solution)/shard_map/ppermute | solution.py:11
  25.8 8.7 %collective-permute-start.2 = (bf16[64,2304]{1,0:T(8,128)(2,1)}, bf16[64,2304]{1,0:T(8,128)(2,1)S(1)}, u32[]{:S(2)}, u32[]{:S(2)}) collective-permute-start(bf16[64,2304]{1,0:T(8,128)(2,1)} %get-tuple-element.35), channel_id=1, source_target_pairs={{0,12},{4,8},{8,4},{12,0},{1,13},{5,9},{9,5},{13,1},{2,14},{6,10},... | collective-permute-start | bytes 884744 | tf_op jit(solution)/shard_map/ppermute | solution.py:11
  35.1 10.1 %collective-permute-start.10 = (bf16[112,1536]{1,0:T(8,128)(2,1)S(1)}, bf16[112,1536]{1,0:T(8,128)(2,1)S(1)}, u32[]{:S(2)}, u32[]{:S(2)}) collective-permute-start(bf16[112,1536]{1,0:T(8,128)(2,1)S(1)} %collective-permute-done.6.refs_12_), channel_id=1, source_target_pairs={{0,2},{1,3},{2,0},{3,1},{4,6},{5,7},{6,4},{7,5},{8,10},{9,11},{10,... | collective-permute-start | bytes 1032200 | tf_op jit(solution)/shard_map/ppermute | solution.py:11
  36.7 9.8 %collective-permute-start.11 = (bf16[112,1536]{1,0:T(8,128)(2,1)S(1)}, bf16[112,1536]{1,0:T(8,128)(2,1)S(1)}, u32[]{:S(2)}, u32[]{:S(2)}) collective-permute-start(bf16[112,1536]{1,0:T(8,128)(2,1)S(1)} %collective-permute-done.9.refs_15_), channel_id=1, source_target_pairs={{0,1},{1,0},{2,3},{3,2},{4,5},{5,4},{6,7},{7,6},{8,9},{9,8},{10,11... | collective-permute-start | bytes 1032200 | tf_op jit(solution)/shard_map/ppermute | solution.py:11
  37.8 8.7 %collective-permute-start.14 = (bf16[112,1536]{1,0:T(8,128)(2,1)S(1)}, bf16[112,1536]{1,0:T(8,128)(2,1)S(1)}, u32[]{:S(2)}, u32[]{:S(2)}) collective-permute-start(bf16[112,1536]{1,0:T(8,128)(2,1)S(1)} %collective-permute-done.6.refs_12_), channel_id=1, source_target_pairs={{0,16},{16,0},{1,17},{17,1},{2,18},{18,2},{3,19},{19,3},{4,20},{20... | collective-permute-start | bytes 1032200 | tf_op jit(solution)/shard_map/ppermute | solution.py:11
  38.0 9.7 %collective-permute-start.17 = (bf16[112,1536]{1,0:T(8,128)(2,1)S(1)}, bf16[112,1536]{1,0:T(8,128)(2,1)S(1)}, u32[]{:S(2)}, u32[]{:S(2)}) collective-permute-start(bf16[112,1536]{1,0:T(8,128)(2,1)S(1)} %collective-permute-done.9.refs_15_), channel_id=1, source_target_pairs={{0,16},{16,0},{1,17},{17,1},{2,18},{18,2},{3,19},{19,3},{4,20},{20... | collective-permute-start | bytes 1032200 | tf_op jit(solution)/shard_map/ppermute | solution.py:11
  38.5 9.2 %collective-permute-start.15 = (bf16[112,1536]{1,0:T(8,128)(2,1)S(1)}, bf16[112,1536]{1,0:T(8,128)(2,1)}, u32[]{:S(2)}, u32[]{:S(2)}) collective-permute-start(bf16[112,1536]{1,0:T(8,128)(2,1)S(1)} %collective-permute-done.7.refs_13_), channel_id=1, source_target_pairs={{0,16},{16,0},{1,17},{17,1},{2,18},{18,2},{3,19},{19,3},{4,20},{20... | collective-permute-start | bytes 1032200 | tf_op jit(solution)/shard_map/ppermute | solution.py:11
  56.3 13.8 %collective-permute-start.20 = (f32[4,64]{1,0:T(4,128)}, f32[4,64]{1,0:T(4,128)S(1)}, u32[]{:S(2)}, u32[]{:S(2)}) collective-permute-start(f32[4,64]{1,0:T(4,128)} %bitcast.34), channel_id=1, source_target_pairs={{0,4},{4,0},{8,12},{12,8},{1,5},{5,1},{9,13},{13,9},{2,6},{6,2},{1... | collective-permute-start | bytes 3080 | tf_op jit(solution)/shard_map/ppermute | solution.py:11
  61.4 10.9 %collective-permute-start.21 = (f32[4,64]{1,0:T(4,128)}, f32[4,64]{1,0:T(4,128)S(1)}, u32[]{:S(2)}, u32[]{:S(2)}) collective-permute-start(f32[4,64]{1,0:T(4,128)} %bitcast.35), channel_id=1, source_target_pairs={{0,8},{4,12},{8,0},{12,4},{1,9},{5,13},{9,1},{13,5},{2,10},{6,14},... | collective-permute-start | bytes 3080 | tf_op jit(solution)/shard_map/ppermute | solution.py:11
  61.7 10.6 %collective-permute-start.22 = (f32[4,64]{1,0:T(4,128)}, f32[4,64]{1,0:T(4,128)S(1)}, u32[]{:S(2)}, u32[]{:S(2)}) collective-permute-start(f32[4,64]{1,0:T(4,128)} %bitcast.36), channel_id=1, source_target_pairs={{0,12},{4,8},{8,4},{12,0},{1,13},{5,9},{9,5},{13,1},{2,14},{6,10},... | collective-permute-start | bytes 3080 | tf_op jit(solution)/shard_map/ppermute | solution.py:11
  65.6 8.7 %collective-permute-start.23 = (f16[64,1536]{1,0:T(8,128)(2,1)S(1)}, f16[64,1536]{1,0:T(8,128)(2,1)S(1)}, u32[]{:S(2)}, u32[]{:S(2)}) collective-permute-start(f16[64,1536]{1,0:T(8,128)(2,1)S(1)} %convert_element_type.76), channel_id=1, source_target_pairs={{0,4},{4,0},{8,12},{12,8},{1,5},{5,1},{9,13},{13,9},{2,6},{6,2},{1... | collective-permute-start | bytes 589832 | tf_op jit(solution)/shard_map/ppermute | solution.py:11
  67.7 16.5 %collective-permute-start.24 = (f16[64,1536]{1,0:T(8,128)(2,1)S(1)}, f16[64,1536]{1,0:T(8,128)(2,1)S(1)}, u32[]{:S(2)}, u32[]{:S(2)}) collective-permute-start(f16[64,1536]{1,0:T(8,128)(2,1)S(1)} %convert_element_type.78), channel_id=1, source_target_pairs={{0,8},{4,12},{8,0},{12,4},{1,9},{5,13},{9,1},{13,5},{2,10},{6,14},... | collective-permute-start | bytes 589832 | tf_op jit(solution)/shard_map/ppermute | solution.py:11
  70.0 14.3 %collective-permute-start.25 = (f16[64,1536]{1,0:T(8,128)(2,1)S(1)}, f16[64,1536]{1,0:T(8,128)(2,1)S(1)}, u32[]{:S(2)}, u32[]{:S(2)}) collective-permute-start(f16[64,1536]{1,0:T(8,128)(2,1)S(1)} %convert_element_type.80), channel_id=1, source_target_pairs={{0,12},{4,8},{8,4},{12,0},{1,13},{5,9},{9,5},{13,1},{2,14},{6,10},... | collective-permute-start | bytes 589832 | tf_op jit(solution)/shard_map/ppermute | solution.py:11
  112.7 15.4 %collective-permute-start.29 = (bf16[192,1536]{1,0:T(8,128)(2,1)S(1)}, bf16[192,1536]{1,0:T(8,128)(2,1)S(1)}, u32[]{:S(2)}, u32[]{:S(2)}) collective-permute-start(bf16[192,1536]{1,0:T(8,128)(2,1)S(1)} %pad_maximum_fusion.1), channel_id=1, source_target_pairs={{0,2},{1,3},{2,0},{3,1},{4,6},{5,7},{6,4},{7,5},{8,10},{9,11},{10,... | collective-permute-start | bytes 1769480 | tf_op jit(solution)/shard_map/ppermute | solution.py:11
  113.1 15.1 %collective-permute-start.28 = (bf16[192,1536]{1,0:T(8,128)(2,1)S(1)}, bf16[192,1536]{1,0:T(8,128)(2,1)S(1)}, u32[]{:S(2)}, u32[]{:S(2)}) collective-permute-start(bf16[192,1536]{1,0:T(8,128)(2,1)S(1)} %pad_maximum_fusion), channel_id=1, source_target_pairs={{0,1},{1,0},{2,3},{3,2},{4,5},{5,4},{6,7},{7,6},{8,9},{9,8},{10,11... | collective-permute-start | bytes 1769480 | tf_op jit(solution)/shard_map/ppermute | solution.py:11
  128.3 8.3 %collective-permute-start.30 = (bf16[96,1536]{1,0:T(8,128)(2,1)S(1)}, bf16[96,1536]{1,0:T(8,128)(2,1)S(1)}, u32[]{:S(2)}, u32[]{:S(2)}) collective-permute-start(bf16[96,1536]{1,0:T(8,128)(2,1)S(1)} %add_convert_fusion.1), channel_id=1, source_target_pairs={{0,2},{1,3},{2,0},{3,1},{4,6},{5,7},{6,4},{7,5},{8,10},{9,11},{10,... | collective-permute-start | bytes 884744 | tf_op jit(solution)/shard_map/ppermute | solution.py:11
  (32 other events, 364.6 us)
